TPU v7x, 32 devices: a whole 2x2x4 slice. The times are simulated.
32 devices in a mesh: band: 2 (over x), vis: 16 (over z, y, core).
Axes of the slice: x: 2, y: 2, z: 4, core: 2. Of those that a mesh axis runs over, the one named last changes fastest.
Arguments:
- sky_image: float32 [4096, 4096], P(('band', 'vis')), as said below
- coef_dual: float32 [4, 2048, 2048], P(None, ('band', 'vis')), may hold values from -12 to 12
- vis_dual: float32 [2, 16, 16, 4, 2, 32], P('band', 'vis'), may hold values from -12 to 12
- visibilities: float32 [2, 16, 16, 4, 2, 32], P('band', 'vis')
- kernel_blocks: bfloat16 [2, 16, 16, 4, 2, 32, 256], P('band', 'vis'), may hold values from -0.375 to 0.375
- tile_rows: int32 [2, 16, 16, 4], P('band', 'vis'), may hold values from 0 to 2047
- tile_counts: int32 [2, 16, 16], P('band', 'vis'), may hold values from 1 to 4, as said below
Outputs:
- new_image: float32 [4096, 4096], P(('band', 'vis'))
- new_coef_dual: float32 [4, 2048, 2048], P(None, ('band', 'vis'))
- new_vis_dual: float32 [2, 16, 16, 4, 2, 32], P('band', 'vis')
Inputs may be any that keep to these rules, and one draw needn't show every extreme that they name: `sky_image`: nonnegative. `tile_counts`: in every band some owner q has all 4 slots live from every device of that band.
All inputs are finite; a program needn't handle non-finite values.
Results may differ from a plain program's by a relative error of at most 0.0018.
Values may be sent and summed in bfloat16 or wider, within the bound.
No kernel may reach another device: no remote copies, remote signals or barrier semaphores. Data moves between devices by JAX's collectives and lax.ppermute only.
A program may use at most 128 MiB of HBM per device.

v0:
```python
import math

import jax
import jax.numpy as jnp
from jax import lax
from jax.sharding import PartitionSpec as P

IMG = 4096


low_taps = (
    -0.010597401784997278,
    0.032883011666982945,
    0.030841381835986965,
    -0.18703481171888114,
    -0.02798376941698385,
    0.6308807679295904,
    0.7148465705525415,
    0.23037781330885523,
)
high_taps = tuple(((-1.0) ** offset * low_taps[7 - offset] for offset in range(8)))
highest = lax.Precision.HIGHEST


def shifted(block, axis, distance):
    devices = range(lax.axis_size(axis))
    route = [((i - distance) % len(devices), i) for i in devices]
    return lax.ppermute(block, axis, route)


def dft_table(table_size, sign):
    positions = jnp.arange(table_size, dtype=jnp.int32)
    phase = positions[:, None] * positions[None, :] % table_size
    angle = 2.0 * math.pi / table_size * phase.astype(jnp.float32)
    return (jnp.cos(angle), sign * jnp.sin(angle))


def section_one(table, values):
    return jnp.einsum("kn,...nm->...km", table, values, precision=highest)


def section_two(table, values):
    return jnp.einsum("qm,...km->...qk", table, values, precision=highest)


def dft_last(real_in, imag_in, sign):
    leading = real_in.shape[:-1]
    length = real_in.shape[-1]
    inner_len = 64
    outer_len = length // inner_len
    split_real = real_in.reshape(leading + (outer_len, inner_len))
    table_real, table_imag = dft_table(outer_len, sign)
    first_real = section_one(table_real, split_real)
    first_imag = section_one(table_imag, split_real)
    if imag_in is not None:
        split_imag = imag_in.reshape(leading + (outer_len, inner_len))
        first_real = first_real - section_one(table_imag, split_imag)
        first_imag = first_imag + section_one(table_real, split_imag)
    outer_index = jnp.arange(outer_len, dtype=jnp.int32)
    inner_index = jnp.arange(inner_len, dtype=jnp.int32)
    twist_phase = outer_index[:, None] * inner_index[None, :] % length
    twist_angle = 2.0 * math.pi / length * twist_phase.astype(jnp.float32)
    twist_real = jnp.cos(twist_angle)
    twist_imag = sign * jnp.sin(twist_angle)
    mid_real = first_real * twist_real - first_imag * twist_imag
    mid_imag = first_real * twist_imag + first_imag * twist_real
    last_real, last_imag = dft_table(inner_len, sign)
    out_real = section_two(last_real, mid_real) - section_two(last_imag, mid_imag)
    out_imag = section_two(last_real, mid_imag) + section_two(last_imag, mid_real)
    factor = 1.0 / math.sqrt(length)
    return (
        (out_real * factor).reshape(leading + (length,)),
        (out_imag * factor).reshape(leading + (length,)),
    )


def pieces_from_image(extrap, band_count, group_count):
    rows_dev = extrap.shape[0]
    image_width = extrap.shape[1]
    stripe = image_width // band_count
    piece_cols = stripe // group_count
    piece_rows = image_width // group_count
    col_real, col_imag = dft_last(extrap, None, -1.0)
    shaped = jnp.stack([col_real, col_imag]).reshape(
        2, 1, 1, rows_dev, band_count, group_count, piece_cols
    )
    moved = lax.all_to_all(
        lax.all_to_all(shaped, "band", split_axis=4, concat_axis=1, tiled=True),
        "vis",
        split_axis=5,
        concat_axis=2,
        tiled=True,
    )
    columns = jnp.transpose(moved.reshape(2, image_width, piece_cols), (2, 0, 1))
    row_real, row_imag = dft_last(columns[:, 0], columns[:, 1], -1.0)
    stacked = (
        jnp.stack([row_real, row_imag], axis=1)
        .astype(jnp.bfloat16)
        .reshape(piece_cols, 2, group_count, piece_rows)
    )
    pieces = lax.all_to_all(stacked, "vis", split_axis=2, concat_axis=0, tiled=True)
    return pieces.reshape(stripe, 2, piece_rows)


def image_from_pieces(piece_sum, band_count, group_count):
    stripe = piece_sum.shape[0]
    piece_rows = piece_sum.shape[2]
    piece_cols = stripe // group_count
    image_width = piece_rows * group_count
    rows_dev = image_width // (band_count * group_count)
    spread = lax.all_to_all(
        piece_sum.reshape(stripe, 2, 1, piece_rows), "vis", split_axis=0, concat_axis=2, tiled=True
    )
    spread = spread.reshape(piece_cols, 2, image_width)
    col_real, col_imag = dft_last(spread[:, 0], spread[:, 1], 1.0)
    stacked = jnp.transpose(jnp.stack([col_real, col_imag]), (0, 2, 1))
    shaped = stacked.reshape(2, band_count, group_count, rows_dev, 1, 1, piece_cols)
    moved = lax.all_to_all(
        lax.all_to_all(shaped, "band", split_axis=1, concat_axis=4, tiled=True),
        "vis",
        split_axis=2,
        concat_axis=5,
        tiled=True,
    )
    moved = moved.reshape(2, rows_dev, image_width)
    out_real, out_imag = dft_last(moved[0], moved[1], 1.0)
    return out_real


def cols_down(field):
    image_width = field.shape[1]
    extended = jnp.concatenate([field, field[:, :6]], axis=1)
    low_part = 0.0
    high_part = 0.0
    for offset in range(8):
        taken = extended[:, offset : offset + image_width : 2]
        low_part = low_part + low_taps[offset] * taken
        high_part = high_part + high_taps[offset] * taken
    return (low_part, high_part)


def cols_up(low_part, high_part):
    halves = []
    for parity in range(2):
        summed = 0.0
        for delay in range(4):
            summed = summed + low_taps[parity + 2 * delay] * jnp.roll(low_part, delay, axis=1)
            summed = summed + high_taps[parity + 2 * delay] * jnp.roll(high_part, delay, axis=1)
        halves.append(summed)
    return jnp.stack(halves, axis=2).reshape(low_part.shape[0], 2 * low_part.shape[1])


def rows_up(low_ext, high_ext, half_rows):
    halves = []
    for parity in range(2):
        summed = 0.0
        for delay in range(4):
            begin = 3 - delay
            summed = summed + low_taps[parity + 2 * delay] * low_ext[begin : begin + half_rows]
            summed = summed + high_taps[parity + 2 * delay] * high_ext[begin : begin + half_rows]
        halves.append(summed)
    return jnp.stack(halves, axis=1).reshape(2 * half_rows, low_ext.shape[1])


def analysis(extrap):
    rows_dev = extrap.shape[0]
    taken_rows = min(6, rows_dev)
    parts_list = [extrap]
    parts_list.append(shifted(extrap[:taken_rows], ("band", "vis"), -1))
    extended = jnp.concatenate(parts_list, axis=0)
    half_rows = rows_dev // 2
    rows_low = 0.0
    rows_high = 0.0
    for offset in range(8):
        taken = extended[offset : offset + 2 * half_rows : 2]
        rows_low = rows_low + low_taps[offset] * taken
        rows_high = rows_high + high_taps[offset] * taken
    low_low, low_high = cols_down(rows_low)
    high_low, high_high = cols_down(rows_high)
    return jnp.stack([low_low, low_high, high_low, high_high])


def synthesis(coef_dual):
    half_rows = coef_dual.shape[1]
    taken_rows = min(3, half_rows)
    parts_list = [shifted(coef_dual[:, half_rows - taken_rows :, :], ("band", "vis"), 1)]
    joined = jnp.concatenate(parts_list[::-1] + [coef_dual], axis=1)
    cols_low = rows_up(joined[0], joined[2], half_rows)
    cols_high = rows_up(joined[1], joined[3], half_rows)
    return cols_up(cols_low, cols_high)


def degrid(kernel_here, tiles):
    kernel_real = kernel_here[:, :, 0]
    kernel_imag = kernel_here[:, :, 1]
    tile_real = tiles[:, :, 0]
    tile_imag = tiles[:, :, 1]
    out_real = jnp.einsum(
        "qsat,qst->qsa", kernel_real, tile_real, preferred_element_type=jnp.float32
    ) - jnp.einsum("qsat,qst->qsa", kernel_imag, tile_imag, preferred_element_type=jnp.float32)
    out_imag = jnp.einsum(
        "qsat,qst->qsa", kernel_real, tile_imag, preferred_element_type=jnp.float32
    ) + jnp.einsum("qsat,qst->qsa", kernel_imag, tile_real, preferred_element_type=jnp.float32)
    return jnp.stack([out_real, out_imag], axis=2)


def grid_back(kernel_here, weights):
    kernel_real = kernel_here[:, :, 0]
    kernel_imag = kernel_here[:, :, 1]
    weight_real = weights[:, :, 0]
    weight_imag = weights[:, :, 1]
    grid_real = jnp.einsum(
        "qsat,qsa->qst", kernel_real, weight_real, preferred_element_type=jnp.float32
    ) + jnp.einsum("qsat,qsa->qst", kernel_imag, weight_imag, preferred_element_type=jnp.float32)
    grid_imag = jnp.einsum(
        "qsat,qsa->qst", kernel_real, weight_imag, preferred_element_type=jnp.float32
    ) - jnp.einsum("qsat,qsa->qst", kernel_imag, weight_real, preferred_element_type=jnp.float32)
    return jnp.stack([grid_real, grid_imag], axis=2)


def local(sky_image, coef_dual, vis_dual, visibilities, kernel_blocks, tile_rows, tile_counts):
    band_count = lax.axis_size("band")
    group_count = lax.axis_size("vis")
    kernel_here = kernel_blocks[0, 0]
    rows_here = tile_rows[0, 0]
    slot_count = rows_here.shape[1]
    live_slots = (
        jnp.arange(slot_count, dtype=jnp.int32)[None, :] < tile_counts[0, 0][:, None]
    ).astype(jnp.float32)[:, :, None, None]
    vis_data = visibilities[0, 0]
    vis_state = vis_dual[0, 0]
    image_width = sky_image.shape[1]
    stripe = image_width // band_count
    piece_rows = image_width // group_count
    incoming_rows = lax.all_to_all(rows_here, "vis", split_axis=0, concat_axis=0, tiled=True)
    data_part = jnp.sum(live_slots * vis_data * vis_data)
    weights = (live_slots * vis_state).astype(jnp.bfloat16)
    contrib = grid_back(kernel_here, weights)
    arrived = lax.all_to_all(contrib, "vis", split_axis=0, concat_axis=0, tiled=True)
    piece_sum = jax.ops.segment_sum(
        arrived.reshape(-1, 2, piece_rows), incoming_rows.reshape(-1), num_segments=stripe
    )
    adjoint_part = image_from_pieces(piece_sum, band_count, group_count)
    smooth = synthesis(coef_dual)
    new_image = jnp.maximum(sky_image - smooth - adjoint_part, 0.0)
    extrap = 2.0 * new_image - sky_image
    coeffs = analysis(extrap)
    abs_total = jnp.sum(jnp.abs(coeffs))
    coef_total = lax.psum(abs_total, ("band", "vis"))
    threshold = 0.5 * coef_total / (IMG * IMG)
    coef_dual = jnp.clip(coef_dual + coeffs, -threshold, threshold)
    piece_grid = pieces_from_image(extrap, band_count, group_count)
    tiles = lax.all_to_all(
        piece_grid[incoming_rows], "vis", split_axis=0, concat_axis=0, tiled=True
    )
    predicted = degrid(kernel_here, tiles)
    residual = live_slots * (vis_state + predicted - vis_data)
    resid_square = jnp.sum(residual * residual)
    norm_square, data_square = lax.psum((resid_square, data_part), ("band", "vis"))
    radius = 0.5 * jnp.sqrt(data_square + 1e-06)
    size_value = jnp.sqrt(norm_square + 1e-06)
    vis_state = residual * (1.0 - jnp.minimum(1.0, radius / size_value))
    return (new_image, coef_dual, vis_state[None, None])


def solution(mesh):
    return jax.shard_map(
        local,
        mesh=mesh,
        in_specs=(
            P(("band", "vis"), None),
            P(None, ("band", "vis"), None),
            P("band", "vis", None, None, None, None),
            P("band", "vis", None, None, None, None),
            P("band", "vis", None, None, None, None, None),
            P("band", "vis", None, None),
            P("band", "vis", None),
        ),
        out_specs=(
            P(("band", "vis"), None),
            P(None, ("band", "vis"), None),
            P("band", "vis", None, None, None, None),
        ),
        check_vma=False,
    )
```

profile of v0, /device:TPU:0, one launch (start us, length us, event | category | flops | bytes accessed | tf_op | source)
XLA Modules:
  0.0 1030.4 jit_solution(3161300191963925182)
XLA Ops:
  2.1 7.4 all-to-all-start
  15.9 5.8 all-to-all-start.1
  23.0 6.6 all-to-all-done.1
  32.6 7.0 scatter_fusion
  39.6 4.5 all-to-all-start.2
  44.6 77.0 %all-to-all-done.2 = f32[2048,2,1,256]{3,1,2,0:T(2,128)} async-done(((f32[2048,2,1,256]{3,1,2,0:T(2,128)}), f32[2048,2,1,256]{3,1,2,0:T(2,128)}, u32[]{:S(2)}, u32[]{:S(2)}) %all-to-all-start.2) | async-done | bytes 4194336 | tf_op jit(solution)/shard_map/all_to_all | solution.py:111
  121.7 4.6 copy.230
  126.2 5.8 copy.231
  144.5 4.5 fusion.7
  155.7 3.7 multiply_bitcast_fusion.4
  167.6 5.4 copy.244
  172.9 52.8 %all_to_all.118 = f32[2,2,16,128,1,1,128]{3,6,2,0,5,4,1:T(8,128)S(1)} all-to-all(f32[2,2,16,128,1,1,128]{3,6,2,0,5,4,1:T(8,128)} %copy.244), channel_id=1, replica_groups=mesh['band'=2,'vis'=16] {'band'}, dimensions={1} | all-to-all | bytes 8388608 | tf_op jit(solution)/shard_map/all_to_all | solution.py:119
  228.1 19.2 %all-to-all-start.4 = ((f32[2,1,16,128,2,1,128]{3,6,4,0,5,1,2:T(8,128)}), f32[2,1,16,128,2,1,128]{3,6,4,0,5,1,2:T(8,128)}, u32[]{:S(2)}, u32[]{:S(2)}) async-start(f32[2,1,16,128,2,1,128]{3,6,4,0,5,1,2:T(8,128)} %copy.245), calls=%async_computation.4 | async-start | bytes 8388608 | tf_op jit(solution)/shard_map/all_to_all | solution.py:118
  250.9 71.3 %collective-permute-done = f32[4,3,2048]{2,1,0:T(4,128)S(1)} collective-permute-done((f32[4,3,2048]{2,1,0:T(4,128)S(1)}, f32[4,3,2048]{2,1,0:T(4,128)S(1)}, u32[]{:S(2)}, u32[]{:S(2)}) %collective-permute-start) | collective-permute-done | bytes 98336 | tf_op jit(solution)/shard_map/ppermute | solution.py:28
  361.3 4.6 fusion.5
  376.6 3.8 fusion.39
  380.3 4.4 fusion.2
  388.1 3.5 fusion.29
  396.3 3.5 multiply_bitcast_fusion
  402.0 29.7 %all_to_all.119 = f32[2,1,1,128,2,16,128]{3,6,5,2,1,0,4:T(8,128)S(1)} all-to-all(f32[2,1,1,128,2,16,128]{3,6,5,2,1,0,4:T(8,128)S(1)} %copy.267), channel_id=1, replica_groups=mesh['band'=2,'vis'=16] {'band'}, dimensions={4} | all-to-all | bytes 8388608 | tf_op jit(solution)/shard_map/all_to_all | solution.py:88
  434.0 22.5 %all-to-all-start.6 = ((f32[2,2,1,128,1,16,128]{3,6,1,0,4,2,5:T(8,128)}), f32[2,2,1,128,1,16,128]{3,6,1,0,4,2,5:T(8,128)}, u32[]{:S(2)}, u32[]{:S(2)}) async-start(f32[2,2,1,128,1,16,128]{3,6,1,0,4,2,5:T(8,128)} %copy.268), calls=%async_computation.6 | async-start | bytes 8388608 | tf_op jit(solution)/shard_map/all_to_all | solution.py:87
  456.6 3.8 copy.257
  461.3 3.8 collective-permute-start.1
  465.1 41.1 %slice.319 = f32[64,4096]{0,1:T(8,128)} slice(f32[128,4096]{0,1:T(8,128)S(1)} %get-tuple-element.20), slice={[0:128:2], [0:4096:1]} | slice | bytes 2097152 | tf_op jit(solution)/shard_map/slice | solution.py:175
  509.0 17.5 %collective-permute-done.1 = f32[6,4096]{1,0:T(8,128)S(1)} collective-permute-done((f32[6,4096]{1,0:T(8,128)S(1)}, f32[6,4096]{1,0:T(8,128)S(1)}, u32[]{:S(2)}, u32[]{:S(2)}) %collective-permute-start.1) | collective-permute-done | bytes 98336 | tf_op jit(solution)/shard_map/ppermute | solution.py:28
  528.5 3.8 pad_maximum_fusion.1
  532.3 39.0 %slice.321 = f32[64,4096]{0,1:T(8,128)} slice(f32[134,4096]{0,1:T(8,128)} %pad_maximum_fusion.1), slice={[1:129:2], [0:4096:1]} | slice | bytes 2097152 | tf_op jit(solution)/shard_map/slice | solution.py:175
  571.3 39.0 %slice.322 = f32[64,4096]{0,1:T(8,128)} slice(f32[134,4096]{0,1:T(8,128)} %pad_maximum_fusion.1), slice={[2:130:2], [0:4096:1]} | slice | bytes 2097152 | tf_op jit(solution)/shard_map/slice | solution.py:175
  610.2 39.0 %slice.323 = f32[64,4096]{0,1:T(8,128)} slice(f32[134,4096]{0,1:T(8,128)} %pad_maximum_fusion.1), slice={[3:131:2], [0:4096:1]} | slice | bytes 2097152 | tf_op jit(solution)/shard_map/slice | solution.py:175
  649.2 39.0 %slice.324 = f32[64,4096]{0,1:T(8,128)} slice(f32[134,4096]{0,1:T(8,128)} %pad_maximum_fusion.1), slice={[4:132:2], [0:4096:1]} | slice | bytes 2097152 | tf_op jit(solution)/shard_map/slice | solution.py:175
  688.2 39.0 %slice.325 = f32[64,4096]{0,1:T(8,128)} slice(f32[134,4096]{0,1:T(8,128)} %pad_maximum_fusion.1), slice={[5:133:2], [0:4096:1]} | slice | bytes 2097152 | tf_op jit(solution)/shard_map/slice | solution.py:175
  727.1 39.0 %slice.326 = f32[64,4096]{0,1:T(8,128)} slice(f32[134,4096]{0,1:T(8,128)} %pad_maximum_fusion.1), slice={[6:134:2], [0:4096:1]} | slice | bytes 2097152 | tf_op jit(solution)/shard_map/slice | solution.py:175
  766.1 39.0 %slice.327 = f32[64,4096]{0,1:T(8,128)} slice(f32[134,4096]{0,1:T(8,128)} %pad_maximum_fusion.1), slice={[7:134:2], [0:4096:1]} | slice | bytes 2097152 | tf_op jit(solution)/shard_map/slice | solution.py:175
  805.0 5.5 copy.269
  823.0 4.8 fusion
  834.5 3.6 fusion.97
  844.7 27.9 %all-to-all-start.7 = ((bf16[128,2,16,256]{0,3,1,2:T(8,128)(2,1)}), bf16[128,2,16,256]{0,3,1,2:T(8,128)(2,1)}, u32[]{:S(2)}, u32[]{:S(2)}) async-start(bf16[128,2,16,256]{0,3,1,2:T(8,128)(2,1)} %copy.280), calls=%async_computation.7 | async-start | bytes 4194304 | tf_op jit(solution)/shard_map/all_to_all | solution.py:101
  872.6 7.4 multiply_add_fusion.1
  903.2 6.2 slice.328
  936.1 6.2 slice.337
  942.4 4.4 add_bitcast_fusion.3
  950.0 3.9 copy.281
  953.9 5.8 copy.284
  962.6 6.0 all-to-all-start.8
  971.5 4.0 all-to-all-done.8
  980.7 38.1 %all-reduce = (f32[]{:T(128)}, f32[]{:T(128)}, f32[]{:T(128)}) all-reduce(f32[]{:T(128)} %abs_reduce_fusion, f32[]{:T(128)} %get-tuple-element.16, f32[]{:T(128)} %get-tuple-element.15), channel_id=1, replica_groups=mesh['band'=2,'vis'=16] {'band','vis'}, use_global_device_ids=true, to_apply=%region_2.3 | all-reduce | flops 3 | bytes 24 | tf_op jit(solution)/shard_map/psum | solution.py:249
  1020.7 5.0 maximum_minimum_fusion
  1025.7 3.8 copy.290
  (169 shorter events, 203.9 us)
Async XLA Ops:
  0.6 13.6 %copy-start.18 = (bf16[1,1,16,4,2,32,256]{6,5,4,3,2,1,0:T(8,128)(2,1)S(1)}, bf16[1,1,16,4,2,32,256]{6,5,4,3,2,1,0:T(8,128)(2,1)}, u32[]{:S(2)}) copy-start(bf16[1,1,16,4,2,32,256]{6,5,4,3,2,1,0:T(8,128)(2,1)} %param.11) | copy-start | bytes 6291460
  2.1 13.8 %all-to-all-start = ((s32[16,1,4]{2,1,0:T(1,128)}), s32[16,1,4]{2,1,0:T(1,128)S(1)}, u32[]{:S(2)}, u32[]{:S(2)}) async-start(s32[16,1,4]{2,1,0:T(1,128)} %copy.227), calls=%async_computation | async-start | bytes 16384 | tf_op jit(solution)/shard_map/all_to_all | solution.py:235
  10.3 1.0 copy-start.16
  15.9 13.7 %all-to-all-start.1 = ((f32[16,4,2,256]{3,2,1,0:T(2,128)}), f32[16,4,2,256]{3,2,1,0:T(2,128)S(1)}, u32[]{:S(2)}, u32[]{:S(2)}) async-start(f32[16,4,2,256]{3,2,1,0:T(2,128)} %pad_maximum_fusion.17), calls=%async_computation.1 | async-start | bytes 262144 | tf_op jit(solution)/shard_map/all_to_all | solution.py:239
  39.6 82.0 %all-to-all-start.2 = ((f32[2048,2,1,256]{3,1,2,0:T(2,128)}), f32[2048,2,1,256]{3,1,2,0:T(2,128)}, u32[]{:S(2)}, u32[]{:S(2)}) async-start(f32[2048,2,1,256]{3,1,2,0:T(2,128)} %bitcast.318), calls=%async_computation.2 | async-start | bytes 8388608 | tf_op jit(solution)/shard_map/all_to_all | solution.py:111
  228.1 19.2 %copy-start = (f32[4,64,2048]{2,1,0:T(8,128)S(1)}, f32[4,64,2048]{2,1,0:T(8,128)}, u32[]{:S(2)}) copy-start(f32[4,64,2048]{2,1,0:T(8,128)} %param.8) | copy-start | bytes 6291460
  228.1 120.3 %all-to-all-start.4 = ((f32[2,1,16,128,2,1,128]{3,6,4,0,5,1,2:T(8,128)}), f32[2,1,16,128,2,1,128]{3,6,4,0,5,1,2:T(8,128)}, u32[]{:S(2)}, u32[]{:S(2)}) async-start(f32[2,1,16,128,2,1,128]{3,6,4,0,5,1,2:T(8,128)} %copy.245), calls=%async_computation.4 | async-start | bytes 8388608 | tf_op jit(solution)/shard_map/all_to_all | solution.py:118
  247.3 74.8 %collective-permute-start = (f32[4,3,2048]{2,1,0:T(4,128)S(1)}, f32[4,3,2048]{2,1,0:T(4,128)S(1)}, u32[]{:S(2)}, u32[]{:S(2)}) collective-permute-start(f32[4,3,2048]{2,1,0:T(4,128)S(1)} %slice.284), channel_id=1, source_target_pairs={{31,0},{0,1},{1,2},{2,3},{3,4},{4,5},{5,6},{6,7},{7,8},{8,9},{9,10... | collective-permute-start | bytes 294920 | tf_op jit(solution)/shard_map/ppermute | solution.py:28
  342.3 1.7 copy-start.5
  372.7 1.6 copy-start.2
  372.7 2.2 copy-start.4
  434.0 371.0 %all-to-all-start.6 = ((f32[2,2,1,128,1,16,128]{3,6,1,0,4,2,5:T(8,128)}), f32[2,2,1,128,1,16,128]{3,6,1,0,4,2,5:T(8,128)}, u32[]{:S(2)}, u32[]{:S(2)}) async-start(f32[2,2,1,128,1,16,128]{3,6,1,0,4,2,5:T(8,128)} %copy.268), calls=%async_computation.6 | async-start | bytes 8388608 | tf_op jit(solution)/shard_map/all_to_all | solution.py:87
  461.3 65.2 %collective-permute-start.1 = (f32[6,4096]{1,0:T(8,128)S(1)}, f32[6,4096]{1,0:T(8,128)S(1)}, u32[]{:S(2)}, u32[]{:S(2)}) collective-permute-start(f32[6,4096]{1,0:T(8,128)S(1)} %copy.255), channel_id=1, source_target_pairs={{1,0},{2,1},{3,2},{4,3},{5,4},{6,5},{7,6},{8,7},{9,8},{10,9},{11,1... | collective-permute-start | bytes 294920 | tf_op jit(solution)/shard_map/ppermute | solution.py:28
  844.7 27.9 %copy-start.3 = (f32[64,4096]{0,1:T(8,128)S(1)}, f32[64,4096]{0,1:T(8,128)}, u32[]{:S(2)}) copy-start(f32[64,4096]{0,1:T(8,128)} %slice.319) | copy-start | bytes 3145732
  844.7 105.3 %all-to-all-start.7 = ((bf16[128,2,16,256]{0,3,1,2:T(8,128)(2,1)}), bf16[128,2,16,256]{0,3,1,2:T(8,128)(2,1)}, u32[]{:S(2)}, u32[]{:S(2)}) async-start(bf16[128,2,16,256]{0,3,1,2:T(8,128)(2,1)} %copy.280), calls=%async_computation.7 | async-start | bytes 4194304 | tf_op jit(solution)/shard_map/all_to_all | solution.py:101
  880.0 1.4 copy-start.1
  942.4 4.4 copy-start.6
  942.4 4.4 copy-start.7
  942.4 4.4 copy-start.8
  942.4 4.4 copy-start.9
  942.4 4.7 copy-start.10
  942.4 5.0 copy-start.11
  942.4 5.3 copy-start.12
  942.4 5.5 copy-start.13
  962.6 12.9 %all-to-all-start.8 = ((bf16[16,4,2,256]{3,2,1,0:T(2,128)(2,1)}), bf16[16,4,2,256]{3,2,1,0:T(2,128)(2,1)S(1)}, u32[]{:S(2)}, u32[]{:S(2)}) async-start(bf16[16,4,2,256]{3,2,1,0:T(2,128)(2,1)} %bitcast.95), calls=%async_computation.8 | async-start | bytes 131072 | tf_op jit(solution)/shard_map/all_to_all | solution.py:253
  975.5 3.5 copy-start.19
  977.4 2.5 copy-start.14
  977.4 2.5 copy-start.15
  977.4 2.5 copy-start.17
where the time goes:
time: 1040 us; the launch traced here: 1030 us
  local copies, waits for them, and re-layouts  472 us (45%)
  waiting for transfers between devices  177 us (17%)
  blocking collectives  121 us (12%)
  matrix products  108 us (10%)
  starting transfers between devices  97.5 us (9%)
  other arithmetic  51.9 us (5%)
    slice x8, local copies, waits for them, and re-layouts, analysis(): taken = extended[offset:offset + 2 * half_rows:2]  314 us
    ppermute x2, waiting for transfers between devices, shifted(): return lax.ppermute(block, axis, route)  88.9 us
    all_to_all x1, waiting for transfers between devices, image_from_pieces(): lax.all_to_all(piece_sum.reshape(stripe, 2, 1, piece_rows), 'vis', split_...  77 us
    slice x16, local copies, waits for them, and re-layouts, cols_down(): taken = extended[:, offset:offset + image_width:2]  58.4 us
    all_to_all x1, blocking collectives, image_from_pieces(): lax.all_to_all(shaped, 'band', split_axis=1, concat_axis=4, tiled=True)  52.8 us
    dot_general x14, matrix products, section_one(): return jnp.einsum('kn,...nm->...km', table, values, precision=highest)  51.9 us
    dot_general x14, matrix products, section_two(): return jnp.einsum('qm,...km->...qk', table, values, precision=highest)  48.1 us
    psum x1, blocking collectives, local(): coef_total = lax.psum(abs_total, ('band', 'vis'))  38.1 us
  transfers between devices with their start and end apart: 9, of which 6 were waited for; matrix products, arithmetic and copies ran while one was open for 43% of the time, Pallas kernels for 0%

commit v1 on v0

v1 whole, which is shorter than its diff:
```python
import math

import jax
import jax.numpy as jnp
import numpy as np
from jax import lax
from jax.experimental import pallas as pl
from jax.experimental.pallas import tpu as pltpu
from jax.sharding import PartitionSpec as P

LANES = 128
FLAG = 1 << 20

low_taps = (
    -0.010597401784997278,
    0.032883011666982945,
    0.030841381835986965,
    -0.18703481171888114,
    -0.02798376941698385,
    0.6308807679295904,
    0.7148465705525415,
    0.23037781330885523,
)
high_taps = tuple(((-1.0) ** offset * low_taps[7 - offset] for offset in range(8)))
AXES = ("band", "vis")
bf16 = jnp.bfloat16
f32 = jnp.float32


def shifted(block, axis, distance):
    devices = range(lax.axis_size(axis))
    route = [((i - distance) % len(devices), i) for i in devices]
    return lax.ppermute(block, axis, route)


def flipped(block, axis, mask):
    return lax.ppermute(block, axis, [(i, i ^ mask) for i in range(lax.axis_size(axis))])


def split_two(values):
    high = lax.reduce_precision(values, 8, 7)
    return high.astype(bf16), (values - high).astype(bf16)


def split_here(values):
    high = values.astype(bf16)
    return high, (values - high.astype(f32)).astype(bf16)


def dot_nn(left, right):
    return lax.dot_general(left, right, (((1,), (0,)), ((), ())), preferred_element_type=f32)


def dot_nt(left, right):
    return lax.dot_general(left, right, (((1,), (1,)), ((), ())), preferred_element_type=f32)


def dot_three(dot, left, right):
    return dot(left[0], right[0]) + dot(left[0], right[1]) + dot(left[1], right[0])


def scaled_sum(terms):
    total = None
    for weight, value in terms:
        if abs(weight) < 1e-12:
            continue
        part = value if weight == 1.0 else weight * value
        total = part if total is None else total + part
    return total


def cosine_sums(values, size):
    if size == 1:
        return [values[0] + values[1], values[0] - values[1]]
    half = size // 2
    even = cosine_sums(values[0::2], half)
    out = [None] * (size + 1)
    for a in range(half):
        odd = scaled_sum(
            [(math.cos(math.pi * k * a / size) if a else 1.0, values[k]) for k in range(1, size, 2)]
        )
        out[a] = even[a] + odd
        out[size - a] = even[a] - odd
    out[half] = even[half]
    return out


def sine_sums(values, size):
    half = size // 2
    out = [None] * (size + 1)
    if size == 2:
        out[1] = values[1]
        return out
    even = sine_sums(values[0::2], half)
    for a in range(1, half):
        odd = scaled_sum([(math.sin(math.pi * k * a / size), values[k]) for k in range(1, size, 2)])
        out[a] = odd + even[a]
        out[size - a] = odd - even[a]
    out[half] = scaled_sum([(math.sin(math.pi * k / 2), values[k]) for k in range(1, size, 2)])
    return out


def twiddle_seeds(image_width):
    outer = image_width // LANES
    kept = outer // 2 + 1
    inner = image_width // outer
    c = np.arange(LANES)
    one = 2.0 * np.pi * (np.arange(kept)[:, None] * c[None, :] % image_width) / image_width
    two = 2.0 * np.pi * (np.arange(inner)[:, None] * c[None, :] % inner) / inner
    one = np.stack([np.cos(one), np.sin(one)], axis=1).astype(np.float32)
    two = np.stack([np.cos(two), np.sin(two)]).astype(np.float32)
    return jnp.asarray(one), jnp.asarray(two)


def upright(row):
    return jnp.broadcast_to(row, (8, row.shape[1])).T[:, 0:1]


def sign_of(code):
    return jnp.where(code >= FLAG, -1.0, 1.0).astype(f32)


def whole(array):
    return pl.BlockSpec(array.shape, lambda i: (0,) * array.ndim)


def adjoint_map(tile_real, tile_imag, codes, weight_tables, phases, sky_image, smooth):
    blocks_c, blocks_a, blocks_b, blocks_f, tiles, length = tile_real.shape
    blocks_ab = blocks_a * blocks_b
    blocks = blocks_c * blocks_ab * blocks_f
    rows, image_width = sky_image.shape
    outer = image_width // LANES
    kept = outer // 2 + 1
    inner = image_width // outer
    width = kept * inner
    seeds = twiddle_seeds(image_width)
    each = -(-kept // blocks)

    def kernel(
        tre, tim, code_ref, wrh, wrl, wih, wil, pc, ps, one, two, sky, smo,
        new_ref, ext_ref, x_ref, grid_ref, mid_ref, y_ref, mh, ml,
    ):
        step = pl.program_id(0)

        @pl.when(step == 0)
        def _():
            grid_ref[...] = jnp.zeros_like(grid_ref)

        @pl.when(step < blocks)
        def _():
            re = tre[0, 0, 0, 0]
            im = tim[0, 0, 0, 0]
            half = (
                dot_nt(wrh[...], re) + dot_nt(wrl[...], re)
                + dot_nt(wih[...], im) + dot_nt(wil[...], im)
            )
            half_re = half[:rows]
            half_im = half[rows:]
            code = code_ref[0]
            turned_re = pc[...] * half_re - ps[...] * half_im
            turned_im = (pc[...] * half_im + ps[...] * half_re) * sign_of(code)
            turned = jnp.concatenate([turned_re, turned_im], axis=0).astype(bf16)
            column = upright(code & (FLAG - 1))
            lanes = lax.broadcasted_iota(jnp.int32, (tiles, inner), 1)
            within = (lanes == column % inner).astype(f32).astype(bf16)
            major = jnp.broadcast_to((column // inner).astype(f32), (tiles, inner)).astype(bf16)
            zero = jnp.zeros_like(within)
            for begin in range(0, kept, 2):
                hots = [
                    jnp.where(major == jnp.asarray(k, bf16), within, zero)
                    for k in range(begin, min(begin + 2, kept))
                ]
                span = slice(begin * inner, (begin + len(hots)) * inner)
                grid_ref[:, span] += dot_nn(turned, jnp.concatenate(hots, axis=1))
            for u in range(each):
                k = jnp.minimum(step * each + u, kept - 1)
                c1 = one[k, 0:1, :]
                s1 = one[k, 1:2, :]
                c2 = two[0]
                s2 = two[1]
                real = split_here(c1 * c2 - s1 * s2)
                imag = split_here(c1 * s2 + s1 * c2)
                for out, re, im in ((mh, real[0], imag[0]), (ml, real[1], imag[1])):
                    out[k, 0:inner, 0:LANES] = re
                    out[k, 0:inner, LANES : 2 * LANES] = im
                    out[k, inner : 2 * inner, 0:LANES] = -im
                    out[k, inner : 2 * inner, LANES : 2 * LANES] = re

        @pl.when(step == blocks)
        def _():
            for k in range(kept):
                cell = jnp.concatenate(
                    [
                        grid_ref[:rows, k * inner : (k + 1) * inner],
                        grid_ref[rows:, k * inner : (k + 1) * inner],
                    ],
                    axis=1,
                )
                mid_ref[k] = dot_three(dot_nn, split_here(cell), (mh[k], ml[k]))

            def body(chunk, carry):
                at = pl.ds(pl.multiple_of(chunk * 8, 8), 8)
                real = [mid_ref[k, at, 0:LANES] for k in range(kept)]
                imag = [mid_ref[k, at, LANES : 2 * LANES] for k in range(kept)]
                even = cosine_sums(real, outer // 2)
                odd = sine_sums(imag, outer // 2)
                values = []
                for a in range(outer):
                    if a == 0 or a == outer // 2:
                        back = even[a]
                    elif a < outer // 2:
                        back = even[a] - odd[a]
                    else:
                        back = even[outer - a] + odd[outer - a]
                    span = slice(a * LANES, (a + 1) * LANES)
                    old = sky[at, span]
                    new = jnp.maximum(old - smo[at, span] - back, 0.0)
                    extrap = 2.0 * new - old
                    new_ref[at, span] = new
                    ext_ref[at, span] = extrap
                    values.append(extrap)
                mirrored = outer // 2
                even = [values[0]]
                odd = [None]
                for a in range(1, mirrored):
                    even.append(values[a] + values[outer - a])
                    odd.append(values[a] - values[outer - a])
                even.append(values[mirrored])
                odd.append(None)
                real = cosine_sums(even, mirrored)
                imag = sine_sums(odd, mirrored)
                for k in range(kept):
                    y_ref[k, at, 0:LANES] = real[k]
                    y_ref[k, at, LANES : 2 * LANES] = (
                        jnp.zeros_like(real[k]) if imag[k] is None else -imag[k]
                    )
                return carry

            lax.fori_loop(0, rows // 8, body, 0)
            for k in range(kept):
                high, low = split_here(y_ref[k])
                if rows % LANES == 0:
                    both = dot_nt(mh[k], jnp.concatenate([high, low], axis=0))
                    both = both[:, :rows] + both[:, rows:] + dot_nt(ml[k], high)
                else:
                    both = dot_three(dot_nt, (mh[k], ml[k]), (high, low))
                x_ref[k * inner : (k + 1) * inner, :] = jnp.concatenate(
                    [both[:inner], both[inner:]], axis=1
                )

    def tile_block_a(i):
        i = jnp.minimum(i, blocks - 1)
        j, f = i // blocks_f, i % blocks_f
        return (j // blocks_ab, j // blocks_b % blocks_a, j % blocks_b, f, 0, 0)

    def tile_block_b(i):
        c, y, x, f, _, _ = tile_block_a(i)
        return (c, x, y, f, 0, 0)

    image = jax.ShapeDtypeStruct((rows, image_width), f32)
    return pl.pallas_call(
        kernel,
        grid=(blocks + 1,),
        in_specs=[
            pl.BlockSpec((1, 1, 1, 1, tiles, length), tile_block_a),
            pl.BlockSpec((1, 1, 1, 1, tiles, length), tile_block_b),
            pl.BlockSpec((1, 1, tiles), lambda i: (jnp.minimum(i, blocks - 1), 0, 0)),
            *[whole(w) for w in weight_tables],
            *[whole(p) for p in phases],
            *[whole(t) for t in seeds],
            whole(sky_image),
            whole(smooth),
        ],
        out_specs=[
            pl.BlockSpec((rows, image_width), lambda i: (0, 0)),
            pl.BlockSpec((rows, image_width), lambda i: (0, 0)),
            pl.BlockSpec((width, 2 * rows), lambda i: (0, 0)),
        ],
        out_shape=[image, image, jax.ShapeDtypeStruct((width, 2 * rows), f32)],
        scratch_shapes=[
            pltpu.VMEM((2 * rows, width), f32),
            pltpu.VMEM((kept, rows, 2 * LANES), f32),
            pltpu.VMEM((kept, rows, 2 * LANES), f32),
            pltpu.VMEM((kept, 2 * inner, 2 * LANES), bf16),
            pltpu.VMEM((kept, 2 * inner, 2 * LANES), bf16),
        ],
        cost_estimate=pl.CostEstimate(
            flops=8 * blocks * rows * tiles * (width + length), bytes_accessed=1 << 24, transcendentals=0
        ),
        name="adjoint",
    )(tile_real, tile_imag, codes, *weight_tables, *phases, *seeds, sky_image, smooth)


def forward_parts(spectrum, codes, weight_tables, phases, part, counts):
    blocks_a, blocks_b, blocks_f = counts
    blocks = blocks_a * blocks_b * blocks_f
    tiles = codes.shape[2]
    width, rows2 = spectrum.shape
    rows = rows2 // 2
    length = weight_tables[0].shape[1]
    together = 16

    def kernel(x_ref, where, code_ref, wrh, wrl, wih, wil, pc, ps, out_ref, pick_ref):
        def body(chunk, carry):
            begin = chunk * together
            found = [
                x_ref[pl.ds(where[0, 0, begin + u] & (FLAG - 1), 1), :] for u in range(together)
            ]
            for u in range(together):
                pick_ref[pl.ds(begin + u, 1), :] = found[u]
            return carry

        lax.fori_loop(0, tiles // together, body, 0)
        sign = upright(sign_of(code_ref[0]))
        real = pick_ref[:, :rows]
        imag = pick_ref[:, rows:] * sign
        turned_re = pc[...] * real + ps[...] * imag
        turned_im = pc[...] * imag - ps[...] * real
        turned = split_here(jnp.concatenate([turned_re, turned_im], axis=1))
        out_ref[0, 0, 0, 0] = dot_three(dot_nn, turned, (wrh[...], wrl[...]))
        out_ref[1, 0, 0, 0] = dot_three(dot_nn, turned, (wih[...], wil[...]))

    return pl.pallas_call(
        kernel,
        grid=(blocks,),
        in_specs=[
            whole(spectrum),
            pl.BlockSpec((1, 1, tiles), lambda i: (part * blocks + i, 0, 0), memory_space=pltpu.SMEM),
            pl.BlockSpec((1, 1, tiles), lambda i: (part * blocks + i, 0, 0)),
            *[whole(w) for w in weight_tables],
            *[whole(p) for p in phases],
        ],
        out_specs=pl.BlockSpec(
            (2, 1, 1, 1, tiles, length),
            lambda i: (0, i // blocks_f // blocks_b, i // blocks_f % blocks_b, i % blocks_f, 0, 0),
        ),
        out_shape=jax.ShapeDtypeStruct((2, *counts, tiles, length), f32),
        scratch_shapes=[pltpu.VMEM((tiles, 2 * rows), f32)],
        cost_estimate=pl.CostEstimate(
            flops=24 * blocks * rows * tiles * length, bytes_accessed=1 << 23, transcendentals=0
        ),
        name="parts",
    )(spectrum, codes, codes, *weight_tables, *phases)


def row_matrix_up(half_rows, lead):
    ext = half_rows + lead
    matrix = np.zeros((2 * half_rows, 2 * ext), np.float64)
    for n in range(2 * half_rows):
        for k in range(-3, half_rows):
            tap = n - 2 * k
            if 0 <= tap < 8:
                matrix[n, lead + k] = low_taps[tap]
                matrix[n, ext + lead + k] = high_taps[tap]
    return matrix


def row_matrix_down(rows, tail):
    matrix = np.zeros((rows, rows + tail), np.float64)
    for k in range(rows // 2):
        for j in range(8):
            matrix[k, 2 * k + j] = low_taps[j]
            matrix[rows // 2 + k, 2 * k + j] = high_taps[j]
    return matrix


def col_matrix_up():
    matrix = np.zeros((4, LANES, 2 * LANES), np.float64)
    for n in range(2 * LANES):
        for k in range(-LANES, LANES):
            tap = n - 2 * k
            if 0 <= tap < 8:
                where = (0, k + LANES) if k < 0 else (1, k)
                matrix[where[0], where[1], n] = low_taps[tap]
                matrix[2 + where[0], where[1], n] = high_taps[tap]
    return matrix.reshape(4 * LANES, 2 * LANES)


def col_matrix_down():
    matrix = np.zeros((3 * LANES, 2 * LANES), np.float64)
    for k in range(LANES):
        for j in range(8):
            matrix[2 * k + j, k] = low_taps[j]
            matrix[2 * k + j, LANES + k] = high_taps[j]
    return matrix


def split_constant(matrix):
    value = np.asarray(matrix, np.float32)
    high = value.astype(bf16)
    low = (value - high.astype(np.float32)).astype(bf16)
    return jnp.asarray(high), jnp.asarray(low)


def synthesis(halo, coef_dual):
    _, half_rows, half_width = coef_dual.shape
    rows = 2 * half_rows
    lead = halo.shape[1]
    row_tables = split_constant(row_matrix_up(half_rows, lead))
    col_tables = split_constant(col_matrix_up())

    def kernel(halo_ref, coef_ref, rh, rl, ch, cl, out_ref):
        sides = []
        for first, second in ((0, 2), (1, 3)):
            ext = jnp.concatenate(
                [halo_ref[first], coef_ref[first], halo_ref[second], coef_ref[second]], axis=0
            )
            sides.append(dot_three(dot_nn, (rh[...], rl[...]), split_here(ext)))
        low = split_here(sides[0])
        high = split_here(sides[1])
        count = half_width // LANES
        for j in range(count):
            here = slice(j * LANES, (j + 1) * LANES)
            past = (j - 1) % count
            before = slice(past * LANES, (past + 1) * LANES)
            operands = tuple(
                jnp.concatenate(
                    [low[p][:, before], low[p][:, here], high[p][:, before], high[p][:, here]],
                    axis=1,
                )
                for p in range(2)
            )
            out_ref[:, 2 * j * LANES : 2 * (j + 1) * LANES] = dot_three(
                dot_nn, operands, (ch[...], cl[...])
            )

    return pl.pallas_call(
        kernel,
        out_shape=jax.ShapeDtypeStruct((rows, 2 * half_width), f32),
        cost_estimate=pl.CostEstimate(flops=1 << 30, bytes_accessed=1 << 22, transcendentals=0),
        name="synthesis",
    )(halo, coef_dual, *row_tables, *col_tables)


def analysis(extrap, halo, coef_dual):
    rows, image_width = extrap.shape
    half_rows = rows // 2
    half_width = image_width // 2
    row_tables = split_constant(row_matrix_down(rows, halo.shape[0]))
    col_tables = split_constant(col_matrix_down())

    def kernel(ext_ref, halo_ref, coef_ref, rh, rl, ch, cl, out_ref, sum_ref):
        ext = jnp.concatenate([ext_ref[...], halo_ref[...]], axis=0)
        sides = split_here(dot_three(dot_nn, (rh[...], rl[...]), split_here(ext)))
        count = half_width // LANES
        total = jnp.zeros((half_rows, LANES), f32)
        for j in range(count):
            here = slice(2 * j * LANES, 2 * (j + 1) * LANES)
            after = 2 * ((j + 1) % count)
            tail = slice(after * LANES, (after + 1) * LANES)
            operands = tuple(
                jnp.concatenate([sides[p][:, here], sides[p][:, tail]], axis=1) for p in range(2)
            )
            both = dot_three(dot_nn, operands, (ch[...], cl[...]))
            span = slice(j * LANES, (j + 1) * LANES)
            for index, part in enumerate(
                (
                    both[:half_rows, :LANES],
                    both[:half_rows, LANES:],
                    both[half_rows:, :LANES],
                    both[half_rows:, LANES:],
                )
            ):
                total = total + jnp.abs(part)
                out_ref[index, :, span] = coef_ref[index, :, span] + part
        sum_ref[...] = jnp.sum(total.reshape(half_rows // 8, 8, LANES), axis=0)

    return pl.pallas_call(
        kernel,
        out_shape=[
            jax.ShapeDtypeStruct(coef_dual.shape, f32),
            jax.ShapeDtypeStruct((8, LANES), f32),
        ],
        cost_estimate=pl.CostEstimate(flops=1 << 30, bytes_accessed=1 << 22, transcendentals=0),
        name="analysis",
    )(extrap, halo, coef_dual, *row_tables, *col_tables)


def stacked(value, axis, masks, place=0):
    return jnp.stack([value] + [flipped(value, axis, mask) for mask in masks], axis=place)


def exchanged(values):
    count = lax.axis_size(AXES)
    sent = jnp.broadcast_to(values[None, :], (count, values.shape[0]))
    return lax.all_to_all(sent, AXES, split_axis=0, concat_axis=0, tiled=True)


def local(sky_image, coef_dual, vis_dual, visibilities, kernel_blocks, tile_rows, tile_counts):
    band_count = lax.axis_size("band")
    group_count = lax.axis_size("vis")
    band_here = lax.axis_index("band")
    group_here = lax.axis_index("vis")
    device = band_here * group_count + group_here
    kernel_here = kernel_blocks[0, 0]
    rows_here = tile_rows[0, 0]
    owners, slot_count = rows_here.shape
    rows, image_width = sky_image.shape
    stripe = image_width // band_count
    samples, length = kernel_here.shape[-2:]
    half_rows = coef_dual.shape[1]
    outer = image_width // LANES
    inner = image_width // outer
    vis_tiles = owners * slot_count
    far = group_count // 4
    tiles = min(far * vis_tiles, max(vis_tiles, 256))
    blocks_f = far * vis_tiles // tiles
    masks_x = tuple(range(1, band_count))
    masks_z = tuple(range(4, group_count, 4))

    live_slots = (
        jnp.arange(slot_count, dtype=jnp.int32)[None, :] < tile_counts[0, 0][:, None]
    ).astype(f32)[:, :, None, None]
    vis_data = visibilities[0, 0]
    vis_state = vis_dual[0, 0]

    cell = band_here * stripe + rows_here.reshape(-1)
    mirrored = cell % outer > outer // 2
    kept_cell = jnp.where(mirrored, image_width - cell, cell)
    code = (kept_cell % outer) * inner + kept_cell // outer + jnp.where(mirrored, FLAG, 0)
    data_part = jnp.sum(live_slots * vis_data * vis_data)
    told = exchanged(jnp.concatenate([code.astype(f32), data_part[None]]))
    data_square = jnp.sum(told[:, vis_tiles])
    by_core = jnp.arange(2)[:, None, None, None]
    by_y = 2 * jnp.arange(2)[None, :, None, None]
    by_x = jnp.arange(band_count)[None, None, :, None]
    by_z = 4 * jnp.arange(far)[None, None, None, :]
    origin = (band_here ^ by_x) * group_count + (group_here ^ (by_core + by_y + by_z))
    chosen = origin.reshape(-1, 1) == jnp.arange(band_count * group_count)[None, :]
    codes = jnp.dot(chosen.astype(f32), told, precision=lax.Precision.HIGHEST)
    codes = jnp.round(codes[:, :vis_tiles]).astype(jnp.int32)
    codes = codes.reshape(4 * band_count * blocks_f, 1, tiles)

    lead = min(8, half_rows)
    coef_halo = shifted(coef_dual[:, half_rows - lead :, :], AXES, 1)

    weights = (live_slots * vis_state).astype(bf16)
    kernel_flat = kernel_here.reshape(vis_tiles, 2 * samples, length)
    weight_real = weights[:, :, 0].reshape(vis_tiles, samples)
    weight_imag = weights[:, :, 1].reshape(vis_tiles, samples)
    weight_pair = jnp.stack(
        [
            jnp.concatenate([weight_real, weight_imag], axis=1),
            jnp.concatenate([weight_imag, -weight_real], axis=1),
        ]
    )
    sent = jnp.einsum("nmt,ynm->ynt", kernel_flat, weight_pair, preferred_element_type=f32)
    sent = sent.astype(bf16)

    own_rows = device * rows + jnp.arange(rows, dtype=jnp.int32)

    def turns(steps):
        angle = (2.0 * math.pi / image_width) * (steps % image_width).astype(f32)
        return jnp.cos(angle), jnp.sin(angle)

    wave_cos, wave_sin = turns(own_rows[:, None] * jnp.arange(length, dtype=jnp.int32)[None, :])
    scale = 1.0 / image_width
    weight_tables = (
        *split_two(scale * jnp.concatenate([wave_cos, wave_sin], axis=0)),
        *split_two(scale * jnp.concatenate([-wave_sin, wave_cos], axis=0)),
    )
    owner_of = jnp.arange(tiles, dtype=jnp.int32) // slot_count % owners
    phases = turns(own_rows[:, None] * (owner_of * length)[None, :])
    phases_turned = tuple(p.T for p in phases)

    level = stacked(sent, "vis", masks_z, 1)
    level, weight_tables, phases, phases_turned = lax.optimization_barrier(
        (level, weight_tables, phases, phases_turned)
    )
    tile_real = stacked(level[0], "band", masks_x)
    tile_imag = stacked(level[1], "vis", (2,))
    smooth = synthesis(coef_halo, coef_dual)
    tile_real, tile_imag, smooth = lax.optimization_barrier((tile_real, tile_imag, smooth))
    tile_real = stacked(tile_real, "vis", (2,))
    tile_imag = stacked(tile_imag, "band", masks_x)
    tile_real = stacked(tile_real, "vis", (1,))
    tile_imag = stacked(tile_imag, "vis", (1,))
    tile_real = tile_real.reshape(2, 2, band_count, blocks_f, tiles, length)
    tile_imag = tile_imag.reshape(2, band_count, 2, blocks_f, tiles, length)

    new_image, extrap, spectrum = adjoint_map(
        tile_real, tile_imag, codes, weight_tables, phases, sky_image, smooth
    )

    parts = [
        forward_parts(spectrum, codes, weight_tables, phases_turned, part, (2, band_count, blocks_f))
        for part in (1, 0)
    ]
    paired = parts[1] + flipped(parts[0], "vis", 1)
    part_real = paired[0, 0] + flipped(paired[0, 1], "vis", 2)
    part_imag = paired[1, :, 0]
    for mask in masks_x:
        part_imag = part_imag + flipped(paired[1, :, mask], "band", mask)
    part_imag = part_imag[0] + flipped(part_imag[1], "vis", 2)
    left_real = part_real[0]
    for mask in masks_x:
        left_real = left_real + flipped(part_real[mask], "band", mask)
    left = jnp.stack([left_real, part_imag]).reshape(2, far, vis_tiles, length)
    seen = left[:, 0]
    for index, mask in enumerate(masks_z):
        seen = seen + flipped(left[:, 1 + index], "vis", mask)

    image_halo = shifted(extrap[: min(8, rows)], AXES, -1)
    moved_coef, abs_parts = analysis(extrap, image_halo, coef_dual)

    seen = lax.reduce_precision(seen, 8, 7).astype(bf16)
    met = jnp.einsum("nmt,ynt->nym", kernel_flat, seen, preferred_element_type=f32)
    predicted = jnp.stack(
        [
            met[:, 0, :samples] - met[:, 1, samples:],
            met[:, 1, :samples] + met[:, 0, samples:],
        ],
        axis=1,
    ).reshape(vis_state.shape)
    residual = live_slots * (vis_state + predicted - vis_data)
    sums = jnp.sum(
        exchanged(jnp.stack([jnp.sum(residual * residual), jnp.sum(abs_parts)])), axis=0
    )
    threshold = 0.5 * sums[1] / (image_width * image_width)
    new_coef = jnp.clip(moved_coef, -threshold, threshold)
    radius = 0.5 * jnp.sqrt(data_square + 1e-06)
    size_value = jnp.sqrt(sums[0] + 1e-06)
    new_vis = residual * (1.0 - jnp.minimum(1.0, radius / size_value))
    return (new_image, new_coef, new_vis[None, None])


def solution(mesh):
    return jax.shard_map(
        local,
        mesh=mesh,
        in_specs=(
            P(("band", "vis"), None),
            P(None, ("band", "vis"), None),
            P("band", "vis", None, None, None, None),
            P("band", "vis", None, None, None, None),
            P("band", "vis", None, None, None, None, None),
            P("band", "vis", None, None),
            P("band", "vis", None),
        ),
        out_specs=(
            P(("band", "vis"), None),
            P(None, ("band", "vis"), None),
            P("band", "vis", None, None, None, None),
        ),
        check_vma=False,
    )
```

time: 1040 us -> 158 us (0.15)
  local copies, waits for them, and re-layouts: 472 us -> 9.99 us
  waiting for transfers between devices: 177 us -> 33.2 us
  blocking collectives: 121 us -> 0 us
  matrix products: 108 us -> 1.24 us
  starting transfers between devices: 97.5 us -> 33.8 us
  Pallas kernels: 0 us -> 50.7 us
  other arithmetic: 51.9 us -> 25.3 us
    slice x32 -> x5, local copies, waits for them, and re-layouts: 379 us -> 2.91 us  [the longest x1 0.97 us: local(): coef_halo = shifted(coef_dual[:, half_rows - lead:, :], AXES, 1)]
    dot_general x36 -> x3, matrix products: 108 us -> 1.24 us  [the longest x1 0.64 us: local(): jnp.einsum('nmt,ynt->nym', kernel_flat, seen, preferred_element_type=f32)]
    ppermute x2, waiting for transfers between devices: 88.9 us -> 0.01 us  [shifted(): return lax.ppermute(block, axis, route)]
    all_to_all x2 -> x0, blocking collectives: 82.5 us -> none  [the longest x1 52.8 us: image_from_pieces(): lax.all_to_all(shaped, 'band', split_axis=1, concat_axis=4, tiled=True)]
    all_to_all x7 -> x2, starting transfers between devices: 93.3 us -> 11.2 us  [exchanged(): return lax.all_to_all(sent, AXES, split_axis=0, concat_axis=0, tiled=True)]
    all_to_all x7 -> x2, waiting for transfers between devices: 87.9 us -> 5.72 us  [exchanged(): return lax.all_to_all(sent, AXES, split_axis=0, concat_axis=0, tiled=True)]
    pallas_call x0 -> x5, Pallas kernels: none -> 50.7 us  [the longest x1 20.6 us: adjoint_map(): pl.pallas_call(kernel, grid=(blocks + 1,), in_specs=[pl.BlockSpec((1, 1,...]
    psum x1 -> x0, blocking collectives: 38.1 us -> none  [local(): coef_total = lax.psum(abs_total, ('band', 'vis'))]
  transfers between devices with their start and end apart: 9 -> 21, of which waited for: 6 -> 9; matrix products, arithmetic and copies ran while one was open for 43% -> 12% of each run, Pallas kernels for 0% -> 13%
where the time goes in v1:
time: 158 us; the launch traced here: 157 us
  Pallas kernels  50.7 us (32%)
  starting transfers between devices  33.8 us (21%)
  waiting for transfers between devices  33.2 us (21%)
  other arithmetic  25.3 us (16%)
  local copies, waits for them, and re-layouts  9.99 us (6%)
  between operations  3.04 us (2%)
    ppermute x17, waiting for transfers between devices, flipped(): lax.ppermute(block, axis, [(i, i ^ mask) for i in range(lax.axis_size(axi...  27.5 us
    pallas_call x1, Pallas kernels, adjoint_map(): pl.pallas_call(kernel, grid=(blocks + 1,), in_specs=[pl.BlockSpec((1, 1,...  20.6 us
    ppermute x17, starting transfers between devices, flipped(): lax.ppermute(block, axis, [(i, i ^ mask) for i in range(lax.axis_size(axi...  19.4 us
    pallas_call x2, Pallas kernels, forward_parts(): pl.pallas_call(kernel, grid=(blocks,), in_specs=[whole(spectrum), pl.Bloc...  17.8 us
    all_to_all x2, starting transfers between devices, exchanged(): return lax.all_to_all(sent, AXES, split_axis=0, concat_axis=0, tiled=True)  11.2 us
    pallas_call x1, Pallas kernels, analysis(): pl.pallas_call(kernel, out_shape=[jax.ShapeDtypeStruct(coef_dual.shape, f...  6.39 us
    another operation x6, other arithmetic, stacked(): jnp.stack([value] + [flipped(value, axis, mask) for mask in masks], axis=...  6.28 us
    pallas_call x1, Pallas kernels, synthesis(): pl.pallas_call(kernel, out_shape=jax.ShapeDtypeStruct((rows, 2 * half_wid...  5.85 us
  transfers between devices with their start and end apart: 21, of which 9 were waited for; matrix products, arithmetic and copies ran while one was open for 12% of the time, Pallas kernels for 13%

profile of v1, /device:TPU:0, one launch (start us, length us, event | category | flops | bytes accessed | tf_op | source)
XLA Modules:
  0.0 157.3 jit_solution(15282143914610390561)
XLA Ops:
  0.7 0.9 fusion.52
  1.5 1.6 %fusion.31 = (f32[]{:T(128)}, bf16[16,4,2,32]{3,2,1,0:T(2,128)(2,1)S(1)}) fusion(f32[1,1,16,4,2,32]{5,4,3,2,1,0:T(2,128)} %param.20, f32[16,4]{1,0:T(8,128)S(1)} %fusion.52, f32[1,1,16,4,2,32]{5,4,3,2,1,0:T(2,128)} %param.19), kind=kLoop, calls=%fused_computation.78 | loop fusion | flops 20479 | bytes 41220 | tf_op jit(solution)/shard_map/reduce_sum | solution.py:521
  3.8 4.1 %collective-permute-start.1 = (bf16[2,64,256]{2,0,1:T(2,128)(2,1)S(1)}, bf16[2,64,256]{2,0,1:T(2,128)(2,1)S(1)}, u32[]{:S(2)}, u32[]{:S(2)}) collective-permute-start(bf16[2,64,256]{2,0,1:T(2,128)(2,1)S(1)} %bitcast.135), channel_id=1, source_target_pairs={{0,8},{1,9},{2,10},{3,11},{4,12},{5,13},{6,14},{7,15},{8,0},{9,1},... | collective-permute-start | bytes 196616 | tf_op jit(solution)/shard_map/ppermute | solution.py:37
  8.0 1.6 %collective-permute-start = (bf16[2,64,256]{2,0,1:T(2,128)(2,1)S(1)}, bf16[2,64,256]{2,0,1:T(2,128)(2,1)S(1)}, u32[]{:S(2)}, u32[]{:S(2)}) collective-permute-start(bf16[2,64,256]{2,0,1:T(2,128)(2,1)S(1)} %bitcast.136), channel_id=1, source_target_pairs={{0,4},{1,5},{2,6},{3,7},{4,0},{5,1},{6,2},{7,3},{8,12},{9,13},{10,... | collective-permute-start | bytes 196616 | tf_op jit(solution)/shard_map/ppermute | solution.py:37
  9.7 0.7 pad_maximum_fusion.8
  11.1 6.1 %all-to-all-start = ((f32[32,1,65]{2,1,0:T(1,128)}), f32[32,1,65]{2,1,0:T(1,128)S(1)}, u32[]{:S(2)}, u32[]{:S(2)}) async-start(f32[32,1,65]{2,1,0:T(1,128)} %broadcast_in_dim.14), calls=%async_computation | async-start | bytes 32768 | tf_op jit(solution)/shard_map/all_to_all | solution.py:486
  17.2 1.0 slice.82
  18.5 1.3 fusion.39
  19.8 1.8 %fusion.43 = (f32[128,256]{1,0:T(8,128)}, f32[128,256]{1,0:T(8,128)}, f32[128,256]{1,0:T(8,128)S(1)}, f32[128,256]{1,0:T(8,128)S(1)}, f32[128,256]{1,0:T(8,128)S(1)}) fusion(s32[256]{0:T(256)S(1)} %fusion.53, s32[128]{0:T(128)S(1)} %iota_add_fusion.1), kind=kLoop, calls=%fused_computation.93 | loop fusion | flops 950272 | bytes 656896 | tf_op jit(solution)/shard_map/sin | solution.py:554
  21.6 0.9 fusion.4
  23.4 1.7 %collective-permute-start.3 = (bf16[4,64,256]{2,1,0:T(8,128)(2,1)S(1)}, bf16[4,64,256]{2,1,0:T(8,128)(2,1)S(1)}, u32[]{:S(2)}, u32[]{:S(2)}) collective-permute-start(bf16[4,64,256]{2,1,0:T(8,128)(2,1)S(1)} %bitcast.144), channel_id=1, source_target_pairs={{0,16},{16,0},{1,17},{17,1},{2,18},{18,2},{3,19},{19,3},{4,20},{20... | collective-permute-start | bytes 393224 | tf_op jit(solution)/shard_map/ppermute | solution.py:37
  25.1 1.5 collective-permute-start.4
  26.6 2.6 %collective-permute-done.3 = bf16[4,64,256]{2,1,0:T(8,128)(2,1)S(1)} collective-permute-done((bf16[4,64,256]{2,1,0:T(8,128)(2,1)S(1)}, bf16[4,64,256]{2,1,0:T(8,128)(2,1)S(1)}, u32[]{:S(2)}, u32[]{:S(2)}) %collective-permute-start.3) | collective-permute-done | bytes 131104 | tf_op jit(solution)/shard_map/ppermute | solution.py:37
  29.4 1.9 %collective-permute-done.4 = bf16[4,64,256]{2,1,0:T(8,128)(2,1)S(1)} collective-permute-done((bf16[4,64,256]{2,1,0:T(8,128)(2,1)S(1)}, bf16[4,64,256]{2,1,0:T(8,128)(2,1)S(1)}, u32[]{:S(2)}, u32[]{:S(2)}) %collective-permute-start.4) | collective-permute-done | bytes 131104 | tf_op jit(solution)/shard_map/ppermute | solution.py:37
  32.6 0.7 copy-done.3
  33.3 5.8 %synthesis.1.smo = f32[128,4096]{1,0:T(8,128)} custom-call(f32[4,8,2048]{2,1,0:T(8,128)} %copy-done.3, f32[4,64,2048]{2,1,0:T(8,128)} %coef_ref.3, bf16[128,144]{1,0:T(8,128)(2,1)} %constant.147.clone.rh, bf16[128,144]{1,0:T(8,128)(2,1)} %constant.148.clone.rl, bf16[512,256]{1,0:T(8,128)(2,1)} %constant.149.clone.ch, bf16[512,256]{1,0:T(8,128)(2,1)} %constant.150.clone.cl), custom_call_target="tpu_custom_call" | custom-call | flops 1073741824 | bytes 4194304 | tf_op jit(solution)/shard_map/synthesis/pallas_call | solution.py:427
  39.1 0.8 collective-permute-start.8
  40.0 1.2 collective-permute-start.6
  41.2 6.2 %collective-permute-done.8 = bf16[2,4,64,256]{3,0,2,1:T(2,128)(2,1)S(1)} collective-permute-done((bf16[2,4,64,256]{3,0,2,1:T(2,128)(2,1)S(1)}, bf16[2,4,64,256]{3,0,2,1:T(2,128)(2,1)S(1)}, u32[]{:S(2)}, u32[]{:S(2)}) %collective-permute-start.8) | collective-permute-done | bytes 262176 | tf_op jit(solution)/shard_map/ppermute | solution.py:37
  47.5 1.6 pad_maximum_fusion.3
  49.0 1.6 pad_maximum_fusion.2
  51.5 0.7 reshape.175.code_ref.where
  52.3 1.1 copy.109
  53.5 1.1 copy.106
  54.6 1.6 %pad_maximum_fusion = (bf16[2,2,2,1,256,256]{5,4,3,2,1,0:T(8,128)(2,1)}, bf16[2,2,2,1,256,256]{5,4,3,2,1,0:T(8,128)(2,1)}) fusion(bf16[1,2,2,1,256,256]{5,4,3,2,1,0:T(8,128)(2,1)S(1)} %bitcast.122, bf16[1,1,2,1,256,256]{5,4,3,2,1,0:T(8,128)(2,1)S(1)} %bitcast.125, bf16[1,1,2,1,256,256]{5,4,3,2,1,0:T(8,128)(2,1)S(1)} %bitcast.123, ...), kind=kLoop, calls=%fused_computation.4 | loop fusion | flops 2097152 | bytes 4194304 | tf_op jit(solution)/shard_map/stack | solution.py:480
  56.2 20.6 %adjoint.1 = (f32[128,4096]{1,0:T(8,128)}, f32[128,4096]{1,0:T(8,128)}, f32[2176,256]{1,0:T(8,128)}) custom-call(bf16[2,2,2,1,256,256]{5,4,3,2,1,0:T(8,128)(2,1)} %get-tuple-element.65.tre, bf16[2,2,2,1,256,256]{5,4,3,2,1,0:T(8,128)(2,1)} %get-tuple-element.66.tim, s32[8,1,256]{2,1,0:T(1,128)} %reshape.175.code_ref.where, ...), custom_call_target="tpu_custom_call" | custom-call | flops 5100273664 | bytes 16777216 | tf_op jit(solution)/shard_map/adjoint/pallas_call | solution.py:261
  76.8 8.9 %parts.3 = f32[2,2,2,1,256,256]{5,4,3,2,1,0:T(8,128)} custom-call(f32[2176,256]{1,0:T(8,128)} %get-tuple-element.31.x_ref, s32[8,1,256]{2,1,0:T(1,128)} %reshape.175.code_ref.where, s32[8,1,256]{2,1,0:T(1,128)} %reshape.175.code_ref.where, bf16[256,256]{1,0:T(8,128)(2,1)} %get-tuple-element.23.wrh, bf16[256,256]{1,0:T(8,128)(2,1)} %get-tuple-element.24.wrl, ...), custom_call_target="tpu_custom_call" | custom-call | flops 805306368 | bytes 8388608 | tf_op jit(solution)/shard_map/parts/pallas_call | solution.py:323
  85.8 8.9 %parts.2 = f32[2,2,2,1,256,256]{5,4,3,2,1,0:T(8,128)} custom-call(f32[2176,256]{1,0:T(8,128)} %get-tuple-element.31.x_ref, s32[8,1,256]{2,1,0:T(1,128)} %reshape.175.code_ref.where, s32[8,1,256]{2,1,0:T(1,128)} %reshape.175.code_ref.where, bf16[256,256]{1,0:T(8,128)(2,1)} %get-tuple-element.23.wrh, bf16[256,256]{1,0:T(8,128)(2,1)} %get-tuple-element.24.wrl, ...), custom_call_target="tpu_custom_call" | custom-call | flops 805306368 | bytes 8388608 | tf_op jit(solution)/shard_map/parts/pallas_call | solution.py:323
  94.7 2.6 %add.191 = f32[2,2,2,1,256,256]{5,4,3,2,1,0:T(8,128)S(1)} add(f32[2,2,2,1,256,256]{5,4,3,2,1,0:T(8,128)} %parts.2, f32[2,2,2,1,256,256]{5,4,3,2,1,0:T(8,128)} %collective-permute-done.10) | non-fusion elementwise | flops 524288 | bytes 6291456 | tf_op jit(solution)/shard_map/add | solution.py:589
  97.3 1.5 collective-permute-start.11
  99.5 12.1 %collective-permute-done.11 = f32[2,1,256,256]{3,2,0,1:T(8,128)S(1)} collective-permute-done((f32[2,1,256,256]{3,2,0,1:T(8,128)S(1)}, f32[2,1,256,256]{3,2,0,1:T(8,128)S(1)}, u32[]{:S(2)}, u32[]{:S(2)}) %collective-permute-start.11) | collective-permute-done | bytes 524320 | tf_op jit(solution)/shard_map/ppermute | solution.py:37
  111.7 0.9 collective-permute-start.12
  113.0 1.0 collective-permute-start.14
  114.0 0.9 slice.100
  114.9 2.9 %collective-permute-start.18 = (f32[8,4096]{1,0:T(8,128)S(1)}, f32[8,4096]{1,0:T(8,128)S(1)}, u32[]{:S(2)}, u32[]{:S(2)}) collective-permute-start(f32[8,4096]{1,0:T(8,128)S(1)} %slice.100), channel_id=1, source_target_pairs={{1,0},{2,1},{3,2},{4,3},{5,4},{6,5},{7,6},{8,7},{9,8},{10,9},{11,1... | collective-permute-start | bytes 393224 | tf_op jit(solution)/shard_map/ppermute | solution.py:33
  117.8 1.8 %collective-permute-done.12 = f32[1,256,256]{2,1,0:T(8,128)S(1)} collective-permute-done((f32[1,256,256]{2,1,0:T(8,128)S(1)}, f32[1,256,256]{2,1,0:T(8,128)S(1)}, u32[]{:S(2)}, u32[]{:S(2)}) %collective-permute-start.12) | collective-permute-done | bytes 262176 | tf_op jit(solution)/shard_map/ppermute | solution.py:37
  121.3 1.6 collective-permute-start.15
  122.8 2.4 %collective-permute-start.17 = (f32[2,64,256]{2,0,1:T(2,128)S(1)}, f32[2,64,256]{2,0,1:T(2,128)S(1)}, u32[]{:S(2)}, u32[]{:S(2)}) collective-permute-start(f32[2,64,256]{2,0,1:T(2,128)S(1)} %get-tuple-element.38), channel_id=1, source_target_pairs={{0,12},{1,13},{2,14},{3,15},{4,8},{5,9},{6,10},{7,11},{8,4},{9,5},... | collective-permute-start | bytes 393224 | tf_op jit(solution)/shard_map/ppermute | solution.py:37
  125.9 6.4 %analysis.1 = (f32[4,64,2048]{2,1,0:T(8,128)}, f32[8,128]{1,0:T(8,128)}) custom-call(f32[128,4096]{1,0:T(8,128)} %get-tuple-element.34.ext_ref, f32[8,4096]{1,0:T(8,128)} %copy-done.4, f32[4,64,2048]{2,1,0:T(8,128)} %coef_ref.3, bf16[128,136]{1,0:T(8,128)(2,1)} %constant.153.clone.rh, bf16[128,136]{1,0:T(8,128)(2,1)} %constant.154.clone.rl, ...), custom_call_target="tpu_custom_call" | custom-call | flops 1073741824 | bytes 4194304 | tf_op jit(solution)/shard_map/analysis/pallas_call | solution.py:468
  132.3 1.3 reduce_sum.47
  133.7 1.8 %collective-permute-done.16 = f32[2,64,256]{2,0,1:T(2,128)S(1)} collective-permute-done((f32[2,64,256]{2,0,1:T(2,128)S(1)}, f32[2,64,256]{2,0,1:T(2,128)S(1)}, u32[]{:S(2)}, u32[]{:S(2)}) %collective-permute-start.16) | collective-permute-done | bytes 131104 | tf_op jit(solution)/shard_map/ppermute | solution.py:37
  136.4 0.7 fusion.45
  137.1 1.4 pad_maximum_fusion.9
  139.1 5.1 %all-to-all-start.1 = ((f32[32,1,2]{2,1,0:T(1,128)}), f32[32,1,2]{2,1,0:T(1,128)S(1)}, u32[]{:S(2)}, u32[]{:S(2)}) async-start(f32[32,1,2]{2,1,0:T(1,128)} %broadcast_in_dim.15), calls=%async_computation.1 | async-start | bytes 32768 | tf_op jit(solution)/shard_map/all_to_all | solution.py:486
  144.2 0.7 slice_reduce_fusion
  145.6 5.7 %all-to-all-done.1 = f32[32,1,2]{2,1,0:T(1,128)S(1)} async-done(((f32[32,1,2]{2,1,0:T(1,128)}), f32[32,1,2]{2,1,0:T(1,128)S(1)}, u32[]{:S(2)}, u32[]{:S(2)}) %all-to-all-start.1) | async-done | bytes 288 | tf_op jit(solution)/shard_map/all_to_all | solution.py:486
  153.3 3.2 %maximum_minimum_fusion = f32[4,64,2048]{2,1,0:T(8,128)} fusion(f32[4,64,2048]{2,1,0:T(8,128)} %get-tuple-element.36, f32[]{:T(128)S(6)} %neg.11, f32[]{:T(128)} %bitcast.48), kind=kLoop, calls=%fused_computation | loop fusion | flops 1048576 | bytes 4194312 | tf_op jit(solution)/shard_map/jit(clip)/min | solution.py:620
  156.5 0.8 fusion.37
  (87 shorter events, 10.9 us)
Async XLA Ops:
  0.6 2.8 %copy-start = (bf16[1,1,16,4,2,32,256]{6,5,4,3,2,1,0:T(8,128)(2,1)S(1)}, bf16[1,1,16,4,2,32,256]{6,5,4,3,2,1,0:T(8,128)(2,1)}, u32[]{:S(2)}) copy-start(bf16[1,1,16,4,2,32,256]{6,5,4,3,2,1,0:T(8,128)(2,1)} %param.21) | copy-start | bytes 6291460
  0.6 8.9 %copy-start.7 = (s32[1,1,16,4]{2,3,1,0:T(4,128)S(1)}, s32[1,1,16,4]{2,3,1,0:T(4,128)}, u32[]{:S(2)}) copy-start(s32[1,1,16,4]{2,3,1,0:T(4,128)} %param.22) | copy-start | bytes 772
  3.8 18.7 %collective-permute-start.1 = (bf16[2,64,256]{2,0,1:T(2,128)(2,1)S(1)}, bf16[2,64,256]{2,0,1:T(2,128)(2,1)S(1)}, u32[]{:S(2)}, u32[]{:S(2)}) collective-permute-start(bf16[2,64,256]{2,0,1:T(2,128)(2,1)S(1)} %bitcast.135), channel_id=1, source_target_pairs={{0,8},{1,9},{2,10},{3,11},{4,12},{5,13},{6,14},{7,15},{8,0},{9,1},... | collective-permute-start | bytes 196616 | tf_op jit(solution)/shard_map/ppermute | solution.py:37
  8.0 14.5 %collective-permute-start = (bf16[2,64,256]{2,0,1:T(2,128)(2,1)S(1)}, bf16[2,64,256]{2,0,1:T(2,128)(2,1)S(1)}, u32[]{:S(2)}, u32[]{:S(2)}) collective-permute-start(bf16[2,64,256]{2,0,1:T(2,128)(2,1)S(1)} %bitcast.136), channel_id=1, source_target_pairs={{0,4},{1,5},{2,6},{3,7},{4,0},{5,1},{6,2},{7,3},{8,12},{9,13},{10,... | collective-permute-start | bytes 196616 | tf_op jit(solution)/shard_map/ppermute | solution.py:37
  9.5 13.0 %collective-permute-start.2 = (bf16[2,64,256]{2,0,1:T(2,128)(2,1)S(1)}, bf16[2,64,256]{2,0,1:T(2,128)(2,1)S(1)}, u32[]{:S(2)}, u32[]{:S(2)}) collective-permute-start(bf16[2,64,256]{2,0,1:T(2,128)(2,1)S(1)} %bitcast.137), channel_id=1, source_target_pairs={{0,12},{1,13},{2,14},{3,15},{4,8},{5,9},{6,10},{7,11},{8,4},{9,5},... | collective-permute-start | bytes 196616 | tf_op jit(solution)/shard_map/ppermute | solution.py:37
  11.1 40.2 %all-to-all-start = ((f32[32,1,65]{2,1,0:T(1,128)}), f32[32,1,65]{2,1,0:T(1,128)S(1)}, u32[]{:S(2)}, u32[]{:S(2)}) async-start(f32[32,1,65]{2,1,0:T(1,128)} %broadcast_in_dim.14), calls=%async_computation | async-start | bytes 32768 | tf_op jit(solution)/shard_map/all_to_all | solution.py:486
  18.1 14.4 %collective-permute-start.5 = (f32[4,8,2048]{2,1,0:T(8,128)S(1)}, f32[4,8,2048]{2,1,0:T(8,128)S(1)}, u32[]{:S(2)}, u32[]{:S(2)}) collective-permute-start(f32[4,8,2048]{2,1,0:T(8,128)S(1)} %slice.82), channel_id=1, source_target_pairs={{31,0},{0,1},{1,2},{2,3},{3,4},{4,5},{5,6},{6,7},{7,8},{8,9},{9,10... | collective-permute-start | bytes 786440 | tf_op jit(solution)/shard_map/ppermute | solution.py:33
  23.4 5.8 %collective-permute-start.3 = (bf16[4,64,256]{2,1,0:T(8,128)(2,1)S(1)}, bf16[4,64,256]{2,1,0:T(8,128)(2,1)S(1)}, u32[]{:S(2)}, u32[]{:S(2)}) collective-permute-start(bf16[4,64,256]{2,1,0:T(8,128)(2,1)S(1)} %bitcast.144), channel_id=1, source_target_pairs={{0,16},{16,0},{1,17},{17,1},{2,18},{18,2},{3,19},{19,3},{4,20},{20... | collective-permute-start | bytes 393224 | tf_op jit(solution)/shard_map/ppermute | solution.py:37
  25.1 6.2 %collective-permute-start.4 = (bf16[4,64,256]{2,1,0:T(8,128)(2,1)S(1)}, bf16[4,64,256]{2,1,0:T(8,128)(2,1)S(1)}, u32[]{:S(2)}, u32[]{:S(2)}) collective-permute-start(bf16[4,64,256]{2,1,0:T(8,128)(2,1)S(1)} %bitcast.141), channel_id=1, source_target_pairs={{0,2},{1,3},{2,0},{3,1},{4,6},{5,7},{6,4},{7,5},{8,10},{9,11},{10,... | collective-permute-start | bytes 393224 | tf_op jit(solution)/shard_map/ppermute | solution.py:37
  32.6 0.7 copy-start.3
  39.1 8.3 %collective-permute-start.8 = (bf16[2,4,64,256]{3,0,2,1:T(2,128)(2,1)S(1)}, bf16[2,4,64,256]{3,0,2,1:T(2,128)(2,1)S(1)}, u32[]{:S(2)}, u32[]{:S(2)}) collective-permute-start(bf16[2,4,64,256]{3,0,2,1:T(2,128)(2,1)S(1)} %pad_maximum_fusion.6), channel_id=1, source_target_pairs={{0,16},{16,0},{1,17},{17,1},{2,18},{18,2},{3,19},{19,3},{4,20},{20... | collective-permute-start | bytes 786440 | tf_op jit(solution)/shard_map/ppermute | solution.py:37
  40.0 9.1 %collective-permute-start.6 = (bf16[2,4,64,256]{3,0,2,1:T(2,128)(2,1)S(1)}, bf16[2,4,64,256]{3,0,2,1:T(2,128)(2,1)S(1)}, u32[]{:S(2)}, u32[]{:S(2)}) collective-permute-start(bf16[2,4,64,256]{3,0,2,1:T(2,128)(2,1)S(1)} %pad_maximum_fusion.5), channel_id=1, source_target_pairs={{0,2},{1,3},{2,0},{3,1},{4,6},{5,7},{6,4},{7,5},{8,10},{9,11},{10,... | collective-permute-start | bytes 786440 | tf_op jit(solution)/shard_map/ppermute | solution.py:37
  49.0 3.3 %collective-permute-start.9 = (bf16[2,2,4,64,256]{4,1,3,2,0:T(2,128)(2,1)}, bf16[2,2,4,64,256]{4,1,3,2,0:T(2,128)(2,1)}, u32[]{:S(2)}, u32[]{:S(2)}) collective-permute-start(bf16[2,2,4,64,256]{4,1,3,2,0:T(2,128)(2,1)} %pad_maximum_fusion.3), channel_id=1, source_target_pairs={{0,1},{1,0},{2,3},{3,2},{4,5},{5,4},{6,7},{7,6},{8,9},{9,8},{10,11... | collective-permute-start | bytes 1572872 | tf_op jit(solution)/shard_map/ppermute | solution.py:37
  50.6 2.9 %collective-permute-start.7 = (bf16[2,2,4,64,256]{4,1,3,2,0:T(2,128)(2,1)}, bf16[2,2,4,64,256]{4,1,3,2,0:T(2,128)(2,1)}, u32[]{:S(2)}, u32[]{:S(2)}) collective-permute-start(bf16[2,2,4,64,256]{4,1,3,2,0:T(2,128)(2,1)} %pad_maximum_fusion.2), channel_id=1, source_target_pairs={{0,1},{1,0},{2,3},{3,2},{4,5},{5,4},{6,7},{7,6},{8,9},{9,8},{10,11... | collective-permute-start | bytes 1572872 | tf_op jit(solution)/shard_map/ppermute | solution.py:37
  51.3 3.3 %copy-start.5 = (f32[32,1,65]{2,1,0:T(1,128)}, f32[32,1,65]{2,1,0:T(1,128)S(1)}, u32[]{:S(2)}) copy-start(f32[32,1,65]{2,1,0:T(1,128)S(1)} %all-to-all-done) | copy-start | bytes 24964
  85.8 8.9 %collective-permute-start.10 = (f32[2,2,2,1,256,256]{5,4,3,2,1,0:T(8,128)}, f32[2,2,2,1,256,256]{5,4,3,2,1,0:T(8,128)}, u32[]{:S(2)}, u32[]{:S(2)}) collective-permute-start(f32[2,2,2,1,256,256]{5,4,3,2,1,0:T(8,128)} %parts.3), channel_id=1, source_target_pairs={{0,1},{1,0},{2,3},{3,2},{4,5},{5,4},{6,7},{7,6},{8,9},{9,8},{10,11... | collective-permute-start | bytes 6291464 | tf_op jit(solution)/shard_map/ppermute | solution.py:37
  97.3 14.3 %collective-permute-start.11 = (f32[2,1,256,256]{3,2,0,1:T(8,128)S(1)}, f32[2,1,256,256]{3,2,0,1:T(8,128)S(1)}, u32[]{:S(2)}, u32[]{:S(2)}) collective-permute-start(f32[2,1,256,256]{3,2,0,1:T(8,128)S(1)} %slice_bitcast_fusion.2), channel_id=1, source_target_pairs={{0,2},{1,3},{2,0},{3,1},{4,6},{5,7},{6,4},{7,5},{8,10},{9,11},{10,... | collective-permute-start | bytes 1572872 | tf_op jit(solution)/shard_map/ppermute | solution.py:37
  98.9 14.1 %collective-permute-start.13 = (f32[2,1,256,256]{3,2,0,1:T(8,128)S(1)}, f32[2,1,256,256]{3,2,0,1:T(8,128)S(1)}, u32[]{:S(2)}, u32[]{:S(2)}) collective-permute-start(f32[2,1,256,256]{3,2,0,1:T(8,128)S(1)} %slice_bitcast_fusion), channel_id=1, source_target_pairs={{0,16},{16,0},{1,17},{17,1},{2,18},{18,2},{3,19},{19,3},{4,20},{20... | collective-permute-start | bytes 1572872 | tf_op jit(solution)/shard_map/ppermute | solution.py:37
  111.7 7.9 %collective-permute-start.12 = (f32[1,256,256]{2,1,0:T(8,128)S(1)}, f32[1,256,256]{2,1,0:T(8,128)S(1)}, u32[]{:S(2)}, u32[]{:S(2)}) collective-permute-start(f32[1,256,256]{2,1,0:T(8,128)S(1)} %slice_bitcast_fusion.6), channel_id=1, source_target_pairs={{0,16},{16,0},{1,17},{17,1},{2,18},{18,2},{3,19},{19,3},{4,20},{20... | collective-permute-start | bytes 786440 | tf_op jit(solution)/shard_map/ppermute | solution.py:37
  113.0 7.6 %collective-permute-start.14 = (f32[1,256,256]{2,1,0:T(8,128)S(1)}, f32[1,256,256]{2,1,0:T(8,128)S(1)}, u32[]{:S(2)}, u32[]{:S(2)}) collective-permute-start(f32[1,256,256]{2,1,0:T(8,128)S(1)} %slice_bitcast_fusion.4), channel_id=1, source_target_pairs={{0,2},{1,3},{2,0},{3,1},{4,6},{5,7},{6,4},{7,5},{8,10},{9,11},{10,... | collective-permute-start | bytes 786440 | tf_op jit(solution)/shard_map/ppermute | solution.py:37
  114.9 10.3 %collective-permute-start.18 = (f32[8,4096]{1,0:T(8,128)S(1)}, f32[8,4096]{1,0:T(8,128)S(1)}, u32[]{:S(2)}, u32[]{:S(2)}) collective-permute-start(f32[8,4096]{1,0:T(8,128)S(1)} %slice.100), channel_id=1, source_target_pairs={{1,0},{2,1},{3,2},{4,3},{5,4},{6,5},{7,6},{8,7},{9,8},{10,9},{11,1... | collective-permute-start | bytes 393224 | tf_op jit(solution)/shard_map/ppermute | solution.py:33
  121.3 12.4 %collective-permute-start.15 = (f32[2,64,256]{2,0,1:T(2,128)S(1)}, f32[2,64,256]{2,0,1:T(2,128)S(1)}, u32[]{:S(2)}, u32[]{:S(2)}) collective-permute-start(f32[2,64,256]{2,0,1:T(2,128)S(1)} %get-tuple-element.37), channel_id=1, source_target_pairs={{0,4},{1,5},{2,6},{3,7},{4,0},{5,1},{6,2},{7,3},{8,12},{9,13},{10,... | collective-permute-start | bytes 393224 | tf_op jit(solution)/shard_map/ppermute | solution.py:37
  122.8 10.8 %collective-permute-start.17 = (f32[2,64,256]{2,0,1:T(2,128)S(1)}, f32[2,64,256]{2,0,1:T(2,128)S(1)}, u32[]{:S(2)}, u32[]{:S(2)}) collective-permute-start(f32[2,64,256]{2,0,1:T(2,128)S(1)} %get-tuple-element.38), channel_id=1, source_target_pairs={{0,12},{1,13},{2,14},{3,15},{4,8},{5,9},{6,10},{7,11},{8,4},{9,5},... | collective-permute-start | bytes 393224 | tf_op jit(solution)/shard_map/ppermute | solution.py:37
  125.2 10.3 %collective-permute-start.16 = (f32[2,64,256]{2,0,1:T(2,128)S(1)}, f32[2,64,256]{2,0,1:T(2,128)S(1)}, u32[]{:S(2)}, u32[]{:S(2)}) collective-permute-start(f32[2,64,256]{2,0,1:T(2,128)S(1)} %get-tuple-element.39), channel_id=1, source_target_pairs={{0,8},{1,9},{2,10},{3,11},{4,12},{5,13},{6,14},{7,15},{8,0},{9,1},... | collective-permute-start | bytes 393224 | tf_op jit(solution)/shard_map/ppermute | solution.py:37
  125.2 0.7 copy-start.4
  132.3 4.1 %copy-start.1 = (f32[1,1,16,4,2,32]{5,4,3,2,1,0:T(2,128)S(1)}, f32[1,1,16,4,2,32]{5,4,3,2,1,0:T(2,128)}, u32[]{:S(2)}) copy-start(f32[1,1,16,4,2,32]{5,4,3,2,1,0:T(2,128)} %param.20) | copy-start | bytes 49156
  132.3 4.1 %copy-start.2 = (f32[1,1,16,4,2,32]{5,4,3,2,1,0:T(2,128)S(1)}, f32[1,1,16,4,2,32]{5,4,3,2,1,0:T(2,128)}, u32[]{:S(2)}) copy-start(f32[1,1,16,4,2,32]{5,4,3,2,1,0:T(2,128)} %param.19) | copy-start | bytes 49156
  133.6 10.6 %copy-start.6 = (f32[32,1,65]{2,1,0:T(1,128)S(1)}, f32[32,1,65]{2,1,0:T(1,128)}, u32[]{:S(2)}) copy-start(f32[32,1,65]{2,1,0:T(1,128)} %copy-done.5) | copy-start | bytes 24964
  139.1 12.2 %all-to-all-start.1 = ((f32[32,1,2]{2,1,0:T(1,128)}), f32[32,1,2]{2,1,0:T(1,128)S(1)}, u32[]{:S(2)}, u32[]{:S(2)}) async-start(f32[32,1,2]{2,1,0:T(1,128)} %broadcast_in_dim.15), calls=%async_computation.1 | async-start | bytes 32768 | tf_op jit(solution)/shard_map/all_to_all | solution.py:486

commit v2 on v1

v2 whole, which is shorter than its diff:
```python
import math

import jax
import jax.numpy as jnp
import numpy as np
from jax import lax
from jax.experimental import pallas as pl
from jax.experimental.pallas import tpu as pltpu
from jax.sharding import PartitionSpec as P


LANES = 128
FLAG = 1 << 20

low_taps = (
    -0.010597401784997278,
    0.032883011666982945,
    0.030841381835986965,
    -0.18703481171888114,
    -0.02798376941698385,
    0.6308807679295904,
    0.7148465705525415,
    0.23037781330885523,
)
high_taps = tuple(((-1.0) ** offset * low_taps[7 - offset] for offset in range(8)))
AXES = ("band", "vis")
bf16 = jnp.bfloat16
f32 = jnp.float32


def shifted(block, axis, distance):
    devices = range(lax.axis_size(axis))
    route = [((i - distance) % len(devices), i) for i in devices]
    return lax.ppermute(block, axis, route)


def flipped(block, axis, mask):
    return lax.ppermute(block, axis, [(i, i ^ mask) for i in range(lax.axis_size(axis))])


def split_two(values):
    high = lax.reduce_precision(values, 8, 7)
    return high.astype(bf16), (values - high).astype(bf16)


def split_here(values):
    high = values.astype(bf16)
    return high, (values - high.astype(f32)).astype(bf16)


def dot_nn(left, right):
    return lax.dot_general(left, right, (((1,), (0,)), ((), ())), preferred_element_type=f32)


def dot_nt(left, right):
    return lax.dot_general(left, right, (((1,), (1,)), ((), ())), preferred_element_type=f32)


def dot_three(dot, left, right):
    return dot(left[0], right[0]) + dot(left[0], right[1]) + dot(left[1], right[0])


def scaled_sum(terms):
    total = None
    for weight, value in terms:
        if abs(weight) < 1e-12:
            continue
        part = value if weight == 1.0 else weight * value
        total = part if total is None else total + part
    return total


def cosine_sums(values, size):
    if size == 1:
        return [values[0] + values[1], values[0] - values[1]]
    half = size // 2
    even = cosine_sums(values[0::2], half)
    out = [None] * (size + 1)
    for a in range(half):
        odd = scaled_sum(
            [(math.cos(math.pi * k * a / size) if a else 1.0, values[k]) for k in range(1, size, 2)]
        )
        out[a] = even[a] + odd
        out[size - a] = even[a] - odd
    out[half] = even[half]
    return out


def sine_sums(values, size):
    half = size // 2
    out = [None] * (size + 1)
    if size == 2:
        out[1] = values[1]
        return out
    even = sine_sums(values[0::2], half)
    for a in range(1, half):
        odd = scaled_sum([(math.sin(math.pi * k * a / size), values[k]) for k in range(1, size, 2)])
        out[a] = odd + even[a]
        out[size - a] = odd - even[a]
    out[half] = scaled_sum([(math.sin(math.pi * k / 2), values[k]) for k in range(1, size, 2)])
    return out


def twiddle_seeds(image_width):
    outer = image_width // LANES
    kept = outer // 2 + 1
    inner = image_width // outer
    c = np.arange(LANES)
    one = 2.0 * np.pi * (np.arange(kept)[:, None] * c[None, :] % image_width) / image_width
    two = 2.0 * np.pi * (np.arange(inner)[:, None] * c[None, :] % inner) / inner
    one = np.stack([np.cos(one), np.sin(one)], axis=1).astype(np.float32)
    two = np.stack([np.cos(two), np.sin(two)]).astype(np.float32)
    return jnp.asarray(one), jnp.asarray(two)


def upright(row):
    return jnp.broadcast_to(row, (8, row.shape[1])).T[:, 0:1]


def sign_of(code):
    return jnp.where(code >= FLAG, -1.0, 1.0).astype(f32)


def vmem():
    return pl.BlockSpec(memory_space=pltpu.VMEM)


def emit_part(xr, xi, where, code_ref, tables, turned, real_out, imag_out, pr_ref, pi_ref):
    tiles = pr_ref.shape[0]
    together = 16
    wrh, wrl, wih, wil = tables
    pc, ps = turned

    def body(chunk, inside):
        begin = chunk * together
        spots = [where[0, begin + u] for u in range(together)]
        found = [(xr[pl.ds(at, 1), :], xi[pl.ds(at, 1), :]) for at in spots]
        for u in range(together):
            pr_ref[pl.ds(begin + u, 1), :] = found[u][0]
            pi_ref[pl.ds(begin + u, 1), :] = found[u][1]
        return inside

    lax.fori_loop(0, tiles // together, body, 0)
    sign = upright(sign_of(code_ref[...]))
    real = pr_ref[...]
    imag = pi_ref[...] * sign
    turned_re = pc[...] * real + ps[...] * imag
    turned_im = pc[...] * imag - ps[...] * real
    both = split_here(jnp.concatenate([turned_re, turned_im], axis=1))
    real_out[...] = dot_three(dot_nn, both, (wrh[...], wrl[...])).astype(real_out.dtype)
    imag_out[...] = dot_three(dot_nn, both, (wih[...], wil[...])).astype(imag_out.dtype)


def swapped(block, blocks_a, blocks_b, blocks_f):
    f, j = block % blocks_f, block // blocks_f
    return (j % blocks_b * blocks_a + j // blocks_b) * blocks_f + f


def image_step(
    tile_arrays, codes, columns, weight_tables, phases_turned, sky_image, smooth, held_as
):
    blocks_a, blocks_b, blocks_f, tiles, length = tile_arrays[0].shape
    part = blocks_a * blocks_b * blocks_f
    rows, image_width = sky_image.shape
    outer = image_width // LANES
    kept = outer // 2 + 1
    inner = image_width // outer
    width = kept * inner
    near = min(8, rows)
    seeds = twiddle_seeds(image_width)
    each = -(-kept // (2 * part))
    counts = (blocks_a, blocks_b, blocks_f)

    def kernel(
        tre, tim, tre_far, tim_far, where, code_ref, wrh, wrl, wih, wil, qc, qs,
        one, two, sky_any, smo_any,
        new_any, near_ref, xr_ref, xi_ref, real_out, imag_out,
        grid_ref, mid_ref, y_ref, mh, ml, sky, smo, new_ref, pr_ref, pi_ref, tre_in, tim_in, pc, ps, sems,
    ):
        sky_copy = pltpu.make_async_copy(sky_any, sky, sems.at[0])
        smo_copy = pltpu.make_async_copy(smo_any, smo, sems.at[1])
        tre_copy = pltpu.make_async_copy(tre_far, tre_in, sems.at[3])
        tim_copy = pltpu.make_async_copy(tim_far, tim_in, sems.at[4])
        tre_copy.start()
        tim_copy.start()
        sky_copy.start()
        smo_copy.start()
        pc[...] = qc[...].T
        ps[...] = qs[...].T
        grid_ref[...] = jnp.zeros_like(grid_ref)

        def scatter(i, carry, re_ref, im_ref, begin):
            f, j = i % blocks_f, i // blocks_f
            y, x = j // blocks_b, j % blocks_b
            re = re_ref[y, x, f]
            im = im_ref[x, y, f]
            half = (
                dot_nt(wrh[...], re) + dot_nt(wrl[...], re)
                + dot_nt(wih[...], im) + dot_nt(wil[...], im)
            )
            half_re = half[:rows]
            half_im = half[rows:]
            code = code_ref[begin + i]
            turned_re = pc[...] * half_re - ps[...] * half_im
            turned_im = (pc[...] * half_im + ps[...] * half_re) * sign_of(code)
            turned = jnp.concatenate([turned_re, turned_im], axis=0).astype(bf16)
            column = upright(code & (FLAG - 1))
            lanes = lax.broadcasted_iota(jnp.int32, (tiles, inner), 1)
            within = (lanes == column % inner).astype(f32).astype(bf16)
            major = jnp.broadcast_to((column // inner).astype(f32), (tiles, inner)).astype(bf16)
            zero = jnp.zeros_like(within)
            for first in range(0, kept, 2):
                hots = [
                    jnp.where(major == jnp.asarray(k, bf16), within, zero)
                    for k in range(first, min(first + 2, kept))
                ]
                span = slice(first * inner, (first + len(hots)) * inner)
                grid_ref[:, span] += dot_nn(turned, jnp.concatenate(hots, axis=1))
            for u in range(each):
                k = jnp.minimum((begin + i) * each + u, kept - 1)
                c1 = one[k, 0:1, :]
                s1 = one[k, 1:2, :]
                c2 = two[0]
                s2 = two[1]
                real = split_here(c1 * c2 - s1 * s2)
                imag = split_here(c1 * s2 + s1 * c2)
                for out, re, im in ((mh, real[0], imag[0]), (ml, real[1], imag[1])):
                    out[k, 0:inner, 0:LANES] = re
                    out[k, 0:inner, LANES : 2 * LANES] = im
                    out[k, inner : 2 * inner, 0:LANES] = -im
                    out[k, inner : 2 * inner, LANES : 2 * LANES] = re
            return carry

        lax.fori_loop(0, part, lambda i, c: scatter(i, c, tre, tim, 0), 0)
        tre_copy.wait()
        tim_copy.wait()
        lax.fori_loop(0, part, lambda i, c: scatter(i, c, tre_in, tim_in, part), 0)

        for k in range(kept):
            cell = jnp.concatenate(
                [
                    grid_ref[:rows, k * inner : (k + 1) * inner],
                    grid_ref[rows:, k * inner : (k + 1) * inner],
                ],
                axis=1,
            )
            mid_ref[k] = dot_three(dot_nn, split_here(cell), (mh[k], ml[k]))

        def body(chunk, carry):
            at = pl.ds(pl.multiple_of(chunk * 8, 8), 8)
            real = [mid_ref[k, at, 0:LANES] for k in range(kept)]
            imag = [mid_ref[k, at, LANES : 2 * LANES] for k in range(kept)]
            even = cosine_sums(real, outer // 2)
            odd = sine_sums(imag, outer // 2)
            values = []
            for a in range(outer):
                if a == 0 or a == outer // 2:
                    back = even[a]
                elif a < outer // 2:
                    back = even[a] - odd[a]
                else:
                    back = even[outer - a] + odd[outer - a]
                span = slice(a * LANES, (a + 1) * LANES)
                old = sky[at, span]
                new = jnp.maximum(old - smo[at, span] - back, 0.0)
                new_ref[at, span] = new
                values.append(2.0 * new - old)
            mirrored = outer // 2
            even = [values[0]]
            odd = [None]
            for a in range(1, mirrored):
                even.append(values[a] + values[outer - a])
                odd.append(values[a] - values[outer - a])
            even.append(values[mirrored])
            odd.append(None)
            real = cosine_sums(even, mirrored)
            imag = sine_sums(odd, mirrored)
            for k in range(kept):
                y_ref[k, at, 0:LANES] = real[k]
                y_ref[k, at, LANES : 2 * LANES] = (
                    jnp.zeros_like(real[k]) if imag[k] is None else -imag[k]
                )
            return carry

        sky_copy.wait()
        smo_copy.wait()
        lax.fori_loop(0, rows // 8, body, 0)
        near_ref[...] = 2.0 * new_ref[:near, :] - sky[:near, :]
        written = pltpu.make_async_copy(new_ref, new_any, sems.at[2])
        written.start()
        for k in range(kept):
            high, low = split_here(y_ref[k])
            if rows % LANES == 0:
                both = dot_nt(mh[k], jnp.concatenate([high, low], axis=0))
                both = both[:, :rows] + both[:, rows:] + dot_nt(ml[k], high)
            else:
                both = dot_three(dot_nt, (mh[k], ml[k]), (high, low))
            xr_ref[k * inner : (k + 1) * inner, :] = both[:inner]
            xi_ref[k * inner : (k + 1) * inner, :] = both[inner:]

        def emit(i, carry):
            emit_part(
                xr_ref, xi_ref, where.at[part + i], code_ref.at[part + i], (wrh, wrl, wih, wil), (qc, qs),
                real_out.at[i], imag_out.at[swapped(i, *counts)], pr_ref, pi_ref,
            )
            return carry

        lax.fori_loop(0, part, emit, 0)
        written.wait()

    any_space = pl.BlockSpec(memory_space=pl.ANY)
    return pl.pallas_call(
        kernel,
        in_specs=[
            *[vmem()] * 2,
            any_space,
            any_space,
            pl.BlockSpec(memory_space=pltpu.SMEM),
            *[vmem()] * (1 + 4 + 2 + 2),
            any_space,
            any_space,
        ],
        out_specs=[any_space] + [vmem()] * 5,
        out_shape=[
            jax.ShapeDtypeStruct((rows, image_width), f32),
            jax.ShapeDtypeStruct((near, image_width), f32),
            jax.ShapeDtypeStruct((width, rows), f32),
            jax.ShapeDtypeStruct((width, rows), f32),
            jax.ShapeDtypeStruct((part, tiles, length), held_as),
            jax.ShapeDtypeStruct((part, tiles, length), held_as),
        ],
        scratch_shapes=[
            pltpu.VMEM((2 * rows, width), f32),
            pltpu.VMEM((kept, rows, 2 * LANES), f32),
            pltpu.VMEM((kept, rows, 2 * LANES), f32),
            pltpu.VMEM((kept, 2 * inner, 2 * LANES), bf16),
            pltpu.VMEM((kept, 2 * inner, 2 * LANES), bf16),
            pltpu.VMEM((rows, image_width), f32),
            pltpu.VMEM((rows, image_width), f32),
            pltpu.VMEM((rows, image_width), f32),
            pltpu.VMEM((tiles, rows), f32),
            pltpu.VMEM((tiles, rows), f32),
            pltpu.VMEM(tile_arrays[2].shape, bf16),
            pltpu.VMEM(tile_arrays[3].shape, bf16),
            pltpu.VMEM((rows, tiles), f32),
            pltpu.VMEM((rows, tiles), f32),
            pltpu.SemaphoreType.DMA((5,)),
        ],
        cost_estimate=pl.CostEstimate(
            flops=16 * part * rows * tiles * (width + length), bytes_accessed=1 << 24, transcendentals=0
        ),
        name="image_step",
    )(
        *tile_arrays, columns, codes, *weight_tables, *phases_turned, *seeds,
        sky_image, smooth,
    )


def forward_parts(spectra, codes, columns, weight_tables, phases_turned, counts):
    tiles = codes.shape[2]
    part = math.prod(counts)
    rows = spectra[0].shape[1]
    length = weight_tables[0].shape[1]

    def kernel(
        xr, xi, where, code_ref, wrh, wrl, wih, wil, qc, qs, real_out, imag_out, pr_ref, pi_ref
    ):
        emit_part(
            xr, xi, where.at[0], code_ref.at[0], (wrh, wrl, wih, wil), (qc, qs),
            real_out.at[0], imag_out.at[0], pr_ref, pi_ref,
        )

    def whole(array):
        return pl.BlockSpec(array.shape, lambda i: (0,) * array.ndim)

    shape = jax.ShapeDtypeStruct((part, tiles, length), f32)
    return pl.pallas_call(
        kernel,
        grid=(part,),
        in_specs=[
            *[whole(x) for x in spectra],
            pl.BlockSpec((1, 1, tiles), lambda i: (i, 0, 0), memory_space=pltpu.SMEM),
            pl.BlockSpec((1, 1, tiles), lambda i: (i, 0, 0)),
            *[whole(x) for x in (*weight_tables, *phases_turned)],
        ],
        out_specs=[
            pl.BlockSpec((1, tiles, length), lambda i: (i, 0, 0)),
            pl.BlockSpec((1, tiles, length), lambda i: (swapped(i, *counts), 0, 0)),
        ],
        out_shape=[shape, shape],
        scratch_shapes=[pltpu.VMEM((tiles, rows), f32)] * 2,
        cost_estimate=pl.CostEstimate(
            flops=24 * part * rows * tiles * length, bytes_accessed=1 << 23, transcendentals=0
        ),
        name="parts",
    )(*spectra, columns, codes, *weight_tables, *phases_turned)


def row_matrix_up(half_rows, lead):
    ext = half_rows + lead
    matrix = np.zeros((2 * half_rows, 2 * ext), np.float64)
    for n in range(2 * half_rows):
        for k in range(-3, half_rows):
            tap = n - 2 * k
            if 0 <= tap < 8:
                matrix[n, lead + k] = low_taps[tap]
                matrix[n, ext + lead + k] = high_taps[tap]
    return matrix


def row_matrix_down(rows, tail):
    matrix = np.zeros((rows, rows + tail), np.float64)
    for k in range(rows // 2):
        for j in range(8):
            matrix[k, 2 * k + j] = low_taps[j]
            matrix[rows // 2 + k, 2 * k + j] = high_taps[j]
    return matrix


def col_matrix_up():
    matrix = np.zeros((4, LANES, 2 * LANES), np.float64)
    for n in range(2 * LANES):
        for k in range(-LANES, LANES):
            tap = n - 2 * k
            if 0 <= tap < 8:
                where = (0, k + LANES) if k < 0 else (1, k)
                matrix[where[0], where[1], n] = low_taps[tap]
                matrix[2 + where[0], where[1], n] = high_taps[tap]
    return matrix.reshape(4 * LANES, 2 * LANES)


def col_matrix_down():
    matrix = np.zeros((3 * LANES, 2 * LANES), np.float64)
    for k in range(LANES):
        for j in range(8):
            matrix[2 * k + j, k] = low_taps[j]
            matrix[2 * k + j, LANES + k] = high_taps[j]
    return matrix


def split_constant(matrix):
    value = np.asarray(matrix, np.float32)
    high = value.astype(bf16)
    low = (value - high.astype(np.float32)).astype(bf16)
    return jnp.asarray(high), jnp.asarray(low)


def synthesis(halo, coef_dual):
    _, half_rows, half_width = coef_dual.shape
    rows = 2 * half_rows
    lead = halo.shape[1]
    row_tables = split_constant(row_matrix_up(half_rows, lead))
    col_tables = split_constant(col_matrix_up())

    def kernel(halo_ref, coef_ref, rh, rl, ch, cl, out_ref):
        sides = []
        for first, second in ((0, 2), (1, 3)):
            ext = jnp.concatenate(
                [halo_ref[first], coef_ref[first], halo_ref[second], coef_ref[second]], axis=0
            )
            sides.append(dot_three(dot_nn, (rh[...], rl[...]), split_here(ext)))
        low = split_here(sides[0])
        high = split_here(sides[1])
        count = half_width // LANES
        for j in range(count):
            here = slice(j * LANES, (j + 1) * LANES)
            past = (j - 1) % count
            before = slice(past * LANES, (past + 1) * LANES)
            operands = tuple(
                jnp.concatenate(
                    [low[p][:, before], low[p][:, here], high[p][:, before], high[p][:, here]],
                    axis=1,
                )
                for p in range(2)
            )
            out_ref[:, 2 * j * LANES : 2 * (j + 1) * LANES] = dot_three(
                dot_nn, operands, (ch[...], cl[...])
            )

    return pl.pallas_call(
        kernel,
        out_shape=jax.ShapeDtypeStruct((rows, 2 * half_width), f32),
        cost_estimate=pl.CostEstimate(flops=1 << 30, bytes_accessed=1 << 22, transcendentals=0),
        name="synthesis",
    )(halo, coef_dual, *row_tables, *col_tables)


def analysis(new_image, sky_image, halo, coef_dual):
    rows, image_width = new_image.shape
    half_rows = rows // 2
    half_width = image_width // 2
    row_tables = split_constant(row_matrix_down(rows, halo.shape[0]))
    col_tables = split_constant(col_matrix_down())

    def kernel(new_ref, sky_ref, halo_ref, coef_ref, rh, rl, ch, cl, out_ref, sum_ref):
        extrap = 2.0 * new_ref[...] - sky_ref[...]
        ext = jnp.concatenate([extrap, halo_ref[...]], axis=0)
        sides = split_here(dot_three(dot_nn, (rh[...], rl[...]), split_here(ext)))
        count = half_width // LANES
        total = jnp.zeros((half_rows, LANES), f32)
        for j in range(count):
            here = slice(2 * j * LANES, 2 * (j + 1) * LANES)
            after = 2 * ((j + 1) % count)
            tail = slice(after * LANES, (after + 1) * LANES)
            operands = tuple(
                jnp.concatenate([sides[p][:, here], sides[p][:, tail]], axis=1) for p in range(2)
            )
            both = dot_three(dot_nn, operands, (ch[...], cl[...]))
            span = slice(j * LANES, (j + 1) * LANES)
            for index, part in enumerate(
                (
                    both[:half_rows, :LANES],
                    both[:half_rows, LANES:],
                    both[half_rows:, :LANES],
                    both[half_rows:, LANES:],
                )
            ):
                total = total + jnp.abs(part)
                out_ref[index, :, span] = coef_ref[index, :, span] + part
        sum_ref[...] = jnp.sum(total, axis=0, keepdims=True)

    return pl.pallas_call(
        kernel,
        out_shape=[
            jax.ShapeDtypeStruct(coef_dual.shape, f32),
            jax.ShapeDtypeStruct((1, LANES), f32),
        ],
        cost_estimate=pl.CostEstimate(flops=1 << 30, bytes_accessed=1 << 22, transcendentals=0),
        name="analysis",
    )(new_image, sky_image, halo, coef_dual, *row_tables, *col_tables)


def joined(value, axis, masks, place=0):
    return jnp.concatenate([value] + [flipped(value, axis, mask) for mask in masks], axis=place)


def exchanged(values):
    count = lax.axis_size(AXES)
    sent = jnp.broadcast_to(values[None, :], (count, values.shape[0]))
    return lax.all_to_all(sent, AXES, split_axis=0, concat_axis=0, tiled=True)


def local(sky_image, coef_dual, vis_dual, visibilities, kernel_blocks, tile_rows, tile_counts):
    band_count = lax.axis_size("band")
    group_count = lax.axis_size("vis")
    band_here = lax.axis_index("band")
    group_here = lax.axis_index("vis")
    device = band_here * group_count + group_here
    kernel_here = kernel_blocks[0, 0]
    rows_here = tile_rows[0, 0]
    owners, slot_count = rows_here.shape
    rows, image_width = sky_image.shape
    stripe = image_width // band_count
    samples, length = kernel_here.shape[-2:]
    half_rows = coef_dual.shape[1]
    outer = image_width // LANES
    inner = image_width // outer
    vis_tiles = owners * slot_count
    far = group_count // 4
    tiles = min(far * vis_tiles, max(vis_tiles, 256))
    blocks_f = far * vis_tiles // tiles
    masks_x = tuple(range(1, band_count))
    masks_z = tuple(range(4, group_count, 4))

    live_slots = (
        jnp.arange(slot_count, dtype=jnp.int32)[None, :] < tile_counts[0, 0][:, None]
    ).astype(f32)[:, :, None, None]
    vis_data = visibilities[0, 0]
    vis_state = vis_dual[0, 0]

    cell = band_here * stripe + rows_here.reshape(-1)
    mirrored = cell % outer > outer // 2
    kept_cell = jnp.where(mirrored, image_width - cell, cell)
    code = (kept_cell % outer) * inner + kept_cell // outer + jnp.where(mirrored, FLAG, 0)
    told = exchanged(code.astype(f32))
    by_core = jnp.arange(2)[:, None, None, None]
    by_y = 2 * jnp.arange(2)[None, :, None, None]
    by_x = jnp.arange(band_count)[None, None, :, None]
    by_z = 4 * jnp.arange(far)[None, None, None, :]
    origin = (band_here ^ by_x) * group_count + (group_here ^ (by_core + by_y + by_z))
    chosen = origin.reshape(-1, 1) == jnp.arange(band_count * group_count)[None, :]
    codes = jnp.dot(chosen.astype(f32), told, precision=lax.Precision.HIGHEST)
    codes = jnp.round(codes).astype(jnp.int32)
    codes = codes.reshape(4 * band_count * blocks_f, 1, tiles)
    columns = codes & (FLAG - 1)

    lead = min(8, half_rows)
    coef_halo = shifted(coef_dual[:, half_rows - lead :, :], AXES, 1)

    weights = (live_slots * vis_state).astype(bf16)
    kernel_flat = kernel_here.reshape(vis_tiles, 2 * samples, length)
    weight_real = weights[:, :, 0].reshape(vis_tiles, samples)
    weight_imag = weights[:, :, 1].reshape(vis_tiles, samples)
    weight_pair = jnp.stack(
        [
            jnp.concatenate([weight_real, weight_imag], axis=1),
            jnp.concatenate([weight_imag, -weight_real], axis=1),
        ]
    )
    sent = jnp.einsum("nmt,ynm->ynt", kernel_flat, weight_pair, preferred_element_type=f32)
    sent = sent.astype(bf16)

    def unit(steps):
        angle = (2.0 * math.pi / image_width) * (steps % image_width).astype(f32)
        return jnp.cos(angle), jnp.sin(angle)

    def turned_by(steps, axis):
        near = np.arange(rows)[:, None] * steps[None, :] % image_width * (2.0 * np.pi / image_width)
        near = near if axis else near.T
        near_cos = np.cos(near).astype(np.float32)
        near_sin = np.sin(near).astype(np.float32)
        far_cos, far_sin = unit(device * rows * jnp.expand_dims(jnp.asarray(steps, jnp.int32), 1 - axis))
        return (
            near_cos * far_cos - near_sin * far_sin,
            near_sin * far_cos + near_cos * far_sin,
        )

    wave_cos, wave_sin = turned_by(np.arange(length), 1)
    scale = 1.0 / image_width
    weight_tables = (
        *split_two(scale * jnp.concatenate([wave_cos, wave_sin], axis=0)),
        *split_two(scale * jnp.concatenate([-wave_sin, wave_cos], axis=0)),
    )
    phases_turned = turned_by(np.arange(tiles) // slot_count % owners * length, 0)
    data_parts = jnp.sum(live_slots * vis_data * vis_data, axis=(0, 1)).reshape(-1)
    phases_turned, data_parts = lax.optimization_barrier((phases_turned, data_parts))

    level = joined(sent, "vis", masks_z, 1)
    tile_real = joined(level[0], "band", masks_x)
    tile_imag = joined(level[1], "vis", (2,))
    tile_real = joined(tile_real, "vis", (2,))
    tile_imag = joined(tile_imag, "band", masks_x)
    tile_real = tile_real.reshape(2, band_count, blocks_f, tiles, length)
    tile_imag = tile_imag.reshape(band_count, 2, blocks_f, tiles, length)
    far_real = flipped(tile_real, "vis", 1)
    far_imag = flipped(tile_imag, "vis", 1)
    smooth = synthesis(coef_halo, coef_dual)

    counts = (2, band_count, blocks_f)
    large = 8 * band_count * far * vis_tiles * length * 4 > 1 << 23
    new_image, near_rows, spec_real, spec_imag, sent_real, sent_imag = image_step(
        (tile_real, tile_imag, far_real, far_imag), codes, columns, weight_tables,
        phases_turned, sky_image, smooth, bf16 if large else f32,
    )
    image_halo = shifted(near_rows, AXES, -1)
    mine_real, mine_imag = forward_parts(
        (spec_real, spec_imag), codes, columns, weight_tables, phases_turned, counts
    )
    other_real = flipped(sent_real, "vis", 1)
    other_imag = flipped(sent_imag, "vis", 1)
    step_y = band_count * blocks_f
    step_x = 2 * blocks_f

    def real_at(begin, size):
        return mine_real[begin : begin + size] + other_real[begin : begin + size]

    def imag_at(begin, size):
        return mine_imag[begin : begin + size] + other_imag[begin : begin + size]

    met_real = flipped(real_at(step_y, step_y), "vis", 2)
    met_imag = [flipped(imag_at(m * step_x, step_x), "band", m) for m in masks_x]

    def real_kept(m):
        return real_at(m * blocks_f, blocks_f) + met_real[m * blocks_f : (m + 1) * blocks_f]

    def imag_kept(y):
        span = slice(y * blocks_f, (y + 1) * blocks_f)
        return sum([met[span] for met in met_imag], imag_at(y * blocks_f, blocks_f))

    left_real = [flipped(real_kept(m), "band", m) for m in masks_x]
    left_imag = flipped(imag_kept(1), "vis", 2)
    left_real = sum(left_real, real_kept(0))
    left_imag = left_imag + imag_kept(0)
    left = jnp.stack([left_real, left_imag]).reshape(2, far, vis_tiles, length)
    seen = [flipped(left[:, 1 + index], "vis", mask) for index, mask in enumerate(masks_z)]
    seen = sum(seen, left[:, 0])

    moved_coef, abs_parts = analysis(new_image, sky_image, image_halo, coef_dual)
    totals = exchanged(jnp.concatenate([abs_parts[0], data_parts]))
    coef_total = jnp.sum(totals[:, :LANES])
    data_square = jnp.sum(totals[:, LANES:])
    threshold = 0.5 * coef_total / (image_width * image_width)
    new_coef = jnp.clip(moved_coef, -threshold, threshold)

    seen = lax.reduce_precision(seen, 8, 7).astype(bf16)
    met = jnp.einsum("nmt,ynt->nym", kernel_flat, seen, preferred_element_type=f32)
    predicted = jnp.stack(
        [
            met[:, 0, :samples] - met[:, 1, samples:],
            met[:, 1, :samples] + met[:, 0, samples:],
        ],
        axis=1,
    ).reshape(vis_state.shape)
    residual = live_slots * (vis_state + predicted - vis_data)
    squares = jnp.sum(residual * residual, axis=(0, 1)).reshape(-1)
    norm_square = jnp.sum(exchanged(squares))
    radius = 0.5 * jnp.sqrt(data_square + 1e-06)
    size_value = jnp.sqrt(norm_square + 1e-06)
    new_vis = residual * (1.0 - jnp.minimum(1.0, radius / size_value))
    return (new_image, new_coef, new_vis[None, None])


def solution(mesh):
    return jax.shard_map(
        local,
        mesh=mesh,
        in_specs=(
            P(("band", "vis"), None),
            P(None, ("band", "vis"), None),
            P("band", "vis", None, None, None, None),
            P("band", "vis", None, None, None, None),
            P("band", "vis", None, None, None, None, None),
            P("band", "vis", None, None),
            P("band", "vis", None),
        ),
        out_specs=(
            P(("band", "vis"), None),
            P(None, ("band", "vis"), None),
            P("band", "vis", None, None, None, None),
        ),
        check_vma=False,
    )
```

time: 158 us -> 145 us (0.918)
  Pallas kernels: 50.7 us -> 40.5 us
  blocking collectives: 0 us -> 9.4 us
  waiting for transfers between devices: 33.2 us -> 27.9 us
  local copies, waits for them, and re-layouts: 9.99 us -> 5.27 us
  other arithmetic: 25.3 us -> 23.4 us
    pallas_call x3 -> x2, Pallas kernels: 38.5 us -> 27.6 us  [the longest x1 21 us: image_step(): pl.pallas_call(kernel, in_specs=[*[vmem()] * 2, any_space, any_space, pl....]
    all_to_all x0 -> x1, blocking collectives: none -> 9.4 us  [exchanged(): return lax.all_to_all(sent, AXES, split_axis=0, concat_axis=0, tiled=True)]
    add x6 -> x7, other arithmetic: 2.77 us -> 10.8 us  [the longest x1 2.06 us: imag_at(): return mine_imag[begin:begin + size] + other_imag[begin:begin + size]]
    another operation x7 -> x0, other arithmetic: 7.63 us -> none  [the longest x6 6.28 us: stacked(): jnp.stack([value] + [flipped(value, axis, mask) for mask in masks], axis=...]
    ppermute x17 -> x18, waiting for transfers between devices: 27.5 us -> 22.2 us  [flipped(): lax.ppermute(block, axis, [(i, i ^ mask) for i in range(lax.axis_size(axi...]
    ppermute x17 -> x18, starting transfers between devices: 19.4 us -> 22.6 us  [flipped(): lax.ppermute(block, axis, [(i, i ^ mask) for i in range(lax.axis_size(axi...]
    concatenate x1 -> x6, other arithmetic: 0.72 us -> 3.86 us  [the longest x5 3.2 us: joined(): jnp.concatenate([value] + [flipped(value, axis, mask) for mask in masks],...]
    sin x2 -> x1, other arithmetic: 3.16 us -> 0.05 us  [unit(): return (jnp.cos(angle), jnp.sin(angle))]
  transfers between devices with their start and end apart: 21 -> 22, of which waited for: 9 -> 8; matrix products, arithmetic and copies ran while one was open for 12% -> 16% of each run, Pallas kernels for 13% -> 13%
where the time goes in v2:
time: 145 us
  Pallas kernels  40.5 us (28%)
  starting transfers between devices  32.9 us (23%)
  waiting for transfers between devices  27.9 us (19%)
  other arithmetic  23.4 us (16%)
  blocking collectives  9.4 us (6%)
  local copies, waits for them, and re-layouts  5.27 us (4%)
  between operations  3.13 us (2%)
  matrix products  1.97 us (1%)
    ppermute x18, starting transfers between devices, flipped(): lax.ppermute(block, axis, [(i, i ^ mask) for i in range(lax.axis_size(axi...  22.6 us
    ppermute x18, waiting for transfers between devices, flipped(): lax.ppermute(block, axis, [(i, i ^ mask) for i in range(lax.axis_size(axi...  22.2 us
    pallas_call x1, Pallas kernels, image_step(): pl.pallas_call(kernel, in_specs=[*[vmem()] * 2, any_space, any_space, pl....  21 us
    all_to_all x1, blocking collectives, exchanged(): return lax.all_to_all(sent, AXES, split_axis=0, concat_axis=0, tiled=True)  9.4 us
    all_to_all x2, starting transfers between devices, exchanged(): return lax.all_to_all(sent, AXES, split_axis=0, concat_axis=0, tiled=True)  8.67 us
    pallas_call x1, Pallas kernels, analysis(): pl.pallas_call(kernel, out_shape=[jax.ShapeDtypeStruct(coef_dual.shape, f...  7.02 us
    pallas_call x1, Pallas kernels, forward_parts(): pl.pallas_call(kernel, grid=(part,), in_specs=[*[whole(x) for x in spectr...  6.57 us
    pallas_call x1, Pallas kernels, synthesis(): pl.pallas_call(kernel, out_shape=jax.ShapeDtypeStruct((rows, 2 * half_wid...  5.85 us
  transfers between devices with their start and end apart: 22, of which 8 were waited for; matrix products, arithmetic and copies ran while one was open for 16% of the time, Pallas kernels for 13%

profile of v2, /device:TPU:0, one launch (start us, length us, event | category | flops | bytes accessed | tf_op | source)
XLA Modules:
  0.0 144.5 jit_solution(15896456731549521440)
XLA Ops:
  0.7 0.9 fusion.32
  1.6 1.0 fusion.18
  3.3 5.1 %collective-permute-start.2 = (bf16[2,64,256]{2,0,1:T(2,128)(2,1)S(1)}, bf16[2,64,256]{2,0,1:T(2,128)(2,1)S(1)}, u32[]{:S(2)}, u32[]{:S(2)}) collective-permute-start(bf16[2,64,256]{2,0,1:T(2,128)(2,1)S(1)} %fusion), channel_id=1, source_target_pairs={{0,12},{1,13},{2,14},{3,15},{4,8},{5,9},{6,10},{7,11},{8,4},{9,5},... | collective-permute-start | bytes 196616 | tf_op jit(solution)/shard_map/ppermute | solution.py:38
  8.4 0.6 collective-permute-start
  9.3 0.6 broadcast_in_dim.15
  9.9 6.1 %all-to-all-start = ((f32[32,1,64]{2,1,0:T(1,128)}), f32[32,1,64]{2,1,0:T(1,128)}, u32[]{:S(2)}, u32[]{:S(2)}) async-start(f32[32,1,64]{2,1,0:T(1,128)} %broadcast_in_dim.15), calls=%async_computation | async-start | bytes 32768 | tf_op jit(solution)/shard_map/all_to_all | solution.py:540
  16.0 1.7 %slice.97 = f32[4,8,2048]{2,1,0:T(8,128)} slice(f32[4,64,2048]{2,1,0:T(8,128)} %coef_ref.3), slice={[0:4], [56:64], [0:2048]} | slice | bytes 524288 | tf_op jit(solution)/shard_map/slice | solution.py:588
  18.1 0.8 multiply_add_fusion
  19.8 1.7 %collective-permute-start.3 = (bf16[256,256]{1,0:T(8,128)(2,1)S(1)}, bf16[256,256]{1,0:T(8,128)(2,1)S(1)}, u32[]{:S(2)}, u32[]{:S(2)}) collective-permute-start(bf16[256,256]{1,0:T(8,128)(2,1)S(1)} %bitcast.74), channel_id=1, source_target_pairs={{0,16},{16,0},{1,17},{17,1},{2,18},{18,2},{3,19},{19,3},{4,20},{20... | collective-permute-start | bytes 393224 | tf_op jit(solution)/shard_map/ppermute | solution.py:38
  21.6 1.5 %collective-permute-start.5 = (bf16[256,256]{1,0:T(8,128)(2,1)S(1)}, bf16[256,256]{1,0:T(8,128)(2,1)S(1)}, u32[]{:S(2)}, u32[]{:S(2)}) collective-permute-start(bf16[256,256]{1,0:T(8,128)(2,1)S(1)} %bitcast.77), channel_id=1, source_target_pairs={{0,2},{1,3},{2,0},{3,1},{4,6},{5,7},{6,4},{7,5},{8,10},{9,11},{10,... | collective-permute-start | bytes 393224 | tf_op jit(solution)/shard_map/ppermute | solution.py:38
  23.1 2.4 %collective-permute-done.3 = bf16[256,256]{1,0:T(8,128)(2,1)S(1)} collective-permute-done((bf16[256,256]{1,0:T(8,128)(2,1)S(1)}, bf16[256,256]{1,0:T(8,128)(2,1)S(1)}, u32[]{:S(2)}, u32[]{:S(2)}) %collective-permute-start.3) | collective-permute-done | bytes 131104 | tf_op jit(solution)/shard_map/ppermute | solution.py:38
  25.6 5.1 %collective-permute-start.4 = (bf16[512,256]{1,0:T(8,128)(2,1)S(1)}, bf16[512,256]{1,0:T(8,128)(2,1)}, u32[]{:S(2)}, u32[]{:S(2)}) collective-permute-start(bf16[512,256]{1,0:T(8,128)(2,1)S(1)} %pad_maximum_fusion.3), channel_id=1, source_target_pairs={{0,2},{1,3},{2,0},{3,1},{4,6},{5,7},{6,4},{7,5},{8,10},{9,11},{10,... | collective-permute-start | bytes 786440 | tf_op jit(solution)/shard_map/ppermute | solution.py:38
  30.7 0.7 pad_maximum_fusion.4
  31.4 1.2 collective-permute-start.6
  32.9 0.9 fusion.3
  33.8 6.0 %collective-permute-done.6 = bf16[512,256]{1,0:T(8,128)(2,1)} collective-permute-done((bf16[512,256]{1,0:T(8,128)(2,1)}, bf16[512,256]{1,0:T(8,128)(2,1)}, u32[]{:S(2)}, u32[]{:S(2)}) %collective-permute-start.6) | collective-permute-done | bytes 262176 | tf_op jit(solution)/shard_map/ppermute | solution.py:38
  39.8 1.0 pad_maximum_fusion.1
  40.9 1.1 pad_maximum_fusion
  42.4 0.9 fusion.1
  44.0 5.8 %synthesis.1.smo_any = f32[128,4096]{1,0:T(8,128)} custom-call(f32[4,8,2048]{2,1,0:T(8,128)} %collective-permute-done.9.halo_ref, f32[4,64,2048]{2,1,0:T(8,128)} %coef_ref.3, bf16[128,144]{1,0:T(8,128)(2,1)} %constant.137.clone.rh, bf16[128,144]{1,0:T(8,128)(2,1)} %constant.138.clone.rl, bf16[512,256]{1,0:T(8,128)(2,1)} %constant.139.clone.ch, ...), custom_call_target="tpu_custom_call" | custom-call | flops 1073741824 | bytes 4194304 | tf_op jit(solution)/shard_map/synthesis/pallas_call | solution.py:480
  49.9 21.0 %image_step.1 = (f32[128,4096]{1,0:T(8,128)}, f32[8,4096]{1,0:T(8,128)}, f32[2176,128]{1,0:T(8,128)}, f32[2176,128]{1,0:T(8,128)}, f32[4,256,256]{2,1,0:T(8,128)}, /*index=5*/f32[4,256,256]{2,1,0:T(8,128)}) custom-call(bf16[2,2,1,256,256]{4,3,2,1,0:T(8,128)(2,1)} %bitcast.85, bf16[2,2,1,256,256]{4,3,2,1,0:T(8,128)(2,1)} %bitcast.83, ...), custom_call_target="tpu_custom_call" | custom-call | flops 5100273664 | bytes 16777216 | tf_op jit(solution)/shard_map/image_step/pallas_call | solution.py:312
  71.5 1.5 %collective-permute-start.10 = (f32[8,4096]{1,0:T(8,128)}, f32[8,4096]{1,0:T(8,128)S(1)}, u32[]{:S(2)}, u32[]{:S(2)}) collective-permute-start(f32[8,4096]{1,0:T(8,128)} %get-tuple-element.19), channel_id=1, source_target_pairs={{1,0},{2,1},{3,2},{4,3},{5,4},{6,5},{7,6},{8,7},{9,8},{10,9},{11,1... | collective-permute-start | bytes 393224 | tf_op jit(solution)/shard_map/ppermute | solution.py:34
  73.0 6.6 %parts.1 = (f32[4,256,256]{2,1,0:T(8,128)}, f32[4,256,256]{2,1,0:T(8,128)}) custom-call(f32[2176,128]{1,0:T(8,128)} %get-tuple-element.23.xr, f32[2176,128]{1,0:T(8,128)} %get-tuple-element.24.xi, s32[8,1,256]{2,1,0:T(1,128)} %broadcast_and_fusion.where, s32[8,1,256]{2,1,0:T(1,128)} %copy-done.11, bf16[256,256]{1,0:T(8,128)(2,1)} %get-tuple-element.45.wrh, ...), custom_call_target="tpu_custom_call" | custom-call | flops 805306368 | bytes 8388608 | tf_op jit(solution)/shard_map/parts/pallas_call | solution.py:377
  79.6 2.1 %slice_add_fusion = f32[2,256,256]{2,1,0:T(8,128)} fusion(f32[4,256,256]{2,1,0:T(8,128)} %collective-permute-done.14, f32[4,256,256]{2,1,0:T(8,128)} %get-tuple-element.27), kind=kLoop, calls=%fused_computation.11 | loop fusion | flops 131072 | bytes 1572864 | tf_op jit(solution)/shard_map/add | solution.py:658
  82.0 1.9 %slice_add_fusion.1 = f32[2,256,256]{2,1,0:T(8,128)} fusion(f32[4,256,256]{2,1,0:T(8,128)S(1)} %collective-permute-done.11, f32[4,256,256]{2,1,0:T(8,128)} %get-tuple-element.25), kind=kLoop, calls=%fused_computation.12 | loop fusion | flops 131072 | bytes 1572864 | tf_op jit(solution)/shard_map/add | solution.py:655
  83.9 1.2 collective-permute-start.12
  85.1 0.6 copy-done.8
  85.7 7.0 %analysis.1 = (f32[4,64,2048]{2,1,0:T(8,128)}, f32[1,128]{1,0:T(1,128)}) custom-call(f32[128,4096]{1,0:T(8,128)} %get-tuple-element.13.new_ref, f32[128,4096]{1,0:T(8,128)} %sky_ref.1, f32[8,4096]{1,0:T(8,128)} %copy-done.8, f32[4,64,2048]{2,1,0:T(8,128)} %coef_ref.3, bf16[128,136]{1,0:T(8,128)(2,1)} %constant.143.clone.rh, ...), custom_call_target="tpu_custom_call" | custom-call | flops 1073741824 | bytes 4194304 | tf_op jit(solution)/shard_map/analysis/pallas_call | solution.py:522
  92.8 0.7 pad_maximum_fusion.6
  93.4 9.4 %all_to_all.24 = f32[32,1,192]{2,1,0:T(1,128)S(1)} all-to-all(f32[32,1,192]{2,1,0:T(1,128)S(1)} %broadcast_in_dim.16), channel_id=1, replica_groups=mesh['band'=2,'vis'=16] {'band','vis'}, dimensions={0} | all-to-all | bytes 49152 | tf_op jit(solution)/shard_map/all_to_all | solution.py:540
  102.9 1.9 %slice_add_fusion.4 = f32[1,256,256]{2,1,0:T(8,128)} fusion(f32[2,256,256]{2,1,0:T(8,128)} %collective-permute-done.15, f32[4,256,256]{2,1,0:T(8,128)} %collective-permute-done.14, f32[4,256,256]{2,1,0:T(8,128)} %get-tuple-element.27), kind=kLoop, calls=%fused_computation.24 | loop fusion | flops 131072 | bytes 1048576 | tf_op jit(solution)/shard_map/add | solution.py:668
  105.2 1.8 %slice_add_fusion.6 = f32[1,256,256]{2,1,0:T(8,128)} fusion(f32[2,256,256]{2,1,0:T(8,128)} %collective-permute-done.12, f32[4,256,256]{2,1,0:T(8,128)S(1)} %collective-permute-done.11, f32[4,256,256]{2,1,0:T(8,128)} %get-tuple-element.25), kind=kLoop, calls=%fused_computation.26 | loop fusion | flops 131072 | bytes 1048576 | tf_op jit(solution)/shard_map/add | solution.py:664
  107.0 0.6 collective-permute-start.13
  108.9 4.5 %collective-permute-done.16 = f32[1,256,256]{2,1,0:T(8,128)} collective-permute-done((f32[1,256,256]{2,1,0:T(8,128)}, f32[1,256,256]{2,1,0:T(8,128)}, u32[]{:S(2)}, u32[]{:S(2)}) %collective-permute-start.16) | collective-permute-done | bytes 262176 | tf_op jit(solution)/shard_map/ppermute | solution.py:38
  113.4 1.3 fusion.4
  115.3 1.1 fusion.5
  117.6 1.5 %collective-permute-start.19 = (f32[2,64,256]{2,0,1:T(2,128)S(1)}, f32[2,64,256]{2,0,1:T(2,128)S(1)}, u32[]{:S(2)}, u32[]{:S(2)}) collective-permute-start(f32[2,64,256]{2,0,1:T(2,128)S(1)} %get-tuple-element.32), channel_id=1, source_target_pairs={{0,12},{1,13},{2,14},{3,15},{4,8},{5,9},{6,10},{7,11},{8,4},{9,5},... | collective-permute-start | bytes 393224 | tf_op jit(solution)/shard_map/ppermute | solution.py:38
  119.1 1.5 %collective-permute-start.18 = (f32[2,64,256]{2,0,1:T(2,128)S(1)}, f32[2,64,256]{2,0,1:T(2,128)S(1)}, u32[]{:S(2)}, u32[]{:S(2)}) collective-permute-start(f32[2,64,256]{2,0,1:T(2,128)S(1)} %get-tuple-element.33), channel_id=1, source_target_pairs={{0,8},{1,9},{2,10},{3,11},{4,12},{5,13},{6,14},{7,15},{8,0},{9,1},... | collective-permute-start | bytes 393224 | tf_op jit(solution)/shard_map/ppermute | solution.py:38
  120.6 1.6 %maximum_minimum_fusion = f32[4,64,2048]{2,1,0:T(8,128)} fusion(f32[4,64,2048]{2,1,0:T(8,128)S(1)} %copy-done.1, f32[]{:T(128)S(6)} %neg.11, f32[]{:T(128)S(6)} %div.22), kind=kLoop, calls=%fused_computation | loop fusion | flops 1048576 | bytes 4194312 | tf_op jit(solution)/shard_map/jit(clip)/min | solution.py:683
  122.1 2.0 %collective-permute-done.17 = f32[2,64,256]{2,0,1:T(2,128)S(1)} collective-permute-done((f32[2,64,256]{2,0,1:T(2,128)S(1)}, f32[2,64,256]{2,0,1:T(2,128)S(1)}, u32[]{:S(2)}, u32[]{:S(2)}) %collective-permute-start.17) | collective-permute-done | bytes 131104 | tf_op jit(solution)/shard_map/ppermute | solution.py:38
  124.2 2.0 %collective-permute-done.19 = f32[2,64,256]{2,0,1:T(2,128)S(1)} collective-permute-done((f32[2,64,256]{2,0,1:T(2,128)S(1)}, f32[2,64,256]{2,0,1:T(2,128)S(1)}, u32[]{:S(2)}, u32[]{:S(2)}) %collective-permute-start.19) | collective-permute-done | bytes 131104 | tf_op jit(solution)/shard_map/ppermute | solution.py:38
  126.2 4.9 %collective-permute-done.18 = f32[2,64,256]{2,0,1:T(2,128)S(1)} collective-permute-done((f32[2,64,256]{2,0,1:T(2,128)S(1)}, f32[2,64,256]{2,0,1:T(2,128)S(1)}, u32[]{:S(2)}, u32[]{:S(2)}) %collective-permute-start.18) | collective-permute-done | bytes 131104 | tf_op jit(solution)/shard_map/ppermute | solution.py:38
  131.1 0.7 fusion.16
  132.2 0.6 broadcast_in_dim.18
  132.8 2.5 %all-to-all-start.2 = ((f32[32,1,64]{2,1,0:T(1,128)}), f32[32,1,64]{2,1,0:T(1,128)S(1)}, u32[]{:S(2)}, u32[]{:S(2)}) async-start(f32[32,1,64]{2,1,0:T(1,128)} %broadcast_in_dim.18), calls=%async_computation.2 | async-start | bytes 32768 | tf_op jit(solution)/shard_map/all_to_all | solution.py:540
  135.4 0.7 slice_reduce_fusion
  136.8 5.7 %all-to-all-done.2 = f32[32,1,64]{2,1,0:T(1,128)S(1)} async-done(((f32[32,1,64]{2,1,0:T(1,128)}), f32[32,1,64]{2,1,0:T(1,128)S(1)}, u32[]{:S(2)}, u32[]{:S(2)}) %all-to-all-start.2) | async-done | bytes 8224 | tf_op jit(solution)/shard_map/all_to_all | solution.py:540
  143.8 0.8 fusion.21
  (92 shorter events, 8.6 us)
Async XLA Ops:
  0.6 2.3 %copy-start = (bf16[1,1,16,4,2,32,256]{6,5,4,3,2,1,0:T(8,128)(2,1)S(1)}, bf16[1,1,16,4,2,32,256]{6,5,4,3,2,1,0:T(8,128)(2,1)}, u32[]{:S(2)}) copy-start(bf16[1,1,16,4,2,32,256]{6,5,4,3,2,1,0:T(8,128)(2,1)} %param.27) | copy-start | bytes 6291460
  0.6 17.3 %copy-start.13 = (s32[256]{0:T(256)S(1)}, s32[256]{0:T(256)}, u32[]{:S(2)}) copy-start(s32[256]{0:T(256)} %constant.134.clone) | copy-start | bytes 3076
  0.7 17.4 %copy-start.9 = (f32[256,128]{1,0:T(8,128)S(1)}, f32[256,128]{1,0:T(8,128)}, u32[]{:S(2)}) copy-start(f32[256,128]{1,0:T(8,128)} %constant.136.clone) | copy-start | bytes 393220
  0.7 17.4 %copy-start.10 = (f32[256,128]{1,0:T(8,128)S(1)}, f32[256,128]{1,0:T(8,128)}, u32[]{:S(2)}) copy-start(f32[256,128]{1,0:T(8,128)} %constant.135.clone) | copy-start | bytes 393220
  0.7 18.3 %copy-start.6 = (f32[128,256]{1,0:T(8,128)S(1)}, f32[128,256]{1,0:T(8,128)}, u32[]{:S(2)}) copy-start(f32[128,256]{1,0:T(8,128)} %constant.133.clone) | copy-start | bytes 393220
  0.7 18.2 %copy-start.7 = (f32[128,256]{1,0:T(8,128)S(1)}, f32[128,256]{1,0:T(8,128)}, u32[]{:S(2)}) copy-start(f32[128,256]{1,0:T(8,128)} %constant.132.clone) | copy-start | bytes 393220
  0.7 8.4 %copy-start.12 = (s32[1,1,16,4]{2,3,1,0:T(4,128)S(1)}, s32[1,1,16,4]{2,3,1,0:T(4,128)}, u32[]{:S(2)}) copy-start(s32[1,1,16,4]{2,3,1,0:T(4,128)} %param.28) | copy-start | bytes 772
  3.3 15.7 %collective-permute-start.2 = (bf16[2,64,256]{2,0,1:T(2,128)(2,1)S(1)}, bf16[2,64,256]{2,0,1:T(2,128)(2,1)S(1)}, u32[]{:S(2)}, u32[]{:S(2)}) collective-permute-start(bf16[2,64,256]{2,0,1:T(2,128)(2,1)S(1)} %fusion), channel_id=1, source_target_pairs={{0,12},{1,13},{2,14},{3,15},{4,8},{5,9},{6,10},{7,11},{8,4},{9,5},... | collective-permute-start | bytes 196616 | tf_op jit(solution)/shard_map/ppermute | solution.py:38
  8.4 10.6 %collective-permute-start.1 = (bf16[2,64,256]{2,0,1:T(2,128)(2,1)S(1)}, bf16[2,64,256]{2,0,1:T(2,128)(2,1)S(1)}, u32[]{:S(2)}, u32[]{:S(2)}) collective-permute-start(bf16[2,64,256]{2,0,1:T(2,128)(2,1)S(1)} %fusion), channel_id=1, source_target_pairs={{0,8},{1,9},{2,10},{3,11},{4,12},{5,13},{6,14},{7,15},{8,0},{9,1},... | collective-permute-start | bytes 196616 | tf_op jit(solution)/shard_map/ppermute | solution.py:38
  8.4 10.6 %collective-permute-start = (bf16[2,64,256]{2,0,1:T(2,128)(2,1)S(1)}, bf16[2,64,256]{2,0,1:T(2,128)(2,1)S(1)}, u32[]{:S(2)}, u32[]{:S(2)}) collective-permute-start(bf16[2,64,256]{2,0,1:T(2,128)(2,1)S(1)} %fusion), channel_id=1, source_target_pairs={{0,4},{1,5},{2,6},{3,7},{4,0},{5,1},{6,2},{7,3},{8,12},{9,13},{10,... | collective-permute-start | bytes 196616 | tf_op jit(solution)/shard_map/ppermute | solution.py:38
  9.9 32.5 %all-to-all-start = ((f32[32,1,64]{2,1,0:T(1,128)}), f32[32,1,64]{2,1,0:T(1,128)}, u32[]{:S(2)}, u32[]{:S(2)}) async-start(f32[32,1,64]{2,1,0:T(1,128)} %broadcast_in_dim.15), calls=%async_computation | async-start | bytes 32768 | tf_op jit(solution)/shard_map/all_to_all | solution.py:540
  17.7 26.3 %collective-permute-start.9 = (f32[4,8,2048]{2,1,0:T(8,128)}, f32[4,8,2048]{2,1,0:T(8,128)}, u32[]{:S(2)}, u32[]{:S(2)}) collective-permute-start(f32[4,8,2048]{2,1,0:T(8,128)} %slice.97), channel_id=1, source_target_pairs={{31,0},{0,1},{1,2},{2,3},{3,4},{4,5},{5,6},{6,7},{7,8},{8,9},{9,10... | collective-permute-start | bytes 786440 | tf_op jit(solution)/shard_map/ppermute | solution.py:34
  19.8 5.8 %collective-permute-start.3 = (bf16[256,256]{1,0:T(8,128)(2,1)S(1)}, bf16[256,256]{1,0:T(8,128)(2,1)S(1)}, u32[]{:S(2)}, u32[]{:S(2)}) collective-permute-start(bf16[256,256]{1,0:T(8,128)(2,1)S(1)} %bitcast.74), channel_id=1, source_target_pairs={{0,16},{16,0},{1,17},{17,1},{2,18},{18,2},{3,19},{19,3},{4,20},{20... | collective-permute-start | bytes 393224 | tf_op jit(solution)/shard_map/ppermute | solution.py:38
  21.6 9.1 %collective-permute-start.5 = (bf16[256,256]{1,0:T(8,128)(2,1)S(1)}, bf16[256,256]{1,0:T(8,128)(2,1)S(1)}, u32[]{:S(2)}, u32[]{:S(2)}) collective-permute-start(bf16[256,256]{1,0:T(8,128)(2,1)S(1)} %bitcast.77), channel_id=1, source_target_pairs={{0,2},{1,3},{2,0},{3,1},{4,6},{5,7},{6,4},{7,5},{8,10},{9,11},{10,... | collective-permute-start | bytes 393224 | tf_op jit(solution)/shard_map/ppermute | solution.py:38
  25.6 15.2 %collective-permute-start.4 = (bf16[512,256]{1,0:T(8,128)(2,1)S(1)}, bf16[512,256]{1,0:T(8,128)(2,1)}, u32[]{:S(2)}, u32[]{:S(2)}) collective-permute-start(bf16[512,256]{1,0:T(8,128)(2,1)S(1)} %pad_maximum_fusion.3), channel_id=1, source_target_pairs={{0,2},{1,3},{2,0},{3,1},{4,6},{5,7},{6,4},{7,5},{8,10},{9,11},{10,... | collective-permute-start | bytes 786440 | tf_op jit(solution)/shard_map/ppermute | solution.py:38
  31.4 8.4 %collective-permute-start.6 = (bf16[512,256]{1,0:T(8,128)(2,1)}, bf16[512,256]{1,0:T(8,128)(2,1)}, u32[]{:S(2)}, u32[]{:S(2)}) collective-permute-start(bf16[512,256]{1,0:T(8,128)(2,1)} %pad_maximum_fusion.4), channel_id=1, source_target_pairs={{0,16},{16,0},{1,17},{17,1},{2,18},{18,2},{3,19},{19,3},{4,20},{20... | collective-permute-start | bytes 786440 | tf_op jit(solution)/shard_map/ppermute | solution.py:38
  40.8 9.1 %copy-start.4 = (bf16[1024,256]{1,0:T(8,128)(2,1)}, bf16[1024,256]{1,0:T(8,128)(2,1)S(1)}, u32[]{:S(2)}) copy-start(bf16[1024,256]{1,0:T(8,128)(2,1)S(1)} %pad_maximum_fusion.1) | copy-start | bytes 1572868
  40.8 9.1 %collective-permute-start.8 = (bf16[2,2,1,256,256]{4,3,2,1,0:T(8,128)(2,1)S(1)}, bf16[2,2,1,256,256]{4,3,2,1,0:T(8,128)(2,1)}, u32[]{:S(2)}, u32[]{:S(2)}) collective-permute-start(bf16[2,2,1,256,256]{4,3,2,1,0:T(8,128)(2,1)S(1)} %bitcast.82), channel_id=1, source_target_pairs={{0,1},{1,0},{2,3},{3,2},{4,5},{5,4},{6,7},{7,6},{8,9},{9,8},{10,11... | collective-permute-start | bytes 1572872 | tf_op jit(solution)/shard_map/ppermute | solution.py:38
  41.9 7.9 %copy-start.5 = (bf16[1024,256]{1,0:T(8,128)(2,1)}, bf16[1024,256]{1,0:T(8,128)(2,1)S(1)}, u32[]{:S(2)}) copy-start(bf16[1024,256]{1,0:T(8,128)(2,1)S(1)} %pad_maximum_fusion) | copy-start | bytes 1572868
  42.0 7.9 %collective-permute-start.7 = (bf16[2,2,1,256,256]{4,3,2,1,0:T(8,128)(2,1)S(1)}, bf16[2,2,1,256,256]{4,3,2,1,0:T(8,128)(2,1)}, u32[]{:S(2)}, u32[]{:S(2)}) collective-permute-start(bf16[2,2,1,256,256]{4,3,2,1,0:T(8,128)(2,1)S(1)} %bitcast.84), channel_id=1, source_target_pairs={{0,1},{1,0},{2,3},{3,2},{4,5},{5,4},{6,7},{7,6},{8,9},{9,8},{10,11... | collective-permute-start | bytes 1572872 | tf_op jit(solution)/shard_map/ppermute | solution.py:38
  43.4 6.5 %copy-start.11 = (s32[8,1,256]{2,1,0:T(1,128)}, s32[8,1,256]{2,1,0:T(1,128)S(1)}, u32[]{:S(2)}) copy-start(s32[8,1,256]{2,1,0:T(1,128)S(1)} %reshape.230.code_ref) | copy-start | bytes 24580
  70.9 8.7 %collective-permute-start.14 = (f32[4,256,256]{2,1,0:T(8,128)}, f32[4,256,256]{2,1,0:T(8,128)}, u32[]{:S(2)}, u32[]{:S(2)}) collective-permute-start(f32[4,256,256]{2,1,0:T(8,128)} %get-tuple-element.28), channel_id=1, source_target_pairs={{0,1},{1,0},{2,3},{3,2},{4,5},{5,4},{6,7},{7,6},{8,9},{9,8},{10,11... | collective-permute-start | bytes 3145736 | tf_op jit(solution)/shard_map/ppermute | solution.py:38
  71.1 10.8 %collective-permute-start.11 = (f32[4,256,256]{2,1,0:T(8,128)}, f32[4,256,256]{2,1,0:T(8,128)S(1)}, u32[]{:S(2)}, u32[]{:S(2)}) collective-permute-start(f32[4,256,256]{2,1,0:T(8,128)} %get-tuple-element.26), channel_id=1, source_target_pairs={{0,1},{1,0},{2,3},{3,2},{4,5},{5,4},{6,7},{7,6},{8,9},{9,8},{10,11... | collective-permute-start | bytes 3145736 | tf_op jit(solution)/shard_map/ppermute | solution.py:38
  71.5 13.6 %collective-permute-start.10 = (f32[8,4096]{1,0:T(8,128)}, f32[8,4096]{1,0:T(8,128)S(1)}, u32[]{:S(2)}, u32[]{:S(2)}) collective-permute-start(f32[8,4096]{1,0:T(8,128)} %get-tuple-element.19), channel_id=1, source_target_pairs={{1,0},{2,1},{3,2},{4,3},{5,4},{6,5},{7,6},{8,7},{9,8},{10,9},{11,1... | collective-permute-start | bytes 393224 | tf_op jit(solution)/shard_map/ppermute | solution.py:34
  81.7 21.2 %collective-permute-start.15 = (f32[2,256,256]{2,1,0:T(8,128)}, f32[2,256,256]{2,1,0:T(8,128)}, u32[]{:S(2)}, u32[]{:S(2)}) collective-permute-start(f32[2,256,256]{2,1,0:T(8,128)} %slice_add_fusion), channel_id=1, source_target_pairs={{0,16},{16,0},{1,17},{17,1},{2,18},{18,2},{3,19},{19,3},{4,20},{20... | collective-permute-start | bytes 1572872 | tf_op jit(solution)/shard_map/ppermute | solution.py:38
  83.9 21.4 %collective-permute-start.12 = (f32[2,256,256]{2,1,0:T(8,128)}, f32[2,256,256]{2,1,0:T(8,128)}, u32[]{:S(2)}, u32[]{:S(2)}) collective-permute-start(f32[2,256,256]{2,1,0:T(8,128)} %slice_add_fusion.1), channel_id=1, source_target_pairs={{0,2},{1,3},{2,0},{3,1},{4,6},{5,7},{6,4},{7,5},{8,10},{9,11},{10,... | collective-permute-start | bytes 1572872 | tf_op jit(solution)/shard_map/ppermute | solution.py:38
  85.1 0.7 copy-start.8
  104.7 8.6 %collective-permute-start.16 = (f32[1,256,256]{2,1,0:T(8,128)}, f32[1,256,256]{2,1,0:T(8,128)}, u32[]{:S(2)}, u32[]{:S(2)}) collective-permute-start(f32[1,256,256]{2,1,0:T(8,128)} %slice_add_fusion.4), channel_id=1, source_target_pairs={{0,2},{1,3},{2,0},{3,1},{4,6},{5,7},{6,4},{7,5},{8,10},{9,11},{10,... | collective-permute-start | bytes 786440 | tf_op jit(solution)/shard_map/ppermute | solution.py:38
  107.0 8.3 %collective-permute-start.13 = (f32[1,256,256]{2,1,0:T(8,128)}, f32[1,256,256]{2,1,0:T(8,128)S(1)}, u32[]{:S(2)}, u32[]{:S(2)}) collective-permute-start(f32[1,256,256]{2,1,0:T(8,128)} %slice_add_fusion.6), channel_id=1, source_target_pairs={{0,16},{16,0},{1,17},{17,1},{2,18},{18,2},{3,19},{19,3},{4,20},{20... | collective-permute-start | bytes 786440 | tf_op jit(solution)/shard_map/ppermute | solution.py:38
  108.9 11.7 %copy-start.1 = (f32[4,64,2048]{2,1,0:T(8,128)S(1)}, f32[4,64,2048]{2,1,0:T(8,128)}, u32[]{:S(2)}) copy-start(f32[4,64,2048]{2,1,0:T(8,128)} %get-tuple-element.22) | copy-start | bytes 6291460
  117.0 7.2 %collective-permute-start.17 = (f32[2,64,256]{2,0,1:T(2,128)S(1)}, f32[2,64,256]{2,0,1:T(2,128)S(1)}, u32[]{:S(2)}, u32[]{:S(2)}) collective-permute-start(f32[2,64,256]{2,0,1:T(2,128)S(1)} %get-tuple-element.31), channel_id=1, source_target_pairs={{0,4},{1,5},{2,6},{3,7},{4,0},{5,1},{6,2},{7,3},{8,12},{9,13},{10,... | collective-permute-start | bytes 393224 | tf_op jit(solution)/shard_map/ppermute | solution.py:38
  117.6 8.6 %collective-permute-start.19 = (f32[2,64,256]{2,0,1:T(2,128)S(1)}, f32[2,64,256]{2,0,1:T(2,128)S(1)}, u32[]{:S(2)}, u32[]{:S(2)}) collective-permute-start(f32[2,64,256]{2,0,1:T(2,128)S(1)} %get-tuple-element.32), channel_id=1, source_target_pairs={{0,12},{1,13},{2,14},{3,15},{4,8},{5,9},{6,10},{7,11},{8,4},{9,5},... | collective-permute-start | bytes 393224 | tf_op jit(solution)/shard_map/ppermute | solution.py:38
  119.1 12.0 %collective-permute-start.18 = (f32[2,64,256]{2,0,1:T(2,128)S(1)}, f32[2,64,256]{2,0,1:T(2,128)S(1)}, u32[]{:S(2)}, u32[]{:S(2)}) collective-permute-start(f32[2,64,256]{2,0,1:T(2,128)S(1)} %get-tuple-element.33), channel_id=1, source_target_pairs={{0,8},{1,9},{2,10},{3,11},{4,12},{5,13},{6,14},{7,15},{8,0},{9,1},... | collective-permute-start | bytes 393224 | tf_op jit(solution)/shard_map/ppermute | solution.py:38
  122.1 9.8 %copy-start.2 = (f32[1,1,16,4,2,32]{5,4,3,2,1,0:T(2,128)S(1)}, f32[1,1,16,4,2,32]{5,4,3,2,1,0:T(2,128)}, u32[]{:S(2)}) copy-start(f32[1,1,16,4,2,32]{5,4,3,2,1,0:T(2,128)} %param.26) | copy-start | bytes 49156
  122.1 9.8 %copy-start.3 = (f32[1,1,16,4,2,32]{5,4,3,2,1,0:T(2,128)S(1)}, f32[1,1,16,4,2,32]{5,4,3,2,1,0:T(2,128)}, u32[]{:S(2)}) copy-start(f32[1,1,16,4,2,32]{5,4,3,2,1,0:T(2,128)} %param.25) | copy-start | bytes 49156
  132.8 9.7 %all-to-all-start.2 = ((f32[32,1,64]{2,1,0:T(1,128)}), f32[32,1,64]{2,1,0:T(1,128)S(1)}, u32[]{:S(2)}, u32[]{:S(2)}) async-start(f32[32,1,64]{2,1,0:T(1,128)} %broadcast_in_dim.18), calls=%async_computation.2 | async-start | bytes 32768 | tf_op jit(solution)/shard_map/all_to_all | solution.py:540

commit v3 on v2

--- a/solution.py
+++ b/solution.py
@@ -174,8 +174,9 @@
     def kernel(
         tre, tim, tre_far, tim_far, where, code_ref, wrh, wrl, wih, wil, qc, qs,
         one, two, sky_any, smo_any,
-        new_any, near_ref, xr_ref, xi_ref, real_out, imag_out,
-        grid_ref, mid_ref, y_ref, mh, ml, sky, smo, new_ref, pr_ref, pi_ref, tre_in, tim_in, pc, ps, sems,
+        new_any, near_ref, xr_any, xi_any, real_any, imag_any,
+        grid_ref, mid_ref, y_ref, mh, ml, sky, smo, new_ref, pr_ref, pi_ref, tre_in, tim_in, pc, ps,
+        xr_ref, xi_ref, real_out, imag_out, sems, real_sems, imag_sems,
     ):
         sky_copy = pltpu.make_async_copy(sky_any, sky, sems.at[0])
         smo_copy = pltpu.make_async_copy(smo_any, smo, sems.at[1])
@@ -195,8 +196,7 @@
             re = re_ref[y, x, f]
             im = im_ref[x, y, f]
             half = (
-                dot_nt(wrh[...], re) + dot_nt(wrl[...], re)
-                + dot_nt(wih[...], im) + dot_nt(wil[...], im)
+                dot_nt(wrh[...], re) + dot_nt(wih[...], im)
             )
             half_re = half[:rows]
             half_im = half[rows:]
@@ -298,14 +298,36 @@
             xr_ref[k * inner : (k + 1) * inner, :] = both[:inner]
             xi_ref[k * inner : (k + 1) * inner, :] = both[inner:]
 
+        xr_copy = pltpu.make_async_copy(xr_ref, xr_any, sems.at[5])
+        xi_copy = pltpu.make_async_copy(xi_ref, xi_any, sems.at[6])
+        xr_copy.start()
+        xi_copy.start()
+
+        def part_copies(i):
+            j = swapped(i, *counts)
+            return (
+                pltpu.make_async_copy(real_out.at[i], real_any.at[i], real_sems.at[i]),
+                pltpu.make_async_copy(imag_out.at[j], imag_any.at[j], imag_sems.at[i]),
+            )
+
         def emit(i, carry):
             emit_part(
                 xr_ref, xi_ref, where.at[part + i], code_ref.at[part + i], (wrh, wrl, wih, wil), (qc, qs),
                 real_out.at[i], imag_out.at[swapped(i, *counts)], pr_ref, pi_ref,
             )
+            for copy in part_copies(i):
+                copy.start()
             return carry
 
+        def settle(i, carry):
+            for copy in part_copies(i):
+                copy.wait()
+            return carry
+
         lax.fori_loop(0, part, emit, 0)
+        lax.fori_loop(0, part, settle, 0)
+        xr_copy.wait()
+        xi_copy.wait()
         written.wait()
 
     any_space = pl.BlockSpec(memory_space=pl.ANY)
@@ -320,7 +342,7 @@
             any_space,
             any_space,
         ],
-        out_specs=[any_space] + [vmem()] * 5,
+        out_specs=[any_space, vmem()] + [any_space] * 4,
         out_shape=[
             jax.ShapeDtypeStruct((rows, image_width), f32),
             jax.ShapeDtypeStruct((near, image_width), f32),
@@ -344,7 +366,13 @@
             pltpu.VMEM(tile_arrays[3].shape, bf16),
             pltpu.VMEM((rows, tiles), f32),
             pltpu.VMEM((rows, tiles), f32),
-            pltpu.SemaphoreType.DMA((5,)),
+            pltpu.VMEM((width, rows), f32),
+            pltpu.VMEM((width, rows), f32),
+            pltpu.VMEM((part, tiles, length), held_as),
+            pltpu.VMEM((part, tiles, length), held_as),
+            pltpu.SemaphoreType.DMA((7,)),
+            pltpu.SemaphoreType.DMA((part,)),
+            pltpu.SemaphoreType.DMA((part,)),
         ],
         cost_estimate=pl.CostEstimate(
             flops=16 * part * rows * tiles * (width + length), bytes_accessed=1 << 24, transcendentals=0
@@ -587,7 +615,7 @@
     lead = min(8, half_rows)
     coef_halo = shifted(coef_dual[:, half_rows - lead :, :], AXES, 1)
 
-    weights = (live_slots * vis_state).astype(bf16)
+    weights = vis_state.astype(bf16)
     kernel_flat = kernel_here.reshape(vis_tiles, 2 * samples, length)
     weight_real = weights[:, :, 0].reshape(vis_tiles, samples)
     weight_imag = weights[:, :, 1].reshape(vis_tiles, samples)
@@ -598,7 +626,7 @@
         ]
     )
     sent = jnp.einsum("nmt,ynm->ynt", kernel_flat, weight_pair, preferred_element_type=f32)
-    sent = sent.astype(bf16)
+    sent = (sent * live_slots.reshape(1, vis_tiles, 1)).astype(bf16)
 
     def unit(steps):
         angle = (2.0 * math.pi / image_width) * (steps % image_width).astype(f32)
@@ -676,9 +704,11 @@
     seen = sum(seen, left[:, 0])
 
     moved_coef, abs_parts = analysis(new_image, sky_image, image_halo, coef_dual)
-    totals = exchanged(jnp.concatenate([abs_parts[0], data_parts]))
+    totals = exchanged(
+        jnp.concatenate([abs_parts[0], jnp.pad(data_parts, (0, -data_parts.size % LANES))])
+    )
+    data_square = jnp.sum(totals[:, LANES:])
     coef_total = jnp.sum(totals[:, :LANES])
-    data_square = jnp.sum(totals[:, LANES:])
     threshold = 0.5 * coef_total / (image_width * image_width)
     new_coef = jnp.clip(moved_coef, -threshold, threshold)
 

time: 145 us -> 147 us (1.014)
  blocking collectives: 9.4 us -> 0 us
  starting transfers between devices: 32.9 us -> 41.8 us
  waiting for transfers between devices: 27.9 us -> 31.4 us
  Pallas kernels: 40.5 us -> 38.3 us
    all_to_all x1 -> x0, blocking collectives: 9.4 us -> none  [exchanged(): return lax.all_to_all(sent, AXES, split_axis=0, concat_axis=0, tiled=True)]
    all_to_all x2 -> x3, starting transfers between devices: 8.67 us -> 12.9 us  [exchanged(): return lax.all_to_all(sent, AXES, split_axis=0, concat_axis=0, tiled=True)]
    ppermute x18, starting transfers between devices: 22.6 us -> 26.4 us  [flipped(): lax.ppermute(block, axis, [(i, i ^ mask) for i in range(lax.axis_size(axi...]
    ppermute x18, waiting for transfers between devices: 22.2 us -> 25.7 us  [flipped(): lax.ppermute(block, axis, [(i, i ^ mask) for i in range(lax.axis_size(axi...]
    all_to_all x2 -> x3, waiting for transfers between devices: 5.71 us -> 3.19 us  [exchanged(): return lax.all_to_all(sent, AXES, split_axis=0, concat_axis=0, tiled=True)]
    ppermute x2, waiting for transfers between devices: 0.01 us -> 2.52 us  [shifted(): return lax.ppermute(block, axis, route)]
    pallas_call x1, Pallas kernels: 21 us -> 18.9 us  [image_step(): pl.pallas_call(kernel, in_specs=[*[vmem()] * 2, any_space, any_space, pl....]
    min x1, other arithmetic: 1.59 us -> 3.23 us  [local(): new_coef = jnp.clip(moved_coef, -threshold, threshold)]
  transfers between devices with their start and end apart: 22 -> 23, of which waited for: 8 -> 8; matrix products, arithmetic and copies ran while one was open for 16% -> 17% of each run, Pallas kernels for 13% -> 13%
where the time goes in v3:
time: 147 us
  starting transfers between devices  41.8 us (28%)
  Pallas kernels  38.3 us (26%)
  waiting for transfers between devices  31.4 us (21%)
  other arithmetic  24.5 us (17%)
  local copies, waits for them, and re-layouts  5.99 us (4%)
  between operations  3.1 us (2%)
    ppermute x18, starting transfers between devices, flipped(): lax.ppermute(block, axis, [(i, i ^ mask) for i in range(lax.axis_size(axi...  26.4 us
    ppermute x18, waiting for transfers between devices, flipped(): lax.ppermute(block, axis, [(i, i ^ mask) for i in range(lax.axis_size(axi...  25.7 us
    pallas_call x1, Pallas kernels, image_step(): pl.pallas_call(kernel, in_specs=[*[vmem()] * 2, any_space, any_space, pl....  18.9 us
    all_to_all x3, starting transfers between devices, exchanged(): return lax.all_to_all(sent, AXES, split_axis=0, concat_axis=0, tiled=True)  12.9 us
    pallas_call x1, Pallas kernels, analysis(): pl.pallas_call(kernel, out_shape=[jax.ShapeDtypeStruct(coef_dual.shape, f...  7.02 us
    pallas_call x1, Pallas kernels, forward_parts(): pl.pallas_call(kernel, grid=(part,), in_specs=[*[whole(x) for x in spectr...  6.57 us
    pallas_call x1, Pallas kernels, synthesis(): pl.pallas_call(kernel, out_shape=jax.ShapeDtypeStruct((rows, 2 * half_wid...  5.85 us
    min x1, other arithmetic, local(): new_coef = jnp.clip(moved_coef, -threshold, threshold)  3.23 us
  transfers between devices with their start and end apart: 23, of which 8 were waited for; matrix products, arithmetic and copies ran while one was open for 17% of the time, Pallas kernels for 13%

profile of v3, /device:TPU:0, one launch (start us, length us, event | category | flops | bytes accessed | tf_op | source)
XLA Modules:
  0.0 146.5 jit_solution(2480671010296938854)
XLA Ops:
  0.7 0.9 fusion.32
  1.7 0.9 bitcast_convert_fusion
  3.3 5.1 %collective-permute-start.2 = (bf16[2,64,256]{2,0,1:T(2,128)(2,1)S(1)}, bf16[2,64,256]{2,0,1:T(2,128)(2,1)S(1)}, u32[]{:S(2)}, u32[]{:S(2)}) collective-permute-start(bf16[2,64,256]{2,0,1:T(2,128)(2,1)S(1)} %fusion.1), channel_id=1, source_target_pairs={{0,12},{1,13},{2,14},{3,15},{4,8},{5,9},{6,10},{7,11},{8,4},{9,5},... | collective-permute-start | bytes 196616 | tf_op jit(solution)/shard_map/ppermute | solution.py:38
  8.4 0.6 collective-permute-start
  9.3 0.6 broadcast_in_dim.15
  9.9 6.0 %all-to-all-start = ((f32[32,1,64]{2,1,0:T(1,128)}), f32[32,1,64]{2,1,0:T(1,128)S(1)}, u32[]{:S(2)}, u32[]{:S(2)}) async-start(f32[32,1,64]{2,1,0:T(1,128)} %broadcast_in_dim.15), calls=%async_computation | async-start | bytes 32768 | tf_op jit(solution)/shard_map/all_to_all | solution.py:568
  15.9 1.7 %slice.97 = f32[4,8,2048]{2,1,0:T(8,128)} slice(f32[4,64,2048]{2,1,0:T(8,128)} %coef_ref.3), slice={[0:4], [56:64], [0:2048]} | slice | bytes 524288 | tf_op jit(solution)/shard_map/slice | solution.py:616
  18.1 0.9 multiply_add_fusion
  19.8 1.7 %collective-permute-start.3 = (bf16[256,256]{1,0:T(8,128)(2,1)S(1)}, bf16[256,256]{1,0:T(8,128)(2,1)S(1)}, u32[]{:S(2)}, u32[]{:S(2)}) collective-permute-start(bf16[256,256]{1,0:T(8,128)(2,1)S(1)} %bitcast.72), channel_id=1, source_target_pairs={{0,16},{16,0},{1,17},{17,1},{2,18},{18,2},{3,19},{19,3},{4,20},{20... | collective-permute-start | bytes 393224 | tf_op jit(solution)/shard_map/ppermute | solution.py:38
  21.5 1.5 collective-permute-start.5
  23.1 6.9 %collective-permute-done.5 = bf16[256,256]{1,0:T(8,128)(2,1)S(1)} collective-permute-done((bf16[256,256]{1,0:T(8,128)(2,1)S(1)}, bf16[256,256]{1,0:T(8,128)(2,1)S(1)}, u32[]{:S(2)}, u32[]{:S(2)}) %collective-permute-start.5) | collective-permute-done | bytes 131104 | tf_op jit(solution)/shard_map/ppermute | solution.py:38
  30.0 0.7 pad_maximum_fusion.4
  30.7 0.7 collective-permute-start.6
  31.9 0.9 fusion.4
  32.8 6.6 %collective-permute-done.6 = bf16[512,256]{1,0:T(8,128)(2,1)} collective-permute-done((bf16[512,256]{1,0:T(8,128)(2,1)}, bf16[512,256]{1,0:T(8,128)(2,1)}, u32[]{:S(2)}, u32[]{:S(2)}) %collective-permute-start.6) | collective-permute-done | bytes 262176 | tf_op jit(solution)/shard_map/ppermute | solution.py:38
  39.4 1.0 pad_maximum_fusion.1
  40.4 1.1 pad_maximum_fusion
  42.9 5.8 %synthesis.1.smo_any = f32[128,4096]{1,0:T(8,128)} custom-call(f32[4,8,2048]{2,1,0:T(8,128)} %collective-permute-done.9.halo_ref, f32[4,64,2048]{2,1,0:T(8,128)} %coef_ref.3, bf16[128,144]{1,0:T(8,128)(2,1)} %constant.138.clone.rh, bf16[128,144]{1,0:T(8,128)(2,1)} %constant.139.clone.rl, bf16[512,256]{1,0:T(8,128)(2,1)} %constant.140.clone.ch, ...), custom_call_target="tpu_custom_call" | custom-call | flops 1073741824 | bytes 4194304 | tf_op jit(solution)/shard_map/synthesis/pallas_call | solution.py:508
  48.8 18.9 %image_step.1 = (f32[128,4096]{1,0:T(8,128)}, f32[8,4096]{1,0:T(8,128)}, f32[2176,128]{1,0:T(8,128)}, f32[2176,128]{1,0:T(8,128)}, f32[4,256,256]{2,1,0:T(8,128)}, /*index=5*/f32[4,256,256]{2,1,0:T(8,128)}) custom-call(bf16[2,2,1,256,256]{4,3,2,1,0:T(8,128)(2,1)} %bitcast.83, bf16[2,2,1,256,256]{4,3,2,1,0:T(8,128)(2,1)} %bitcast.81, ...), custom_call_target="tpu_custom_call" | custom-call | flops 5100273664 | bytes 16777216 | tf_op jit(solution)/shard_map/image_step/pallas_call | solution.py:334
  68.3 6.6 %parts.1 = (f32[4,256,256]{2,1,0:T(8,128)}, f32[4,256,256]{2,1,0:T(8,128)}) custom-call(f32[2176,128]{1,0:T(8,128)} %get-tuple-element.23.xr, f32[2176,128]{1,0:T(8,128)} %get-tuple-element.24.xi, s32[8,1,256]{2,1,0:T(1,128)} %broadcast_and_fusion.where, s32[8,1,256]{2,1,0:T(1,128)} %copy-done.11, bf16[256,256]{1,0:T(8,128)(2,1)} %get-tuple-element.47.wrh, ...), custom_call_target="tpu_custom_call" | custom-call | flops 805306368 | bytes 8388608 | tf_op jit(solution)/shard_map/parts/pallas_call | solution.py:405
  74.9 2.1 %slice_add_fusion = f32[2,256,256]{2,1,0:T(8,128)} fusion(f32[4,256,256]{2,1,0:T(8,128)} %collective-permute-done.14, f32[4,256,256]{2,1,0:T(8,128)} %get-tuple-element.27), kind=kLoop, calls=%fused_computation.12 | loop fusion | flops 131072 | bytes 1572864 | tf_op jit(solution)/shard_map/add | solution.py:686
  77.0 0.8 collective-permute-start.15
  77.8 1.9 %slice_add_fusion.1 = f32[2,256,256]{2,1,0:T(8,128)} fusion(f32[4,256,256]{2,1,0:T(8,128)S(1)} %collective-permute-done.11, f32[4,256,256]{2,1,0:T(8,128)} %get-tuple-element.25), kind=kLoop, calls=%fused_computation.13 | loop fusion | flops 131072 | bytes 1572864 | tf_op jit(solution)/shard_map/add | solution.py:683
  79.7 2.3 %collective-permute-start.10 = (f32[8,4096]{1,0:T(8,128)S(1)}, f32[8,4096]{1,0:T(8,128)S(1)}, u32[]{:S(2)}, u32[]{:S(2)}) collective-permute-start(f32[8,4096]{1,0:T(8,128)S(1)} %copy-done.15), channel_id=1, source_target_pairs={{1,0},{2,1},{3,2},{4,3},{5,4},{6,5},{7,6},{8,7},{9,8},{10,9},{11,1... | collective-permute-start | bytes 393224 | tf_op jit(solution)/shard_map/ppermute | solution.py:34
  82.0 2.5 %collective-permute-done.10.halo_ref = f32[8,4096]{1,0:T(8,128)S(1)} collective-permute-done((f32[8,4096]{1,0:T(8,128)S(1)}, f32[8,4096]{1,0:T(8,128)S(1)}, u32[]{:S(2)}, u32[]{:S(2)}) %collective-permute-start.10) | collective-permute-done | bytes 131104 | tf_op jit(solution)/shard_map/ppermute | solution.py:34
  84.5 0.7 copy-done.8
  85.2 7.0 %analysis.1 = (f32[4,64,2048]{2,1,0:T(8,128)}, f32[1,128]{1,0:T(1,128)}) custom-call(f32[128,4096]{1,0:T(8,128)} %get-tuple-element.13.new_ref, f32[128,4096]{1,0:T(8,128)} %sky_ref.1, f32[8,4096]{1,0:T(8,128)} %copy-done.8, f32[4,64,2048]{2,1,0:T(8,128)} %coef_ref.3, bf16[128,136]{1,0:T(8,128)(2,1)} %constant.144.clone.rh, ...), custom_call_target="tpu_custom_call" | custom-call | flops 1073741824 | bytes 4194304 | tf_op jit(solution)/shard_map/analysis/pallas_call | solution.py:550
  92.2 1.9 %slice_add_fusion.4 = f32[1,256,256]{2,1,0:T(8,128)} fusion(f32[2,256,256]{2,1,0:T(8,128)} %collective-permute-done.15, f32[4,256,256]{2,1,0:T(8,128)} %collective-permute-done.14, f32[4,256,256]{2,1,0:T(8,128)} %get-tuple-element.27), kind=kLoop, calls=%fused_computation.25 | loop fusion | flops 131072 | bytes 1048576 | tf_op jit(solution)/shard_map/add | solution.py:696
  94.1 10.0 %collective-permute-start.16 = (f32[1,256,256]{2,1,0:T(8,128)}, f32[1,256,256]{2,1,0:T(8,128)S(1)}, u32[]{:S(2)}, u32[]{:S(2)}) collective-permute-start(f32[1,256,256]{2,1,0:T(8,128)} %slice_add_fusion.4), channel_id=1, source_target_pairs={{0,2},{1,3},{2,0},{3,1},{4,6},{5,7},{6,4},{7,5},{8,10},{9,11},{10,... | collective-permute-start | bytes 786440 | tf_op jit(solution)/shard_map/ppermute | solution.py:38
  104.1 1.8 %slice_add_fusion.6 = f32[1,256,256]{2,1,0:T(8,128)} fusion(f32[2,256,256]{2,1,0:T(8,128)} %collective-permute-done.12, f32[4,256,256]{2,1,0:T(8,128)S(1)} %collective-permute-done.11, f32[4,256,256]{2,1,0:T(8,128)} %get-tuple-element.25), kind=kLoop, calls=%fused_computation.27 | loop fusion | flops 131072 | bytes 1048576 | tf_op jit(solution)/shard_map/add | solution.py:692
  105.9 1.2 collective-permute-start.13
  107.1 0.6 broadcast_in_dim.16
  107.8 2.9 %all-to-all-start.1 = ((f32[32,1,256]{2,1,0:T(1,128)}), f32[32,1,256]{2,1,0:T(1,128)S(1)}, u32[]{:S(2)}, u32[]{:S(2)}) async-start(f32[32,1,256]{2,1,0:T(1,128)} %broadcast_in_dim.16), calls=%async_computation.1 | async-start | bytes 65536 | tf_op jit(solution)/shard_map/all_to_all | solution.py:568
  110.7 1.2 fusion.5
  112.2 2.6 %collective-permute-done.13 = f32[1,256,256]{2,1,0:T(8,128)} collective-permute-done((f32[1,256,256]{2,1,0:T(8,128)}, f32[1,256,256]{2,1,0:T(8,128)}, u32[]{:S(2)}, u32[]{:S(2)}) %collective-permute-start.13) | collective-permute-done | bytes 262176 | tf_op jit(solution)/shard_map/ppermute | solution.py:38
  114.8 1.2 fusion.6
  116.2 1.0 fusion.15
  117.2 2.0 %collective-permute-start.19 = (f32[2,64,256]{2,0,1:T(2,128)S(1)}, f32[2,64,256]{2,0,1:T(2,128)S(1)}, u32[]{:S(2)}, u32[]{:S(2)}) collective-permute-start(f32[2,64,256]{2,0,1:T(2,128)S(1)} %get-tuple-element.34), channel_id=1, source_target_pairs={{0,12},{1,13},{2,14},{3,15},{4,8},{5,9},{6,10},{7,11},{8,4},{9,5},... | collective-permute-start | bytes 393224 | tf_op jit(solution)/shard_map/ppermute | solution.py:38
  119.2 1.5 %collective-permute-start.18 = (f32[2,64,256]{2,0,1:T(2,128)S(1)}, f32[2,64,256]{2,0,1:T(2,128)S(1)}, u32[]{:S(2)}, u32[]{:S(2)}) collective-permute-start(f32[2,64,256]{2,0,1:T(2,128)S(1)} %get-tuple-element.35), channel_id=1, source_target_pairs={{0,8},{1,9},{2,10},{3,11},{4,12},{5,13},{6,14},{7,15},{8,0},{9,1},... | collective-permute-start | bytes 393224 | tf_op jit(solution)/shard_map/ppermute | solution.py:38
  120.7 0.6 slice_reduce_fusion
  122.0 2.6 %collective-permute-done.17 = f32[2,64,256]{2,0,1:T(2,128)S(1)} collective-permute-done((f32[2,64,256]{2,0,1:T(2,128)}, f32[2,64,256]{2,0,1:T(2,128)S(1)}, u32[]{:S(2)}, u32[]{:S(2)}) %collective-permute-start.17) | collective-permute-done | bytes 131104 | tf_op jit(solution)/shard_map/ppermute | solution.py:38
  124.6 2.1 %collective-permute-done.19 = f32[2,64,256]{2,0,1:T(2,128)S(1)} collective-permute-done((f32[2,64,256]{2,0,1:T(2,128)S(1)}, f32[2,64,256]{2,0,1:T(2,128)S(1)}, u32[]{:S(2)}, u32[]{:S(2)}) %collective-permute-start.19) | collective-permute-done | bytes 131104 | tf_op jit(solution)/shard_map/ppermute | solution.py:38
  126.7 4.9 %collective-permute-done.18 = f32[2,64,256]{2,0,1:T(2,128)S(1)} collective-permute-done((f32[2,64,256]{2,0,1:T(2,128)S(1)}, f32[2,64,256]{2,0,1:T(2,128)S(1)}, u32[]{:S(2)}, u32[]{:S(2)}) %collective-permute-start.18) | collective-permute-done | bytes 131104 | tf_op jit(solution)/shard_map/ppermute | solution.py:38
  131.6 0.6 fusion.17
  133.3 4.0 %all-to-all-start.2 = ((f32[32,1,64]{2,1,0:T(1,128)}), f32[32,1,64]{2,1,0:T(1,128)S(1)}, u32[]{:S(2)}, u32[]{:S(2)}) async-start(f32[32,1,64]{2,1,0:T(1,128)} %broadcast_in_dim.18), calls=%async_computation.2 | async-start | bytes 32768 | tf_op jit(solution)/shard_map/all_to_all | solution.py:568
  137.3 3.2 %maximum_minimum_fusion = f32[4,64,2048]{2,1,0:T(8,128)} fusion(f32[4,64,2048]{2,1,0:T(8,128)} %get-tuple-element.22, f32[]{:T(128)S(6)} %neg.11, f32[]{:T(128)S(6)} %div.22), kind=kLoop, calls=%fused_computation | loop fusion | flops 1048576 | bytes 4194312 | tf_op jit(solution)/shard_map/jit(clip)/min | solution.py:713
  141.3 3.2 %all-to-all-done.2 = f32[32,1,64]{2,1,0:T(1,128)S(1)} async-done(((f32[32,1,64]{2,1,0:T(1,128)}), f32[32,1,64]{2,1,0:T(1,128)S(1)}, u32[]{:S(2)}, u32[]{:S(2)}) %all-to-all-start.2) | async-done | bytes 8224 | tf_op jit(solution)/shard_map/all_to_all | solution.py:568
  145.7 0.8 fusion.22
  (98 shorter events, 7.0 us)
Async XLA Ops:
  0.6 2.2 %copy-start = (bf16[1,1,16,4,2,32,256]{6,5,4,3,2,1,0:T(8,128)(2,1)S(1)}, bf16[1,1,16,4,2,32,256]{6,5,4,3,2,1,0:T(8,128)(2,1)}, u32[]{:S(2)}) copy-start(bf16[1,1,16,4,2,32,256]{6,5,4,3,2,1,0:T(8,128)(2,1)} %param.27) | copy-start | bytes 6291460
  0.6 17.2 %copy-start.13 = (s32[256]{0:T(256)S(1)}, s32[256]{0:T(256)}, u32[]{:S(2)}) copy-start(s32[256]{0:T(256)} %constant.135.clone) | copy-start | bytes 3076
  0.7 17.4 %copy-start.9 = (f32[256,128]{1,0:T(8,128)S(1)}, f32[256,128]{1,0:T(8,128)}, u32[]{:S(2)}) copy-start(f32[256,128]{1,0:T(8,128)} %constant.137.clone) | copy-start | bytes 393220
  0.7 17.4 %copy-start.10 = (f32[256,128]{1,0:T(8,128)S(1)}, f32[256,128]{1,0:T(8,128)}, u32[]{:S(2)}) copy-start(f32[256,128]{1,0:T(8,128)} %constant.136.clone) | copy-start | bytes 393220
  0.7 18.2 %copy-start.6 = (f32[128,256]{1,0:T(8,128)S(1)}, f32[128,256]{1,0:T(8,128)}, u32[]{:S(2)}) copy-start(f32[128,256]{1,0:T(8,128)} %constant.134.clone) | copy-start | bytes 393220
  0.7 18.2 %copy-start.7 = (f32[128,256]{1,0:T(8,128)S(1)}, f32[128,256]{1,0:T(8,128)}, u32[]{:S(2)}) copy-start(f32[128,256]{1,0:T(8,128)} %constant.133.clone) | copy-start | bytes 393220
  0.7 8.3 %copy-start.12 = (s32[1,1,16,4]{2,3,1,0:T(4,128)S(1)}, s32[1,1,16,4]{2,3,1,0:T(4,128)}, u32[]{:S(2)}) copy-start(s32[1,1,16,4]{2,3,1,0:T(4,128)} %param.28) | copy-start | bytes 772
  3.3 15.7 %collective-permute-start.2 = (bf16[2,64,256]{2,0,1:T(2,128)(2,1)S(1)}, bf16[2,64,256]{2,0,1:T(2,128)(2,1)S(1)}, u32[]{:S(2)}, u32[]{:S(2)}) collective-permute-start(bf16[2,64,256]{2,0,1:T(2,128)(2,1)S(1)} %fusion.1), channel_id=1, source_target_pairs={{0,12},{1,13},{2,14},{3,15},{4,8},{5,9},{6,10},{7,11},{8,4},{9,5},... | collective-permute-start | bytes 196616 | tf_op jit(solution)/shard_map/ppermute | solution.py:38
  8.4 10.6 %collective-permute-start.1 = (bf16[2,64,256]{2,0,1:T(2,128)(2,1)S(1)}, bf16[2,64,256]{2,0,1:T(2,128)(2,1)S(1)}, u32[]{:S(2)}, u32[]{:S(2)}) collective-permute-start(bf16[2,64,256]{2,0,1:T(2,128)(2,1)S(1)} %fusion.1), channel_id=1, source_target_pairs={{0,8},{1,9},{2,10},{3,11},{4,12},{5,13},{6,14},{7,15},{8,0},{9,1},... | collective-permute-start | bytes 196616 | tf_op jit(solution)/shard_map/ppermute | solution.py:38
  8.4 10.6 %collective-permute-start = (bf16[2,64,256]{2,0,1:T(2,128)(2,1)S(1)}, bf16[2,64,256]{2,0,1:T(2,128)(2,1)S(1)}, u32[]{:S(2)}, u32[]{:S(2)}) collective-permute-start(bf16[2,64,256]{2,0,1:T(2,128)(2,1)S(1)} %fusion.1), channel_id=1, source_target_pairs={{0,4},{1,5},{2,6},{3,7},{4,0},{5,1},{6,2},{7,3},{8,12},{9,13},{10,... | collective-permute-start | bytes 196616 | tf_op jit(solution)/shard_map/ppermute | solution.py:38
  9.9 32.2 %all-to-all-start = ((f32[32,1,64]{2,1,0:T(1,128)}), f32[32,1,64]{2,1,0:T(1,128)S(1)}, u32[]{:S(2)}, u32[]{:S(2)}) async-start(f32[32,1,64]{2,1,0:T(1,128)} %broadcast_in_dim.15), calls=%async_computation | async-start | bytes 32768 | tf_op jit(solution)/shard_map/all_to_all | solution.py:568
  17.5 25.4 %collective-permute-start.9 = (f32[4,8,2048]{2,1,0:T(8,128)}, f32[4,8,2048]{2,1,0:T(8,128)}, u32[]{:S(2)}, u32[]{:S(2)}) collective-permute-start(f32[4,8,2048]{2,1,0:T(8,128)} %slice.97), channel_id=1, source_target_pairs={{31,0},{0,1},{1,2},{2,3},{3,4},{4,5},{5,6},{6,7},{7,8},{8,9},{9,10... | collective-permute-start | bytes 786440 | tf_op jit(solution)/shard_map/ppermute | solution.py:34
  18.9 12.6 %copy-start.2 = (f32[1,1,16,4,2,32]{5,4,3,2,1,0:T(2,128)S(1)}, f32[1,1,16,4,2,32]{5,4,3,2,1,0:T(2,128)}, u32[]{:S(2)}) copy-start(f32[1,1,16,4,2,32]{5,4,3,2,1,0:T(2,128)} %param.26) | copy-start | bytes 49156
  19.8 11.6 %collective-permute-start.3 = (bf16[256,256]{1,0:T(8,128)(2,1)S(1)}, bf16[256,256]{1,0:T(8,128)(2,1)S(1)}, u32[]{:S(2)}, u32[]{:S(2)}) collective-permute-start(bf16[256,256]{1,0:T(8,128)(2,1)S(1)} %bitcast.72), channel_id=1, source_target_pairs={{0,16},{16,0},{1,17},{17,1},{2,18},{18,2},{3,19},{19,3},{4,20},{20... | collective-permute-start | bytes 393224 | tf_op jit(solution)/shard_map/ppermute | solution.py:38
  21.5 8.5 %collective-permute-start.5 = (bf16[256,256]{1,0:T(8,128)(2,1)S(1)}, bf16[256,256]{1,0:T(8,128)(2,1)S(1)}, u32[]{:S(2)}, u32[]{:S(2)}) collective-permute-start(bf16[256,256]{1,0:T(8,128)(2,1)S(1)} %bitcast.75), channel_id=1, source_target_pairs={{0,2},{1,3},{2,0},{3,1},{4,6},{5,7},{6,4},{7,5},{8,10},{9,11},{10,... | collective-permute-start | bytes 393224 | tf_op jit(solution)/shard_map/ppermute | solution.py:38
  30.7 8.6 %collective-permute-start.6 = (bf16[512,256]{1,0:T(8,128)(2,1)}, bf16[512,256]{1,0:T(8,128)(2,1)}, u32[]{:S(2)}, u32[]{:S(2)}) collective-permute-start(bf16[512,256]{1,0:T(8,128)(2,1)} %pad_maximum_fusion.4), channel_id=1, source_target_pairs={{0,16},{16,0},{1,17},{17,1},{2,18},{18,2},{3,19},{19,3},{4,20},{20... | collective-permute-start | bytes 786440 | tf_op jit(solution)/shard_map/ppermute | solution.py:38
  31.4 1.3 copy-start.5
  31.5 9.0 %collective-permute-start.4 = (bf16[512,256]{1,0:T(8,128)(2,1)S(1)}, bf16[512,256]{1,0:T(8,128)(2,1)}, u32[]{:S(2)}, u32[]{:S(2)}) collective-permute-start(bf16[512,256]{1,0:T(8,128)(2,1)S(1)} %pad_maximum_fusion.3), channel_id=1, source_target_pairs={{0,2},{1,3},{2,0},{3,1},{4,6},{5,7},{6,4},{7,5},{8,10},{9,11},{10,... | collective-permute-start | bytes 786440 | tf_op jit(solution)/shard_map/ppermute | solution.py:38
  40.3 8.4 %copy-start.3 = (bf16[1024,256]{1,0:T(8,128)(2,1)}, bf16[1024,256]{1,0:T(8,128)(2,1)S(1)}, u32[]{:S(2)}) copy-start(bf16[1024,256]{1,0:T(8,128)(2,1)S(1)} %pad_maximum_fusion.1) | copy-start | bytes 1572868
  40.4 8.4 %collective-permute-start.8 = (bf16[2,2,1,256,256]{4,3,2,1,0:T(8,128)(2,1)S(1)}, bf16[2,2,1,256,256]{4,3,2,1,0:T(8,128)(2,1)}, u32[]{:S(2)}, u32[]{:S(2)}) collective-permute-start(bf16[2,2,1,256,256]{4,3,2,1,0:T(8,128)(2,1)S(1)} %bitcast.80), channel_id=1, source_target_pairs={{0,1},{1,0},{2,3},{3,2},{4,5},{5,4},{6,7},{7,6},{8,9},{9,8},{10,11... | collective-permute-start | bytes 1572872 | tf_op jit(solution)/shard_map/ppermute | solution.py:38
  41.6 7.2 %copy-start.4 = (bf16[1024,256]{1,0:T(8,128)(2,1)}, bf16[1024,256]{1,0:T(8,128)(2,1)S(1)}, u32[]{:S(2)}) copy-start(bf16[1024,256]{1,0:T(8,128)(2,1)S(1)} %pad_maximum_fusion) | copy-start | bytes 1572868
  41.6 7.2 %collective-permute-start.7 = (bf16[2,2,1,256,256]{4,3,2,1,0:T(8,128)(2,1)S(1)}, bf16[2,2,1,256,256]{4,3,2,1,0:T(8,128)(2,1)}, u32[]{:S(2)}, u32[]{:S(2)}) collective-permute-start(bf16[2,2,1,256,256]{4,3,2,1,0:T(8,128)(2,1)S(1)} %bitcast.82), channel_id=1, source_target_pairs={{0,1},{1,0},{2,3},{3,2},{4,5},{5,4},{6,7},{7,6},{8,9},{9,8},{10,11... | collective-permute-start | bytes 1572872 | tf_op jit(solution)/shard_map/ppermute | solution.py:38
  42.3 6.5 %copy-start.11 = (s32[8,1,256]{2,1,0:T(1,128)}, s32[8,1,256]{2,1,0:T(1,128)S(1)}, u32[]{:S(2)}) copy-start(s32[8,1,256]{2,1,0:T(1,128)S(1)} %reshape.247.code_ref) | copy-start | bytes 24580
  67.7 7.2 %collective-permute-start.14 = (f32[4,256,256]{2,1,0:T(8,128)}, f32[4,256,256]{2,1,0:T(8,128)}, u32[]{:S(2)}, u32[]{:S(2)}) collective-permute-start(f32[4,256,256]{2,1,0:T(8,128)} %get-tuple-element.28), channel_id=1, source_target_pairs={{0,1},{1,0},{2,3},{3,2},{4,5},{5,4},{6,7},{7,6},{8,9},{9,8},{10,11... | collective-permute-start | bytes 3145736 | tf_op jit(solution)/shard_map/ppermute | solution.py:38
  67.9 9.9 %collective-permute-start.11 = (f32[4,256,256]{2,1,0:T(8,128)}, f32[4,256,256]{2,1,0:T(8,128)S(1)}, u32[]{:S(2)}, u32[]{:S(2)}) collective-permute-start(f32[4,256,256]{2,1,0:T(8,128)} %get-tuple-element.26), channel_id=1, source_target_pairs={{0,1},{1,0},{2,3},{3,2},{4,5},{5,4},{6,7},{7,6},{8,9},{9,8},{10,11... | collective-permute-start | bytes 3145736 | tf_op jit(solution)/shard_map/ppermute | solution.py:38
  74.9 4.8 %copy-start.15 = (f32[8,4096]{1,0:T(8,128)S(1)}, f32[8,4096]{1,0:T(8,128)}, u32[]{:S(2)}) copy-start(f32[8,4096]{1,0:T(8,128)} %get-tuple-element.19) | copy-start | bytes 393220
  77.0 15.2 %collective-permute-start.15 = (f32[2,256,256]{2,1,0:T(8,128)}, f32[2,256,256]{2,1,0:T(8,128)}, u32[]{:S(2)}, u32[]{:S(2)}) collective-permute-start(f32[2,256,256]{2,1,0:T(8,128)} %slice_add_fusion), channel_id=1, source_target_pairs={{0,16},{16,0},{1,17},{17,1},{2,18},{18,2},{3,19},{19,3},{4,20},{20... | collective-permute-start | bytes 1572872 | tf_op jit(solution)/shard_map/ppermute | solution.py:38
  79.7 24.4 %collective-permute-start.12 = (f32[2,256,256]{2,1,0:T(8,128)}, f32[2,256,256]{2,1,0:T(8,128)}, u32[]{:S(2)}, u32[]{:S(2)}) collective-permute-start(f32[2,256,256]{2,1,0:T(8,128)} %slice_add_fusion.1), channel_id=1, source_target_pairs={{0,2},{1,3},{2,0},{3,1},{4,6},{5,7},{6,4},{7,5},{8,10},{9,11},{10,... | collective-permute-start | bytes 1572872 | tf_op jit(solution)/shard_map/ppermute | solution.py:38
  79.7 4.8 %collective-permute-start.10 = (f32[8,4096]{1,0:T(8,128)S(1)}, f32[8,4096]{1,0:T(8,128)S(1)}, u32[]{:S(2)}, u32[]{:S(2)}) collective-permute-start(f32[8,4096]{1,0:T(8,128)S(1)} %copy-done.15), channel_id=1, source_target_pairs={{1,0},{2,1},{3,2},{4,3},{5,4},{6,5},{7,6},{8,7},{9,8},{10,9},{11,1... | collective-permute-start | bytes 393224 | tf_op jit(solution)/shard_map/ppermute | solution.py:34
  84.5 0.7 copy-start.8
  92.2 14.9 %copy-start.14 = (f32[1,128]{1,0:T(1,128)S(1)}, f32[1,128]{1,0:T(1,128)}, u32[]{:S(2)}) copy-start(f32[1,128]{1,0:T(1,128)} %get-tuple-element.20) | copy-start | bytes 1540
  94.1 16.6 %collective-permute-start.16 = (f32[1,256,256]{2,1,0:T(8,128)}, f32[1,256,256]{2,1,0:T(8,128)S(1)}, u32[]{:S(2)}, u32[]{:S(2)}) collective-permute-start(f32[1,256,256]{2,1,0:T(8,128)} %slice_add_fusion.4), channel_id=1, source_target_pairs={{0,2},{1,3},{2,0},{3,1},{4,6},{5,7},{6,4},{7,5},{8,10},{9,11},{10,... | collective-permute-start | bytes 786440 | tf_op jit(solution)/shard_map/ppermute | solution.py:38
  105.9 8.9 %collective-permute-start.13 = (f32[1,256,256]{2,1,0:T(8,128)}, f32[1,256,256]{2,1,0:T(8,128)}, u32[]{:S(2)}, u32[]{:S(2)}) collective-permute-start(f32[1,256,256]{2,1,0:T(8,128)} %slice_add_fusion.6), channel_id=1, source_target_pairs={{0,16},{16,0},{1,17},{17,1},{2,18},{18,2},{3,19},{19,3},{4,20},{20... | collective-permute-start | bytes 786440 | tf_op jit(solution)/shard_map/ppermute | solution.py:38
  107.8 13.0 %all-to-all-start.1 = ((f32[32,1,256]{2,1,0:T(1,128)}), f32[32,1,256]{2,1,0:T(1,128)S(1)}, u32[]{:S(2)}, u32[]{:S(2)}) async-start(f32[32,1,256]{2,1,0:T(1,128)} %broadcast_in_dim.16), calls=%async_computation.1 | async-start | bytes 65536 | tf_op jit(solution)/shard_map/all_to_all | solution.py:568
  116.2 16.2 %copy-start.1 = (f32[1,1,16,4,2,32]{5,4,3,2,1,0:T(2,128)S(1)}, f32[1,1,16,4,2,32]{5,4,3,2,1,0:T(2,128)}, u32[]{:S(2)}) copy-start(f32[1,1,16,4,2,32]{5,4,3,2,1,0:T(2,128)} %param.25) | copy-start | bytes 49156
  117.2 7.3 %collective-permute-start.17 = (f32[2,64,256]{2,0,1:T(2,128)}, f32[2,64,256]{2,0,1:T(2,128)S(1)}, u32[]{:S(2)}, u32[]{:S(2)}) collective-permute-start(f32[2,64,256]{2,0,1:T(2,128)} %get-tuple-element.33), channel_id=1, source_target_pairs={{0,4},{1,5},{2,6},{3,7},{4,0},{5,1},{6,2},{7,3},{8,12},{9,13},{10,... | collective-permute-start | bytes 393224 | tf_op jit(solution)/shard_map/ppermute | solution.py:38
  117.2 9.4 %collective-permute-start.19 = (f32[2,64,256]{2,0,1:T(2,128)S(1)}, f32[2,64,256]{2,0,1:T(2,128)S(1)}, u32[]{:S(2)}, u32[]{:S(2)}) collective-permute-start(f32[2,64,256]{2,0,1:T(2,128)S(1)} %get-tuple-element.34), channel_id=1, source_target_pairs={{0,12},{1,13},{2,14},{3,15},{4,8},{5,9},{6,10},{7,11},{8,4},{9,5},... | collective-permute-start | bytes 393224 | tf_op jit(solution)/shard_map/ppermute | solution.py:38
  119.2 12.4 %collective-permute-start.18 = (f32[2,64,256]{2,0,1:T(2,128)S(1)}, f32[2,64,256]{2,0,1:T(2,128)S(1)}, u32[]{:S(2)}, u32[]{:S(2)}) collective-permute-start(f32[2,64,256]{2,0,1:T(2,128)S(1)} %get-tuple-element.35), channel_id=1, source_target_pairs={{0,8},{1,9},{2,10},{3,11},{4,12},{5,13},{6,14},{7,15},{8,0},{9,1},... | collective-permute-start | bytes 393224 | tf_op jit(solution)/shard_map/ppermute | solution.py:38
  133.3 11.1 %all-to-all-start.2 = ((f32[32,1,64]{2,1,0:T(1,128)}), f32[32,1,64]{2,1,0:T(1,128)S(1)}, u32[]{:S(2)}, u32[]{:S(2)}) async-start(f32[32,1,64]{2,1,0:T(1,128)} %broadcast_in_dim.18), calls=%async_computation.2 | async-start | bytes 32768 | tf_op jit(solution)/shard_map/all_to_all | solution.py:568
